TPU v7x, 32 devices: a whole 2x2x4 slice. The times are simulated.
32 devices in a mesh: dp: 8 (over z, y), tensor: 4 (over x, core).
Axes of the slice: x: 2, y: 2, z: 4, core: 2. Of those that a mesh axis runs over, the one named last changes fastest.
Arguments:
- tokens: float32 [50176, 512], P(('dp', 'tensor')), may hold values from -6 to 6
- out_grad: float32 [50176, 512], P(('dp', 'tensor')), may hold values from -6 to 6
- qkv_weight: float32 [512, 4, 384], P(None, 'tensor', 'dp'), may hold values from -0.25 to 0.25
- proj_weight: float32 [4, 128, 512], P('tensor', 'dp'), may hold values from -0.75 to 0.75
- fc1_weight: float32 [512, 4, 512], P(None, 'tensor', 'dp'), may hold values from -0.25 to 0.25
- fc2_weight: float32 [4, 512, 512], P('tensor', 'dp'), may hold values from -0.125 to 0.125
- qkv_momentum: float32 [512, 4, 384], P(None, 'tensor', 'dp'), may hold values from -3 to 3
- proj_momentum: float32 [4, 128, 512], P('tensor', 'dp'), may hold values from -3 to 3
- fc1_momentum: float32 [512, 4, 512], P(None, 'tensor', 'dp'), may hold values from -3 to 3
- fc2_momentum: float32 [4, 512, 512], P('tensor', 'dp'), may hold values from -3 to 3
- norm_gains: float32 [2, 512], replicated, may hold values from 0.5 to 1.5
- shift_biases: float32 [4, 512], replicated, may hold values from -3 to 3
- head_biases: float32 [2, 512], replicated, may hold values from -3 to 3
- hidden_bias: float32 [2048], replicated, may hold values from -3 to 3
- position_table: float32 [169, 16], replicated, may hold values from -5 to 5
- gain_momentum: float32 [2, 512], replicated, may hold values from -3 to 3
- shift_momentum: float32 [4, 512], replicated, may hold values from -3 to 3
- head_bias_momentum: float32 [2, 512], replicated, may hold values from -3 to 3
- hidden_bias_momentum: float32 [2048], replicated, may hold values from -3 to 3
- table_momentum: float32 [169, 16], replicated, may hold values from -3 to 3
- region_ids: int32 [14, 14], replicated, may hold values from 0 to 2
- position_index: int32 [49, 49], replicated, may hold values from 0 to 168
Outputs:
- out_tokens: float32 [50176, 512], P(('dp', 'tensor'))
- input_grad: float32 [50176, 512], P(('dp', 'tensor'))
- qkv_grad: float32 [512, 4, 384], P(None, 'tensor', 'dp')
- proj_grad: float32 [4, 128, 512], P('tensor', 'dp')
- fc1_grad: float32 [512, 4, 512], P(None, 'tensor', 'dp')
- fc2_grad: float32 [4, 512, 512], P('tensor', 'dp')
- qkv_new: float32 [512, 4, 384], P(None, 'tensor', 'dp')
- proj_new: float32 [4, 128, 512], P('tensor', 'dp')
- fc1_new: float32 [512, 4, 512], P(None, 'tensor', 'dp')
- fc2_new: float32 [4, 512, 512], P('tensor', 'dp')
- qkv_momentum_new: float32 [512, 4, 384], P(None, 'tensor', 'dp')
- proj_momentum_new: float32 [4, 128, 512], P('tensor', 'dp')
- fc1_momentum_new: float32 [512, 4, 512], P(None, 'tensor', 'dp')
- fc2_momentum_new: float32 [4, 512, 512], P('tensor', 'dp')
- gain_grad: float32 [2, 512], replicated
- shift_grad: float32 [4, 512], replicated
- head_bias_grad: float32 [2, 512], replicated
- hidden_bias_grad: float32 [2048], replicated
- table_grad: float32 [169, 16], replicated
- gains_new: float32 [2, 512], replicated
- shifts_new: float32 [4, 512], replicated
- head_biases_new: float32 [2, 512], replicated
- hidden_bias_new: float32 [2048], replicated
- table_new: float32 [169, 16], replicated
- gain_momentum_new: float32 [2, 512], replicated
- shift_momentum_new: float32 [4, 512], replicated
- head_bias_momentum_new: float32 [2, 512], replicated
- hidden_bias_momentum_new: float32 [2048], replicated
- table_momentum_new: float32 [169, 16], replicated
All inputs are finite; a program needn't handle non-finite values.
Results may differ from a plain program's by a relative error of at most 0.019.
Values may be sent and summed in bfloat16 or wider, within the bound.
A program may use at most 320 MiB of HBM per device.

v0:
```python
import math

import jax
import jax.numpy as jnp
from jax import lax
from jax.sharding import PartitionSpec as P

D = 512
HEADS = 16
FF = 2048
HEAD = 32
WIN = 7
SIDE = 14
SHIFT = 3
NS_STEPS = 5
IMG_DEV = 32


NORM_EPSILON = 1e-05
MASK_VALUE = -100.0
MUON_EPSILON = 1e-07
QUINTIC_FIRST = 3.4445
QUINTIC_SECOND = -4.775
QUINTIC_THIRD = 2.0315
MOMENTUM = 0.9
MATRIX_RATE = 0.5
VECTOR_RATE = 1.0
HIGHEST = lax.Precision.HIGHEST


def shortened(array):

    def short(part):
        return part.astype(jnp.bfloat16) if part.dtype == jnp.float32 else part

    return jax.tree.map(short, array)


def gelu_tanh(values):
    return jax.nn.gelu(values, approximate=True)


def layer_norm(values, gain_row, shift_row):
    center = values - jnp.mean(values, axis=-1, keepdims=True)
    inverse_std = lax.rsqrt(jnp.mean(center * center, axis=-1, keepdims=True) + NORM_EPSILON)
    whitened = center * inverse_std
    return (whitened, inverse_std, whitened * gain_row + shift_row)


def norm_backward(grad_out, whitened, inverse_std, gain_row):
    scaled = grad_out * gain_row
    centered = (
        scaled
        - jnp.mean(scaled, axis=-1, keepdims=True)
        - whitened * jnp.mean(scaled * whitened, axis=-1, keepdims=True)
    )
    return inverse_std * centered


def to_windows(rows, shift_by):
    images_in = rows.shape[0] // (SIDE * SIDE)
    trailing = rows.shape[1:]
    layout = rows.reshape((images_in, SIDE, SIDE) + trailing)
    if shift_by:
        layout = jnp.roll(layout, (-shift_by, -shift_by), axis=(1, 2))
    across = SIDE // WIN
    layout = layout.reshape((images_in, across, WIN, across, WIN) + trailing)
    axes_order = (0, 1, 3, 2, 4) + tuple(range(5, 5 + len(trailing)))
    return layout.transpose(axes_order).reshape((images_in * across * across, WIN * WIN) + trailing)


def from_windows(windows, shift_by):
    across = SIDE // WIN
    images_in = windows.shape[0] // (across * across)
    trailing = windows.shape[2:]
    layout = windows.reshape((images_in, across, across, WIN, WIN) + trailing)
    axes_order = (0, 1, 3, 2, 4) + tuple(range(5, 5 + len(trailing)))
    layout = layout.transpose(axes_order).reshape((images_in, SIDE, SIDE) + trailing)
    layout = jnp.roll(layout, (shift_by, shift_by), axis=(1, 2))
    return layout.reshape((images_in * SIDE * SIDE,) + trailing)


def window_masks(region_ids):
    regions = to_windows(region_ids.reshape(SIDE * SIDE, 1), 0)[:, :, 0]
    return jnp.where(regions[:, :, None] == regions[:, None, :], 0.0, MASK_VALUE).astype(
        jnp.float32
    )


def attend_block(queries, keys_in, values_in, head_bias, block_mask):
    scores = jnp.einsum("wighd,wjghd->wghij", queries, keys_in, preferred_element_type=jnp.float32)
    scores = scores + head_bias[None] + block_mask[:, None, None]
    row_peak = jnp.max(scores, axis=-1, keepdims=True)
    log_total = row_peak + jnp.log(jnp.sum(jnp.exp(scores - row_peak), axis=-1, keepdims=True))
    probs_low = jnp.exp(scores - log_total).astype(jnp.bfloat16)
    mixed_out = jnp.einsum(
        "wghij,wjghd->wighd", probs_low, values_in, preferred_element_type=jnp.float32
    )
    return (mixed_out.astype(jnp.bfloat16), log_total)


def attend_back(queries, keys_in, values_in, head_bias, block_mask, log_total, grad_out):
    scores = jnp.einsum("wighd,wjghd->wghij", queries, keys_in, preferred_element_type=jnp.float32)
    scores = scores + head_bias[None] + block_mask[:, None, None]
    probs_full = jnp.exp(scores - log_total)
    grad_values = jnp.einsum(
        "wghij,wighd->wjghd",
        probs_full.astype(jnp.bfloat16),
        grad_out,
        preferred_element_type=jnp.float32,
    )
    grad_probs = jnp.einsum(
        "wighd,wjghd->wghij", grad_out, values_in, preferred_element_type=jnp.float32
    )
    centered = grad_probs - jnp.sum(probs_full * grad_probs, axis=-1, keepdims=True)
    grad_scores = probs_full * centered
    rounded = grad_scores.astype(jnp.bfloat16)
    grad_queries = jnp.einsum(
        "wghij,wjghd->wighd", rounded, keys_in, preferred_element_type=jnp.float32
    ) * HEAD ** (-0.5)
    grad_keys = jnp.einsum(
        "wghij,wighd->wjghd", rounded, queries, preferred_element_type=jnp.float32
    )
    return (jnp.stack([grad_queries, grad_keys, grad_values], 3), jnp.sum(grad_scores, 0))


def block_layout(qkv_windows, window_mask):
    windows_total = qkv_windows.shape[0]
    per_image = window_mask.shape[0]
    block_size = 16
    block_mask = jnp.tile(window_mask, (block_size // per_image, 1, 1))
    return (windows_total, block_size, block_mask)


def attention_all(qkv_windows, head_bias, window_mask):
    windows_total, block_size, block_mask = block_layout(qkv_windows, window_mask)
    shaped = qkv_windows.reshape((windows_total // block_size, block_size) + qkv_windows.shape[1:])

    def forward_one(window_block):
        return attend_block(
            window_block[:, :, :, 0],
            window_block[:, :, :, 1],
            window_block[:, :, :, 2],
            head_bias,
            block_mask,
        )

    mixed_out, log_total = lax.map(forward_one, shaped)
    return (mixed_out.reshape((windows_total,) + mixed_out.shape[2:]), log_total)


def attention_back(qkv_windows, head_bias, window_mask, log_total, grad_mixed):
    windows_total, block_size, block_mask = block_layout(qkv_windows, window_mask)
    shaped = qkv_windows.reshape((windows_total // block_size, block_size) + qkv_windows.shape[1:])
    grad_shaped = grad_mixed.reshape(
        (windows_total // block_size, block_size) + grad_mixed.shape[1:]
    )

    def backward_one(pieces):
        window_block, log_block, grad_block = pieces
        return attend_back(
            window_block[:, :, :, 0],
            window_block[:, :, :, 1],
            window_block[:, :, :, 2],
            head_bias,
            block_mask,
            log_block,
            grad_block,
        )

    grad_windows, grad_bias = lax.map(backward_one, (shaped, log_total, grad_shaped))
    return (grad_windows.reshape((windows_total,) + grad_windows.shape[2:]), jnp.sum(grad_bias, 0))


def gram_of(matrix, is_wide):
    if is_wide:
        return jnp.dot(matrix, matrix.T, precision=HIGHEST)
    return jnp.dot(matrix.T, matrix, precision=HIGHEST)


def quintic(matrix, gram_sum, is_wide):
    poly_term = QUINTIC_SECOND * gram_sum + QUINTIC_THIRD * jnp.dot(
        gram_sum, gram_sum, precision=HIGHEST
    )
    if is_wide:
        return QUINTIC_FIRST * matrix + jnp.dot(poly_term, matrix, precision=HIGHEST)
    return QUINTIC_FIRST * matrix + jnp.dot(matrix, poly_term, precision=HIGHEST)


def owner_branch(matrix_id, is_wide, groups, block_size, pad_len, totals):

    def run_owner(received):
        pieces = received[:, :block_size]
        if is_wide:
            matrix = pieces.reshape(groups, D, -1).transpose(1, 0, 2).reshape(D, -1)
        else:
            matrix = pieces.reshape(-1, D)
        iterate = matrix / (jnp.sqrt(totals[matrix_id]) + MUON_EPSILON)
        for ns_turn in range(NS_STEPS):
            iterate = quintic(iterate, gram_of(iterate, is_wide), is_wide)
        if is_wide:
            blocks_back = iterate.reshape(D, groups, -1).transpose(1, 0, 2).reshape(groups, -1)
        else:
            blocks_back = iterate.reshape(groups, -1)
        return jnp.pad(blocks_back, ((0, 0), (0, pad_len - blocks_back.shape[1])))

    return run_owner


def shards(
    tokens,
    out_grad,
    qkv_weight,
    proj_weight,
    fc1_weight,
    fc2_weight,
    qkv_momentum,
    proj_momentum,
    fc1_momentum,
    fc2_momentum,
    norm_gains,
    shift_biases,
    head_biases,
    hidden_bias,
    position_table,
    gain_momentum,
    shift_momentum,
    head_bias_momentum,
    hidden_bias_momentum,
    table_momentum,
    region_ids,
    position_index,
):
    groups = lax.axis_size("tensor")
    dp_count = lax.axis_size("dp")
    images = IMG_DEV * dp_count
    group_width = D // groups
    heads_group = HEADS // groups
    owner_cast = (
        qkv_weight.astype(jnp.bfloat16),
        proj_weight.astype(jnp.bfloat16),
        fc1_weight.astype(jnp.bfloat16),
        fc2_weight.astype(jnp.bfloat16),
    )
    w_qkv, w_proj, w_fc1, w_fc2 = (
        lax.all_gather(owner_cast[0], "dp", axis=2, tiled=True),
        lax.all_gather(owner_cast[1], "dp", axis=1, tiled=True),
        lax.all_gather(owner_cast[2], "dp", axis=2, tiled=True),
        lax.all_gather(owner_cast[3], "dp", axis=1, tiled=True),
    )
    first_group = lax.axis_index("tensor")
    local_groups = w_qkv.shape[1]
    split_bias = lax.dynamic_slice_in_dim(
        head_biases.reshape(2, groups, group_width), first_group, local_groups, 1
    )
    qkv_bias = jnp.stack([split_bias[0], jnp.zeros_like(split_bias[0]), split_bias[1]], 1).reshape(
        -1
    )
    fc1_bias = lax.dynamic_slice_in_dim(
        hidden_bias.reshape(groups, -1), first_group, local_groups, 0
    ).reshape(-1)
    table_rows = position_table.shape[0]
    table_local = lax.dynamic_slice_in_dim(
        position_table.reshape(table_rows, groups, heads_group), first_group, local_groups, 1
    )
    onehot = (
        position_index.reshape(-1)[:, None] == jnp.arange(table_rows, dtype=jnp.int32)[None, :]
    ).astype(jnp.float32)
    head_bias = jnp.dot(onehot, table_local.reshape(table_rows, -1), precision=HIGHEST).T.reshape(
        local_groups, heads_group, WIN * WIN, WIN * WIN
    )
    window_mask = window_masks(region_ids)
    whitened_one, inverse_one, normed = layer_norm(tokens, norm_gains[0], shift_biases[0])
    normed_one = normed.astype(jnp.bfloat16)
    rows_one = lax.all_gather(normed_one, "tensor", axis=0, tiled=True)
    all_rows = rows_one.shape[0]
    qkv_float = (
        jnp.dot(rows_one, w_qkv.reshape(D, -1), preferred_element_type=jnp.float32) + qkv_bias
    )
    qkv_float = qkv_float.reshape(all_rows, local_groups, 3, group_width)
    qkv_round = jnp.concatenate(
        [qkv_float[:, :, :1] * HEAD ** (-0.5), qkv_float[:, :, 1:]], 2
    ).astype(jnp.bfloat16)
    qkv_windows = to_windows(qkv_round, SHIFT).reshape(
        -1, WIN * WIN, local_groups, 3, heads_group, HEAD
    )
    mixed_out, log_total = attention_all(qkv_windows, head_bias, window_mask)
    joined = from_windows(mixed_out.reshape(-1, WIN * WIN, local_groups, group_width), SHIFT)
    part_rows = joined
    attn_out = lax.psum_scatter(
        jnp.einsum("tgc,gcd->td", part_rows, w_proj, preferred_element_type=jnp.float32).astype(
            jnp.bfloat16
        ),
        "tensor",
        scatter_dimension=0,
        tiled=True,
    ).astype(jnp.float32)
    middle = tokens + attn_out + shift_biases[2]
    whitened_two, inverse_two, normed = layer_norm(middle, norm_gains[1], shift_biases[1])
    normed_two = normed.astype(jnp.bfloat16)
    rows_two = lax.all_gather(normed_two, "tensor", axis=0, tiled=True)
    pre_act = jnp.dot(rows_two, w_fc1.reshape(D, -1), preferred_element_type=jnp.float32) + fc1_bias
    hidden = gelu_tanh(pre_act).astype(jnp.bfloat16).reshape(all_rows, local_groups, -1)
    part_rows = hidden
    mlp_out = lax.psum_scatter(
        jnp.einsum("tgf,gfd->td", part_rows, w_fc2, preferred_element_type=jnp.float32).astype(
            jnp.bfloat16
        ),
        "tensor",
        scatter_dimension=0,
        tiled=True,
    ).astype(jnp.float32)
    output = middle + mlp_out + shift_biases[3]
    grad_round = out_grad.astype(jnp.bfloat16)
    grad_rows = lax.all_gather(grad_round, "tensor", axis=0, tiled=True)
    grad_fc2 = jnp.einsum("tgf,td->gfd", hidden, grad_rows, preferred_element_type=jnp.float32)
    grad_hidden = jnp.einsum(
        "td,gfd->tgf", grad_rows, w_fc2, preferred_element_type=jnp.float32
    ).reshape(all_rows, -1)
    grad_pre = jax.vjp(gelu_tanh, pre_act)[1](grad_hidden)[0]
    pre_round = grad_pre.astype(jnp.bfloat16)
    grad_fc1 = jnp.einsum(
        "td,tf->df", rows_two, pre_round, preferred_element_type=jnp.float32
    ).reshape(D, local_groups, -1)
    pre_groups = pre_round.reshape(all_rows, local_groups, -1)
    part_rows = pre_groups
    grad_norm_two = lax.psum_scatter(
        jnp.einsum("tgf,dgf->td", part_rows, w_fc1, preferred_element_type=jnp.float32).astype(
            jnp.bfloat16
        ),
        "tensor",
        scatter_dimension=0,
        tiled=True,
    ).astype(jnp.float32)
    grad_middle = out_grad + norm_backward(grad_norm_two, whitened_two, inverse_two, norm_gains[1])
    middle_round = grad_middle.astype(jnp.bfloat16)
    middle_rows = lax.all_gather(middle_round, "tensor", axis=0, tiled=True)
    grad_proj = jnp.einsum("tgc,td->gcd", joined, middle_rows, preferred_element_type=jnp.float32)
    grad_joined = jnp.einsum(
        "td,gcd->tgc", middle_rows, w_proj, preferred_element_type=jnp.float32
    ).astype(jnp.bfloat16)
    grad_mixed = to_windows(grad_joined, SHIFT).reshape(
        -1, WIN * WIN, local_groups, heads_group, HEAD
    )
    grad_windows, grad_bias = attention_back(
        qkv_windows, head_bias, window_mask, log_total, grad_mixed
    )
    grad_qkv = from_windows(
        grad_windows.reshape(-1, WIN * WIN, local_groups, 3, group_width), SHIFT
    )
    head_grad_local = jnp.stack([jnp.sum(grad_qkv[:, :, 0], 0), jnp.sum(grad_qkv[:, :, 2], 0)])
    qkv_round_grad = grad_qkv.astype(jnp.bfloat16).reshape(all_rows, local_groups, -1)
    grad_qkv_w = jnp.einsum(
        "td,tgc->dgc", rows_one, qkv_round_grad, preferred_element_type=jnp.float32
    )
    part_rows = qkv_round_grad
    grad_norm_one = lax.psum_scatter(
        jnp.einsum("tgc,dgc->td", part_rows, w_qkv, preferred_element_type=jnp.float32).astype(
            jnp.bfloat16
        ),
        "tensor",
        scatter_dimension=0,
        tiled=True,
    ).astype(jnp.float32)
    grad_input = grad_middle + norm_backward(
        grad_norm_one, whitened_one, inverse_one, norm_gains[0]
    )
    gain_part = jnp.stack(
        [jnp.sum(grad_norm_one * whitened_one, 0), jnp.sum(grad_norm_two * whitened_two, 0)]
    )
    shift_part = jnp.stack(
        [
            jnp.sum(grad_norm_one, 0),
            jnp.sum(grad_norm_two, 0),
            jnp.sum(grad_middle, 0),
            jnp.sum(out_grad, 0),
        ]
    )
    head_part = lax.dynamic_update_slice_in_dim(
        jnp.zeros((2, groups, group_width), jnp.float32), head_grad_local, first_group, 1
    ).reshape(2, D)
    hidden_part = lax.dynamic_update_slice_in_dim(
        jnp.zeros((groups, FF // groups), jnp.float32),
        jnp.sum(grad_pre, 0).reshape(local_groups, -1),
        first_group,
        0,
    ).reshape(FF)
    table_local_grad = jnp.dot(
        onehot.T, grad_bias.reshape(local_groups * heads_group, -1).T, precision=HIGHEST
    )
    table_part = lax.dynamic_update_slice_in_dim(
        jnp.zeros((table_rows, groups, heads_group), jnp.float32),
        table_local_grad.reshape(table_rows, local_groups, heads_group),
        first_group,
        1,
    ).reshape(table_rows, HEADS)
    summed = (
        lax.psum_scatter(
            grad_qkv_w.astype(jnp.bfloat16), "dp", scatter_dimension=2, tiled=True
        ).astype(jnp.float32),
        lax.psum_scatter(
            grad_proj.astype(jnp.bfloat16), "dp", scatter_dimension=1, tiled=True
        ).astype(jnp.float32),
        lax.psum_scatter(
            grad_fc1.astype(jnp.bfloat16), "dp", scatter_dimension=2, tiled=True
        ).astype(jnp.float32),
        lax.psum_scatter(
            grad_fc2.astype(jnp.bfloat16), "dp", scatter_dimension=1, tiled=True
        ).astype(jnp.float32),
    )
    weight_grads = tuple((member / images for member in summed))
    weights_old = (qkv_weight, proj_weight, fc1_weight, fc2_weight)
    momenta_old = (qkv_momentum, proj_momentum, fc1_momentum, fc2_momentum)
    momenta_new = tuple(
        (
            MOMENTUM * old_state + grad_part
            for old_state, grad_part in zip(momenta_old, weight_grads)
        )
    )
    matrices = [
        momenta_new[0].reshape(D, -1),
        momenta_new[1].reshape(-1, D),
        momenta_new[2].reshape(D, -1),
        momenta_new[3].reshape(-1, D),
    ]
    wide_flags = (True, False, True, False)
    squares = jnp.stack([jnp.sum(matrix * matrix) for matrix in matrices])
    totals, gain_sum, shift_sum, head_sum, hidden_sum, table_sum = lax.psum(
        (squares, gain_part, shift_part, head_part, hidden_part, table_part), ("dp", "tensor")
    )
    blocks = (
        lax.all_gather(momenta_new[0].astype(jnp.bfloat16), "dp", axis=2, tiled=True).astype(
            jnp.float32
        ),
        lax.all_gather(momenta_new[1].astype(jnp.bfloat16), "dp", axis=1, tiled=True).astype(
            jnp.float32
        ),
        lax.all_gather(momenta_new[2].astype(jnp.bfloat16), "dp", axis=2, tiled=True).astype(
            jnp.float32
        ),
        lax.all_gather(momenta_new[3].astype(jnp.bfloat16), "dp", axis=1, tiled=True).astype(
            jnp.float32
        ),
    )
    block_shapes = [member.shape for member in blocks]
    block_sizes = [member.size for member in blocks]
    pad_len = max(block_sizes)
    stacked = jnp.stack(
        [jnp.pad(member.reshape(-1), (0, pad_len - member.size)) for member in blocks]
    )[:, None, :]
    arrived = lax.all_to_all(
        shortened(stacked), "tensor", split_axis=0, concat_axis=1, tiled=True
    ).astype(stacked.dtype)
    owned = 4 // groups
    branches = [
        owner_branch(
            matrix_id, wide_flags[matrix_id], groups, block_sizes[matrix_id], pad_len, totals
        )
        for matrix_id in range(4)
    ]
    results = jnp.stack([lax.switch(lax.axis_index("tensor") * owned + 0, branches, arrived[0])])
    returned = lax.all_to_all(
        shortened(results), "tensor", split_axis=1, concat_axis=0, tiled=True
    ).astype(results.dtype)
    dp_index = lax.axis_index("dp")
    current = []
    for matrix_id in range(4):
        whole_block = returned[matrix_id, 0, : block_sizes[matrix_id]].reshape(
            block_shapes[matrix_id]
        )
        slab_dim = 2 if wide_flags[matrix_id] else 1
        slab = weights_old[matrix_id].shape[slab_dim]
        current.append(lax.dynamic_slice_in_dim(whole_block, dp_index * slab, slab, slab_dim))
    factors = (
        math.sqrt(max(1.0, 3.0)),
        1.0,
        math.sqrt(max(1.0, FF / D)),
        math.sqrt(max(1.0, D / FF)),
    )
    weights_new = tuple(
        (
            weight - MATRIX_RATE * factor * matrix
            for weight, matrix, factor in zip(weights_old, current, factors)
        )
    )
    small_grads = (
        gain_sum / images,
        shift_sum / images,
        head_sum / images,
        hidden_sum / images,
        table_sum / images,
    )
    small_params = (norm_gains, shift_biases, head_biases, hidden_bias, position_table)
    small_moms = (
        gain_momentum,
        shift_momentum,
        head_bias_momentum,
        hidden_bias_momentum,
        table_momentum,
    )
    small_moms_new = tuple(
        (MOMENTUM * old_state + grad_part for old_state, grad_part in zip(small_moms, small_grads))
    )
    small_new = tuple(
        (param - VECTOR_RATE * state for param, state in zip(small_params, small_moms_new))
    )
    return (
        output,
        grad_input,
        weight_grads[0],
        weight_grads[1],
        weight_grads[2],
        weight_grads[3],
        weights_new[0],
        weights_new[1],
        weights_new[2],
        weights_new[3],
        momenta_new[0],
        momenta_new[1],
        momenta_new[2],
        momenta_new[3],
        small_grads[0],
        small_grads[1],
        small_grads[2],
        small_grads[3],
        small_grads[4],
        small_new[0],
        small_new[1],
        small_new[2],
        small_new[3],
        small_new[4],
        small_moms_new[0],
        small_moms_new[1],
        small_moms_new[2],
        small_moms_new[3],
        small_moms_new[4],
    )


def solution(mesh):
    return jax.shard_map(
        shards,
        mesh=mesh,
        in_specs=(
            P(("dp", "tensor"), None),
            P(("dp", "tensor"), None),
            P(None, "tensor", "dp"),
            P("tensor", "dp", None),
            P(None, "tensor", "dp"),
            P("tensor", "dp", None),
            P(None, "tensor", "dp"),
            P("tensor", "dp", None),
            P(None, "tensor", "dp"),
            P("tensor", "dp", None),
            P(),
            P(),
            P(),
            P(),
            P(),
            P(),
            P(),
            P(),
            P(),
            P(),
            P(),
            P(),
        ),
        out_specs=(
            P(("dp", "tensor"), None),
            P(("dp", "tensor"), None),
            P(None, "tensor", "dp"),
            P("tensor", "dp", None),
            P(None, "tensor", "dp"),
            P("tensor", "dp", None),
            P(None, "tensor", "dp"),
            P("tensor", "dp", None),
            P(None, "tensor", "dp"),
            P("tensor", "dp", None),
            P(None, "tensor", "dp"),
            P("tensor", "dp", None),
            P(None, "tensor", "dp"),
            P("tensor", "dp", None),
            P(),
            P(),
            P(),
            P(),
            P(),
            P(),
            P(),
            P(),
            P(),
            P(),
            P(),
            P(),
            P(),
            P(),
            P(),
        ),
        check_vma=False,
    )
```

profile of v0, /device:TPU:17, one launch (start us, length us, event | category | flops | bytes accessed | tf_op | source)
XLA Modules:
  0.0 1602.8 jit_solution(16248194538489750883)
XLA Ops:
  14.6 22.3 %all_gather.38 = bf16[1,128,512]{2,1,0:T(8,128)(2,1)} all-gather(bf16[1,16,512]{2,1,0:T(8,128)(2,1)S(1)} %convert_element_type.235), channel_id=1, replica_groups=mesh['dp'=8,'tensor'=4] {'dp'}, dimensions={1}, use_global_device_ids=true | all-gather | bytes 147456 | tf_op jit(solution)/shard_map/all_gather | solution.py:247
  36.9 27.3 %all_gather.37 = bf16[512,1,384]{0,2,1:T(8,128)(2,1)} all-gather(bf16[512,1,48]{0,2,1:T(8,128)(2,1)S(1)} %convert_element_type.234), channel_id=1, replica_groups=mesh['dp'=8,'tensor'=4] {'dp'}, dimensions={2}, use_global_device_ids=true | all-gather | bytes 442368 | tf_op jit(solution)/shard_map/all_gather | solution.py:246
  80.8 25.1 %copy.342 = bf16[6272,1,2,128]{3,2,0,1:T(2,128)(2,1)} copy(bf16[6272,1,2,128]{3,0,2,1:T(8,128)(2,1)} %copy.384) | data formatting | bytes 6422528 | tf_op jit(solution)/shard_map/slice | solution.py:282
  109.6 9.9 concatenate.74
  119.5 7.6 fusion.51
  138.7 14.4 fusion.49
  157.1 9.0 copy.345
  166.1 27.5 %reshape_reshape_reshape.16 = bf16[8,16,49,1,3,4,32]{6,5,1,0,4,2,3:T(4,128)(2,1)} reshape(bf16[32,2,2,7,7,1,3,128]{7,2,1,0,6,4,3,5:T(2,128)(2,1)} %copy.345) | data formatting | bytes 9633792 | tf_op jit(solution)/shard_map/reshape;reshape;reshape | solution.py:137
  193.6 39.7 %copy.347 = bf16[8,16,49,1,3,4,32]{2,6,5,1,4,3,0:T(8,128)(2,1)} copy(bf16[8,16,49,1,3,4,32]{6,5,1,0,4,2,3:T(4,128)(2,1)} %reshape_reshape_reshape.16) | data formatting | bytes 9633792
  233.3 45.8 %while.26 = (s32[]{:T(128)}, bf16[8,16,49,1,4,32]{2,5,4,1,3,0:T(8,128)(2,1)}, f32[8,16,1,4,49,1]{4,3,1,5,2,0:T(4,128)}, bf16[8,16,49,1,3,4,32]{2,6,5,1,4,3,0:T(8...) while((s32[]{:T(128)}, bf16[8,16,49,1,4,32]{2,5,4,1,3,0:T(8,128)(2,1)}, ...), condition=%wide.region_5.6_spmd.clone, body=%wide.region_2.5_spmd.clone.sunk | while | flops 20841856 | bytes 7733161 | solution.py:148
  279.2 15.8 copy.348
  295.0 10.2 reshape_reshape_reshape.18
  318.9 76.5 %reduce-scatter.10.cloned.1.call-done = bf16[1568,512]{1,0:T(8,128)(2,1)} async-done(((bf16[6272,512]{1,0:T(8,128)(2,1)}), bf16[1568,512]{1,0:T(8,128)(2,1)}) %reduce-scatter.10.cloned.1.call-update) | async-done | bytes 1605648 | tf_op jit(solution)/shard_map/reduce_scatter | solution.py:290
  404.9 22.1 %all_gather.41 = bf16[1,512,512]{2,1,0:T(8,128)(2,1)S(1)} all-gather(bf16[1,64,512]{2,1,0:T(8,128)(2,1)S(1)} %convert_element_type.241), channel_id=1, replica_groups=mesh['dp'=8,'tensor'=4] {'dp'}, dimensions={1}, use_global_device_ids=true | all-gather | bytes 589824 | tf_op jit(solution)/shard_map/all_gather | solution.py:249
  427.0 25.3 %all_gather.40 = bf16[512,1,512]{0,2,1:T(8,128)(2,1)S(1)} all-gather(bf16[512,1,64]{0,2,1:T(8,128)(2,1)S(1)} %convert_element_type.239), channel_id=1, replica_groups=mesh['dp'=8,'tensor'=4] {'dp'}, dimensions={2}, use_global_device_ids=true | all-gather | bytes 589824 | tf_op jit(solution)/shard_map/all_gather | solution.py:248
  452.3 10.7 fusion.103
  463.0 34.2 %all-gather.9.cloned.1.call-done = bf16[6272,512]{1,0:T(8,128)(2,1)} async-done(((bf16[1568,512]{1,0:T(8,128)(2,1)}), bf16[6272,512]{1,0:T(8,128)(2,1)}) %all-gather.9.cloned.1.call-update) | async-done | bytes 6422544 | tf_op jit(solution)/shard_map/all_gather | solution.py:315
  497.2 17.5 %fusion.118 = (f32[512]{0:T(512)S(1)}, bf16[6272,512]{1,0:T(8,128)(2,1)S(1)}, bf16[6272,512]{1,0:T(8,128)(2,1)}) fusion(f32[6272,512]{1,0:T(8,128)} %fusion.103, f32[512]{0:T(512)S(1)} %bitcast.508, bf16[6272,512]{1,0:T(8,128)(2,1)} %all-gather.9.cloned.1.call-done, bf16[1,512,512]{2,1,0:T(8,128)(2,1)S(1)} %all_gather.41), kind=kOutput, calls=%fused_computation.276 | convolution fusion | flops 3365404160 | bytes 32641024 | tf_op jit(solution)/shard_map/td,gfd->tgf/dot_general | solution.py:317
  522.8 8.2 convolution_convert_fusion.3
  531.1 10.3 fusion.88
  543.6 10.2 fusion.87
  553.9 28.3 %reduce-scatter.14.cloned.1.call-done = bf16[1568,512]{1,0:T(8,128)(2,1)} async-done(((bf16[6272,512]{1,0:T(8,128)(2,1)}), bf16[1568,512]{1,0:T(8,128)(2,1)}) %reduce-scatter.14.cloned.1.call-update) | async-done | bytes 1605648 | tf_op jit(solution)/shard_map/reduce_scatter | solution.py:327
  585.7 58.6 %reduce-scatter.12.cloned.1.call-done = bf16[1568,512]{1,0:T(8,128)(2,1)} async-done(((bf16[6272,512]{1,0:T(8,128)(2,1)}), bf16[1568,512]{1,0:T(8,128)(2,1)}) %reduce-scatter.12.cloned.1.call-update) | async-done | bytes 1605648 | tf_op jit(solution)/shard_map/reduce_scatter | solution.py:305
  656.5 50.9 %reduce-scatter.22.cloned.1.call-done = bf16[64,512]{1,0:T(8,128)(2,1)} async-done(((bf16[512,512]{1,0:T(8,128)(2,1)}), bf16[64,512]{1,0:T(8,128)(2,1)}) %reduce-scatter.22.cloned.1.call-update) | async-done | bytes 65552
  710.0 62.5 %reduce-scatter.20.cloned.1.call-done = bf16[1,64,512]{2,1,0:T(8,128)(2,1)} async-done(((bf16[1,512,512]{2,1,0:T(8,128)(2,1)}), bf16[1,64,512]{2,1,0:T(8,128)(2,1)}) %reduce-scatter.20.cloned.1.call-update) | async-done | bytes 65552 | tf_op jit(solution)/shard_map/reduce_scatter | solution.py:407
  775.3 23.1 %all_gather.47 = bf16[1,512,512]{2,1,0:T(8,128)(2,1)S(1)} all-gather(bf16[1,64,512]{2,1,0:T(8,128)(2,1)S(1)} %convert_element_type.269), channel_id=1, replica_groups=mesh['dp'=8,'tensor'=4] {'dp'}, dimensions={1}, use_global_device_ids=true | all-gather | bytes 589824 | tf_op jit(solution)/shard_map/all_gather | solution.py:441
  800.5 24.9 %all_gather.46 = bf16[512,1,512]{0,2,1:T(8,128)(2,1)S(1)} all-gather(bf16[512,1,64]{0,2,1:T(8,128)(2,1)S(1)} %copy.362), channel_id=1, replica_groups=mesh['dp'=8,'tensor'=4] {'dp'}, dimensions={2}, use_global_device_ids=true | all-gather | bytes 589824 | tf_op jit(solution)/shard_map/all_gather | solution.py:438
  844.5 14.0 copy.354
  858.5 92.0 %while.27 = (s32[]{:T(128)}, f32[8,16,49,1,3,4,32]{2,6,5,1,4,3,0:T(8,128)}, f32[8,1,4,49,49]{3,4,2,1,0:T(8,128)}, bf16[8,16,49,1,3,4,32]{2,6,5,1,4,3,0:T(8,128)(...) while((s32[]{:T(128)}, ...), condition=%wide.region_16.17_spmd.clone, body=%wide.region_13.16_spmd.clone.sunk | while | flops 51398844 | bytes 18672812 | solution.py:171
  950.6 50.0 %copy.355 = f32[8,16,49,1,3,4,32]{6,5,1,0,4,2,3:T(4,128)} copy(f32[8,16,49,1,3,4,32]{2,6,5,1,4,3,0:T(8,128)} %get-tuple-element.144) | data formatting | bytes 19267584 | tf_op jit(solution)/shard_map/while | solution.py:171
  1000.6 34.1 %reshape_reshape_reshape.20 = f32[32,2,2,7,7,1,3,128]{7,2,1,0,6,4,3,5:T(2,128)} reshape(f32[8,16,49,1,3,4,32]{6,5,1,0,4,2,3:T(4,128)} %copy.355) | data formatting | bytes 19267584 | tf_op jit(solution)/shard_map/reshape;reshape;reshape | solution.py:76
  1057.6 8.3 fusion.93
  1068.2 8.3 convolution_convert_fusion.1
  1076.5 46.5 %reduce-scatter.18.cloned.1.call-done = bf16[1,16,512]{2,1,0:T(8,128)(2,1)} async-done(((bf16[1,128,512]{2,1,0:T(8,128)(2,1)}), bf16[1,16,512]{2,1,0:T(8,128)(2,1)}) %reduce-scatter.18.cloned.1.call-update) | async-done | bytes 16400 | tf_op jit(solution)/shard_map/reduce_scatter | solution.py:401
  1125.6 22.0 %all_gather.45 = bf16[1,128,512]{2,1,0:T(8,128)(2,1)S(1)} all-gather(bf16[1,16,512]{2,1,0:T(8,128)(2,1)S(1)} %convert_element_type.267), channel_id=1, replica_groups=mesh['dp'=8,'tensor'=4] {'dp'}, dimensions={1}, use_global_device_ids=true | all-gather | bytes 147456 | tf_op jit(solution)/shard_map/all_gather | solution.py:435
  1148.4 52.5 %all-reduce.8.cloned.1.call-done = bf16[512,1,384]{0,1,2:T(2,128)(2,1)} async-done(((bf16[512,1,384]{0,1,2:T(2,128)(2,1)}), bf16[512,1,384]{0,1,2:T(2,128)(2,1)}) %all-reduce.8.cloned.1.call-update) | async-done | bytes 393232
  1203.8 24.2 %all_gather.44 = bf16[512,1,384]{0,2,1:T(8,128)(2,1)} all-gather(bf16[512,1,48]{0,2,1:T(8,128)(2,1)S(1)} %convert_element_type.266), channel_id=1, replica_groups=mesh['dp'=8,'tensor'=4] {'dp'}, dimensions={2}, use_global_device_ids=true | all-gather | bytes 442368 | tf_op jit(solution)/shard_map/all_gather | solution.py:432
  1233.6 9.4 pad_maximum_fusion.5
  1243.5 15.5 reduce.33
  1264.1 12.1 all-to-all-start
  1281.2 13.9 copy.371
  1313.2 42.9 %all-reduce.5 = (f32[4]{0:T(128)S(1)}, f32[2,512]{1,0:T(2,128)S(1)}, f32[4,512]{1,0:T(4,128)S(1)}, f32[2,512]{1,0:T(2,128)S(1)}, f32[2048]{0:T(1024)S(1)}, /*index=5*/f32[169,16]{0,1:T(8,128)S(1)}) all-reduce(f32[4]{0:T(128)S(1)} %pad_maximum_fusion.12, ...), channel_id=1, replica_groups=mesh['dp'=8,'tensor'=4] {'dp','tensor'}, use_global_device_ids=true, to_apply=%region_28.29 | all-reduce | flops 8852 | bytes 70816 | tf_op jit(solution)/shard_map/psum | solution.py:428
  1356.1 71.7 %conditional.1 = (bf16[4,262144]{1,0:T(4,128)(2,1)}) conditional(s32[]{:T(128)} %clamp.3, (bf16[4,1,262144]{2,1,0:T(2,128)(2,1)}, f32[4]{0:T(128)S(1)}) %tuple.30, (bf16[4,1,262144]{2,1,0:T(2,128)(2,1)}, f32[4]{0:T(128)S(1)}) %tuple.30, (bf16[4,1,262144]{2,1,0:T(2,128)(2,1)}, f32[4]{0:T(128)S(1)}) %tuple.30, ...), branch_computations={%region_29.30_spmd, %region_30.31_spmd, %region_31.32_spmd, %regio... | conditional | flops 72495136768 | bytes 117440584 | solution.py:461
  1435.2 15.5 reduce.34
  1455.9 71.7 %all-to-all-start.1 = ((bf16[4,2,131072]{2,1,0:T(2,128)(2,1)}), bf16[4,2,131072]{2,1,0:T(2,128)(2,1)}, u32[]{:S(2)}, u32[]{:S(2)}) async-start(bf16[4,2,131072]{2,1,0:T(2,128)(2,1)} %reshape.671), calls=%async_computation.7 | async-start | bytes 4194304 | tf_op jit(solution)/shard_map/all_to_all | solution.py:462
  1534.9 17.6 %all-to-all-done.1 = bf16[4,2,131072]{2,1,0:T(2,128)(2,1)} async-done(((bf16[4,2,131072]{2,1,0:T(2,128)(2,1)}), bf16[4,2,131072]{2,1,0:T(2,128)(2,1)}, u32[]{:S(2)}, u32[]{:S(2)}) %all-to-all-start.1) | async-done | bytes 2097184 | tf_op jit(solution)/shard_map/all_to_all | solution.py:462
  1569.7 8.1 slice_reduce_fusion.4
  1577.9 11.2 slice_reduce_fusion.2
  (531 shorter events, 411.9 us)
Async XLA Ops:
  7.2 58.4 %all-gather.5.cloned.1.call-start = ((), (), s32[]{:S(2)}) async-start(), calls=%async_computation.9 | async-start | bytes 8028160 | tf_op jit(solution)/shard_map/all_gather | solution.py:275
  14.0 381.3 %reduce-scatter.10.cloned.1.call-start = ((), (), s32[]{:S(2)}) async-start(), calls=%async_computation.10 | async-start | bytes 8028160 | tf_op jit(solution)/shard_map/reduce_scatter | solution.py:290
  14.3 57.0 %copy-start.52 = (s32[2401]{0:T(1024)}, s32[2401]{0:T(1024)S(1)}, u32[]{:S(2)}) copy-start(s32[2401]{0:T(1024)S(1)} %eq.34) | copy-start | bytes 28816
  119.5 7.6 copy-start.6
  318.8 76.6 %copy-start.63 = (f32[1,512]{1,0:T(1,128)S(1)}, f32[1,512]{1,0:T(1,128)}, u32[]{:S(2)}) copy-start(f32[1,512]{1,0:T(1,128)} %get-tuple-element.643) | copy-start | bytes 6148
  318.9 133.5 %all-gather.7.cloned.1.call-start = ((), (), s32[]{:S(2)}) async-start(), calls=%async_computation.11 | async-start | bytes 8028160 | tf_op jit(solution)/shard_map/all_gather | solution.py:301
  400.8 96.4 %all-gather.9.cloned.1.call-start = ((), (), s32[]{:S(2)}) async-start(), calls=%async_computation.13 | async-start | bytes 8028160 | tf_op jit(solution)/shard_map/all_gather | solution.py:315
  403.0 179.2 %reduce-scatter.14.cloned.1.call-start = ((), (), s32[]{:S(2)}) async-start(), calls=%async_computation.14 | async-start | bytes 8028160 | tf_op jit(solution)/shard_map/reduce_scatter | solution.py:327
  522.8 121.5 %reduce-scatter.12.cloned.1.call-start = ((), (), s32[]{:S(2)}) async-start(), calls=%async_computation.12 | async-start | bytes 8028160 | tf_op jit(solution)/shard_map/reduce_scatter | solution.py:305
  531.1 176.4 %reduce-scatter.22.cloned.1.call-start = ((), (), s32[]{:S(2)}) async-start(), calls=%async_computation.19 | async-start | bytes 589824
  543.3 38.8 %copy-start.3 = (f32[1568,512]{1,0:T(8,128)S(1)}, f32[1568,512]{1,0:T(8,128)}, u32[]{:S(2)}) copy-start(f32[1568,512]{1,0:T(8,128)} %copy-done.2) | copy-start | bytes 9633796
  543.3 229.1 %reduce-scatter.20.cloned.1.call-start = ((), (), s32[]{:S(2)}) async-start(), calls=%async_computation.18 | async-start | bytes 589824 | tf_op jit(solution)/shard_map/reduce_scatter | solution.py:407
  553.8 90.5 %copy-start.58 = (f32[1,512]{1,0:T(1,128)S(1)}, f32[1,512]{1,0:T(1,128)}, u32[]{:S(2)}) copy-start(f32[1,512]{1,0:T(1,128)} %get-tuple-element.641) | copy-start | bytes 6148
  553.8 273.1 %all-gather.11.cloned.1.call-start = ((), (), s32[]{:S(2)}) async-start(), calls=%async_computation.15 | async-start | bytes 8028160 | tf_op jit(solution)/shard_map/all_gather | solution.py:337
  651.3 121.1 %copy-start.34 = (f32[1,64,512]{2,1,0:T(8,128)S(1)}, f32[1,64,512]{2,1,0:T(8,128)}, u32[]{:S(2)}) copy-start(f32[1,64,512]{2,1,0:T(8,128)} %param.39) | copy-start | bytes 393220
  652.7 470.4 %reduce-scatter.18.cloned.1.call-start = ((), (), s32[]{:S(2)}) async-start(), calls=%async_computation.17 | async-start | bytes 147456 | tf_op jit(solution)/shard_map/reduce_scatter | solution.py:401
  708.5 118.4 %copy-start.17 = (bf16[1,128,512]{2,1,0:T(8,128)(2,1)S(1)}, bf16[1,128,512]{2,1,0:T(8,128)(2,1)}, u32[]{:S(2)}) copy-start(bf16[1,128,512]{2,1,0:T(8,128)(2,1)} %all_gather.38) | copy-start | bytes 393220
  1047.3 153.6 %all-reduce.8.cloned.1.call-start = ((), (), s32[]{:S(2)}) async-start(), calls=%async_computation.20 | async-start | bytes 1572864
  1057.6 8.3 copy-start.19
  1057.6 10.6 copy-start.22
  1068.2 241.8 %reduce-scatter.16.cloned.1.call-start = ((), (), s32[]{:S(2)}) async-start(), calls=%async_computation.16 | async-start | bytes 8028160 | tf_op jit(solution)/shard_map/reduce_scatter | solution.py:357
  1076.5 46.6 %copy-start.41 = (f32[1,16,512]{2,1,0:T(8,128)S(1)}, f32[1,16,512]{2,1,0:T(8,128)}, u32[]{:S(2)}) copy-start(f32[1,16,512]{2,1,0:T(8,128)} %param.37) | copy-start | bytes 98308
  1076.5 125.4 %copy-start.35 = (f32[512,1,48]{0,2,1:T(8,128)S(1)}, f32[512,1,48]{0,2,1:T(8,128)}, u32[]{:S(2)}) copy-start(f32[512,1,48]{0,2,1:T(8,128)} %param.36) | copy-start | bytes 294916
  1076.5 157.1 %copy-start.13 = (bf16[1,1,262144]{2,1,0:T(2,128)(2,1)S(1)}, bf16[1,1,262144]{2,1,0:T(2,128)(2,1)}, u32[]{:S(2)}) copy-start(bf16[1,1,262144]{2,1,0:T(2,128)(2,1)} %stack.83) | copy-start | bytes 1572868
  1076.5 157.1 %copy-start.14 = (bf16[1,1,262144]{2,1,0:T(2,128)(2,1)S(1)}, bf16[1,1,262144]{2,1,0:T(2,128)(2,1)}, u32[]{:S(2)}) copy-start(bf16[1,1,262144]{2,1,0:T(2,128)(2,1)} %stack.82) | copy-start | bytes 1572868
  1259.0 17.3 %copy-start.53 = (s32[2401]{0:T(1024)S(1)}, s32[2401]{0:T(1024)}, u32[]{:S(2)}) copy-start(s32[2401]{0:T(1024)} %copy-done.52) | copy-start | bytes 28816
  1259.0 18.2 %copy-start.10 = (f32[32,3,14,1,3,128]{5,0,4,3,2,1:T(8,128)S(1)}, f32[32,3,14,1,3,128]{5,0,4,3,2,1:T(8,128)}, u32[]{:S(2)}) copy-start(f32[32,3,14,1,3,128]{5,0,4,3,2,1:T(8,128)} %slice.216) | copy-start | bytes 6193156
  1264.1 40.9 %all-to-all-start = ((bf16[4,2,131072]{2,1,0:T(2,128)(2,1)}), bf16[4,2,131072]{2,1,0:T(2,128)(2,1)}, u32[]{:S(2)}, u32[]{:S(2)}) async-start(bf16[4,2,131072]{2,1,0:T(2,128)(2,1)} %reshape.669), calls=%async_computation.6 | async-start | bytes 4194304 | tf_op jit(solution)/shard_map/all_to_all | solution.py:451
  1301.8 8.2 copy-start.1
  1301.8 8.2 copy-start.27
  1301.8 8.2 copy-start.29
  1301.9 8.2 copy-start.39
  1305.0 8.1 copy-start.54
  1305.0 8.2 copy-start.55
  1305.0 8.2 copy-start.56
  1305.0 8.2 copy-start.57
  1305.0 8.2 copy-start.46
  1450.7 76.9 %copy-start.48 = (f32[2,512]{1,0:T(2,128)S(1)}, f32[2,512]{1,0:T(2,128)}, u32[]{:S(2)}) copy-start(f32[2,512]{1,0:T(2,128)} %param.40) | copy-start | bytes 12292
  1450.7 76.9 %copy-start.64 = (f32[2,512]{1,0:T(2,128)S(1)}, f32[2,512]{1,0:T(2,128)}, u32[]{:S(2)}) copy-start(f32[2,512]{1,0:T(2,128)} %param.45) | copy-start | bytes 12292
  1450.7 77.5 %copy-start.50 = (f32[2,512]{1,0:T(2,128)S(1)}, f32[2,512]{1,0:T(2,128)}, u32[]{:S(2)}) copy-start(f32[2,512]{1,0:T(2,128)} %param.42) | copy-start | bytes 12292
  1450.7 77.5 %copy-start.65 = (f32[2,512]{1,0:T(2,128)S(1)}, f32[2,512]{1,0:T(2,128)}, u32[]{:S(2)}) copy-start(f32[2,512]{1,0:T(2,128)} %param.47) | copy-start | bytes 12292
  1450.7 78.1 %copy-start.43 = (f32[4,512]{1,0:T(4,128)S(1)}, f32[4,512]{1,0:T(4,128)}, u32[]{:S(2)}) copy-start(f32[4,512]{1,0:T(4,128)} %param.41) | copy-start | bytes 24580
  1450.7 78.1 %copy-start.61 = (f32[4,512]{1,0:T(4,128)S(1)}, f32[4,512]{1,0:T(4,128)}, u32[]{:S(2)}) copy-start(f32[4,512]{1,0:T(4,128)} %param.46) | copy-start | bytes 24580
  1450.8 78.7 %copy-start.45 = (f32[2048]{0:T(1024)S(1)}, f32[2048]{0:T(1024)}, u32[]{:S(2)}) copy-start(f32[2048]{0:T(1024)} %param.43) | copy-start | bytes 24580
  1450.8 78.7 %copy-start.62 = (f32[2048]{0:T(1024)S(1)}, f32[2048]{0:T(1024)}, u32[]{:S(2)}) copy-start(f32[2048]{0:T(1024)} %param.48) | copy-start | bytes 24580
  1450.8 79.3 %copy-start.37 = (f32[169,16]{0,1:T(8,128)S(1)}, f32[169,16]{0,1:T(8,128)}, u32[]{:S(2)}) copy-start(f32[169,16]{0,1:T(8,128)} %param.44) | copy-start | bytes 32452
  1450.8 79.3 %copy-start.51 = (f32[169,16]{0,1:T(8,128)S(1)}, f32[169,16]{0,1:T(8,128)}, u32[]{:S(2)}) copy-start(f32[169,16]{0,1:T(8,128)} %param.49) | copy-start | bytes 32452
  1455.9 96.5 %all-to-all-start.1 = ((bf16[4,2,131072]{2,1,0:T(2,128)(2,1)}), bf16[4,2,131072]{2,1,0:T(2,128)(2,1)}, u32[]{:S(2)}, u32[]{:S(2)}) async-start(bf16[4,2,131072]{2,1,0:T(2,128)(2,1)} %reshape.671), calls=%async_computation.7 | async-start | bytes 4194304 | tf_op jit(solution)/shard_map/all_to_all | solution.py:462
  (49 other events, 142.8 us)
Sparse Core Ops, SparseCore 0:
  14.2 48.5 all-gather.4
  319.0 76.3 reduce-scatter.9
  400.9 47.6 all-gather.6
  450.0 47.0 all-gather.8
  522.9 59.1 reduce-scatter.13
  584.5 59.7 reduce-scatter.11
  647.7 59.7 reduce-scatter.21
  710.8 61.6 reduce-scatter.19
  774.0 49.4 all-gather.10
  1047.4 75.5 reduce-scatter.17
  1126.5 74.3 all-reduce.7
  1203.3 61.5 reduce-scatter.15
where the time goes:
time: 1620 us; the launch traced here: 1600 us
  local copies, waits for them, and re-layouts  453 us (28%)
  waiting for transfers between devices  428 us (26%)
  blocking collectives  234 us (14%)
  matrix products  189 us (12%)
  other arithmetic  174 us (11%)
  starting transfers between devices  84.5 us (5%)
  loops' own time  24.9 us (2%)
  between operations  16.3 us (1%)
    unnamed x14, waiting for transfers between devices  104 us
    unnamed x155, local copies, waits for them, and re-layouts  97.7 us
    reduce_scatter x1, waiting for transfers between devices, shards(): lax.psum_scatter(jnp.einsum('tgc,gcd->td', part_rows, w_proj, preferred_e...  76.5 us
    all_to_all x1, starting transfers between devices, shards(): lax.all_to_all(shortened(results), 'tensor', split_axis=1, concat_axis=0,...  71.7 us
    reduce_scatter x1, waiting for transfers between devices, shards(): lax.psum_scatter(grad_fc2.astype(jnp.bfloat16), 'dp', scatter_dimension=1...  62.5 us
    reduce_scatter x1, waiting for transfers between devices, shards(): lax.psum_scatter(jnp.einsum('tgf,gfd->td', part_rows, w_fc2, preferred_el...  58.6 us
    while x1, local copies, waits for them, and re-layouts, attention_back(): lax.map(backward_one, (shaped, log_total, grad_shaped))  50 us
    reduce_scatter x1, waiting for transfers between devices, shards(): lax.psum_scatter(grad_proj.astype(jnp.bfloat16), 'dp', scatter_dimension=...  46.5 us
  transfers between devices with their start and end apart: 14, of which 9 were waited for; matrix products, arithmetic and copies ran while one was open for 11% of the time, Pallas kernels for 0%

commit v1 on v0

v1 whole, which is shorter than its diff:
```python
import functools
import math

import jax
import jax.numpy as jnp
from jax import lax
from jax.experimental import pallas as pl
from jax.experimental.pallas import tpu as pltpu
from jax.sharding import PartitionSpec as P

D = 512
HEADS = 16
FF = 2048
HEAD = 32
WIN = 7
SIDE = 14
SHIFT = 3
NS_STEPS = 5

NORM_EPSILON = 1e-05
MASK_VALUE = -100.0
MUON_EPSILON = 1e-07
QUINTIC = (3.4445, -4.775, 2.0315)
MOMENTUM = 0.9
MATRIX_RATE = 0.5
VECTOR_RATE = 1.0

AREA = SIDE * SIDE
SPOTS = WIN * WIN
ACROSS = SIDE // WIN
WINDOWS = ACROSS * ACROSS
SLOT = 64
LANES = 128
OCT = 8
OCTS = HEADS // OCT
OCT_W = OCT * HEAD
OCT_S = OCT * SLOT
PAD_SCORE = -1e30
STEP_IMAGES = 2
STEP_ROWS = STEP_IMAGES * AREA
STEP_SLOTS = STEP_IMAGES * WINDOWS * SLOT
PART = 128
GROUPS = 4
F32 = jnp.float32
BF16 = jnp.bfloat16
VMEM_LIMIT = 60 * 1024 * 1024


def window_pieces():
    pieces = []
    for down in range(ACROSS):
        for over in range(ACROSS):
            for line in range(WIN):
                src_row = (down * WIN + line + SHIFT) % SIDE
                column = 0
                while column < WIN:
                    src_col = (over * WIN + column + SHIFT) % SIDE
                    length = min(WIN - column, SIDE - src_col)
                    slot = (down * ACROSS + over) * SLOT + line * WIN + column
                    pieces.append((slot, src_row * SIDE + src_col, length))
                    column += length
    return pieces


PIECES = window_pieces()


def dot_nn(a, b):
    return lax.dot_general(a, b, (((1,), (0,)), ((), ())), preferred_element_type=F32)


def dot_nt(a, b):
    return lax.dot_general(a, b, (((1,), (1,)), ((), ())), preferred_element_type=F32)


def dot_tn(a, b):
    return lax.dot_general(a, b, (((0,), (0,)), ((), ())), preferred_element_type=F32)


def row_mean(values):
    return jnp.mean(values, axis=-1, keepdims=True)


def whiten(values):
    center = values - row_mean(values)
    inverse = lax.rsqrt(row_mean(center * center) + NORM_EPSILON)
    return center * inverse, inverse


def into_slots(src_ref, dst_ref):
    for image in range(STEP_IMAGES):
        for slot, raster, length in PIECES:
            dst_ref[image * WINDOWS * SLOT + slot : image * WINDOWS * SLOT + slot + length, :] = src_ref[
                image * AREA + raster : image * AREA + raster + length, :
            ]


def out_of_slots(src_ref, dst_ref):
    for image in range(STEP_IMAGES):
        for slot, raster, length in PIECES:
            dst_ref[image * AREA + raster : image * AREA + raster + length, :] = src_ref[
                image * WINDOWS * SLOT + slot : image * WINDOWS * SLOT + slot + length, :
            ]


def head_mask(order):
    rows = lax.broadcasted_iota(jnp.int32, (SLOT, OCT_W), 1) // HEAD
    return jnp.concatenate([(rows == head).astype(F32) for head in order], axis=0).astype(BF16)


def spread(values, mask_ref):
    return jnp.concatenate([values] * OCT, axis=0) * mask_ref[...]


def lane_iota(rows):
    return lax.broadcasted_iota(jnp.int32, (rows, LANES), 1)


def build_bias(region_ref, index_ref, table_ref, bias_ref, idx_scr, tab_scr):
    idx_scr[...] = jnp.zeros_like(idx_scr)
    idx_scr[0:SPOTS, 0:SPOTS] = index_ref[...].astype(F32)
    heads, rows = table_ref.shape
    tab_scr[...] = jnp.zeros_like(tab_scr)
    tab_scr[:, 0:rows] = table_ref[...]
    by_head = tab_scr[...]
    index = idx_scr[...].T[0:SLOT, :]
    lanes = lane_iota(SLOT)
    index = jnp.where(lanes < SLOT, index, pltpu.roll(index, SLOT, 1)).astype(jnp.int32)
    sublanes = lax.broadcasted_iota(jnp.int32, (SLOT, LANES), 0)
    spot = lanes % SLOT
    masks = []
    for down in range(ACROSS):
        for over in range(ACROSS):
            row_ids = jnp.full((SLOT, LANES), -1, jnp.int32)
            col_ids = jnp.full((SLOT, LANES), -1, jnp.int32)
            for at in range(SPOTS):
                value = region_ref[down * WIN + at // WIN, over * WIN + at % WIN]
                row_ids = jnp.where(sublanes == at, value, row_ids)
                col_ids = jnp.where(spot == at, value, col_ids)
            masks.append(
                jnp.where(sublanes < SPOTS, jnp.where(row_ids == col_ids, 0.0, MASK_VALUE), PAD_SCORE)
            )
    low = index < LANES
    index_low = jnp.where(low, index, 0)
    index_high = jnp.where(low, 0, index - LANES)

    def gathered(head):
        first = jnp.broadcast_to(by_head[head : head + 1, 0:LANES], (SLOT, LANES))
        second = jnp.broadcast_to(by_head[head : head + 1, LANES : 2 * LANES], (SLOT, LANES))
        return jnp.where(
            low,
            jnp.take_along_axis(first, index_low, axis=1),
            jnp.take_along_axis(second, index_high, axis=1),
        )

    for octet in range(OCTS):
        for pair in range(OCT // 2):
            head = octet * OCT + 2 * pair
            tile = jnp.where(lanes < SLOT, gathered(head), gathered(head + 1))
            for window in range(WINDOWS):
                bias_ref[window, octet, :, pair * LANES : (pair + 1) * LANES] = tile + masks[window]


TURNED = (0, 2, 1, 3, 4, 6, 5, 7)


def turned(values):
    tiles = []
    for at in range(0, OCT_S, 2 * LANES):
        both = jnp.concatenate([values[:, at : at + LANES], values[:, at + LANES : at + 2 * LANES]], axis=0).T
        tiles += [both[0:SLOT, :], both[SLOT:, :]]
    return jnp.concatenate(tiles, axis=1)


def attention_forward_kernel(
    x_ref,
    wqkv_ref,
    wproj_ref,
    gain_ref,
    shift_ref,
    qkvb_ref,
    table_ref,
    index_ref,
    region_ref,
    y_ref,
    xs_ref,
    qkv_ref,
    p_ref,
    o_ref,
    bias_scr,
    idx_scr,
    tab_scr,
    mask_scr,
    turn_scr,
    y_scr,
):
    @pl.when(pl.program_id(0) == 0)
    def _():
        build_bias(region_ref, index_ref, table_ref, bias_scr, idx_scr, tab_scr)
        mask_scr[...] = head_mask(range(OCT))
        turn_scr[...] = head_mask(TURNED)

    xs_ref[...] = jnp.zeros_like(xs_ref)
    into_slots(x_ref, xs_ref)
    white, _ = whiten(xs_ref[...])
    a1 = (white * gain_ref[0:1, :] + shift_ref[0:1, :]).astype(BF16)
    scale = HEAD ** (-0.5)
    for half in range(2):
        columns = 3 * PART * GROUPS // 2
        u = dot_nt(a1, wqkv_ref[half * columns : (half + 1) * columns, :])
        for inner in range(GROUPS // 2):
            group = half * (GROUPS // 2) + inner
            for part in range(3):
                piece = u[:, (inner * 3 + part) * PART : (inner * 3 + part + 1) * PART]
                if part == 0:
                    piece = (piece + qkvb_ref[0:1, group * PART : (group + 1) * PART]) * scale
                elif part == 2:
                    piece = piece + qkvb_ref[1:2, group * PART : (group + 1) * PART]
                at = part * D + group * PART
                qkv_ref[:, at : at + PART] = piece.astype(BF16)

    real_query = (lax.broadcasted_iota(jnp.int32, (1, OCT_S), 1) % SLOT < SPOTS).astype(F32)

    def one_window(at, carry):
        rows = pl.ds(pl.multiple_of(at * SLOT, SLOT), SLOT)
        for octet in range(OCTS):
            q = qkv_ref[rows, octet * OCT_W : (octet + 1) * OCT_W]
            k = qkv_ref[rows, D + octet * OCT_W : D + (octet + 1) * OCT_W]
            v = qkv_ref[rows, 2 * D + octet * OCT_W : 2 * D + (octet + 1) * OCT_W]
            scores = dot_nt(k, spread(q, mask_scr)) + bias_scr[lax.rem(at, WINDOWS), octet]
            grown = jnp.exp(scores - jnp.max(scores, axis=0, keepdims=True))
            probs = grown * (real_query / jnp.sum(grown, axis=0, keepdims=True))
            p_ref[rows, octet * OCT_S : (octet + 1) * OCT_S] = probs.astype(BF16)
            o_ref[rows, octet * OCT_W : (octet + 1) * OCT_W] = dot_nn(
                turned(probs).astype(BF16), spread(v, turn_scr)
            ).astype(BF16)
        return carry

    lax.fori_loop(0, STEP_IMAGES * WINDOWS, one_window, 0)
    y_scr[...] = xs_ref[...] + dot_nn(o_ref[...], wproj_ref[...]) + shift_ref[2:3, :]
    out_of_slots(y_scr, y_ref)


def mlp_kernel(
    y_ref,
    e_ref,
    w1_ref,
    w2_ref,
    gain_ref,
    shift_ref,
    hb_ref,
    out_ref,
    dy_ref,
    g1_ref,
    g2_ref,
    hsum_ref,
    sums_ref,
    acc1,
    acc2,
    m_scr,
    da_scr,
    a2_scr,
    e_scr,
):
    step = pl.program_id(0)

    @pl.when(step == 0)
    def _():
        acc1[...] = jnp.zeros_like(acc1)
        acc2[...] = jnp.zeros_like(acc2)
        hsum_ref[...] = jnp.zeros_like(hsum_ref)
        sums_ref[...] = jnp.zeros_like(sums_ref)

    white, inverse = whiten(y_ref[...])
    a2_scr[...] = (white * gain_ref[1:2, :] + shift_ref[1:2, :]).astype(BF16)
    e_scr[...] = e_ref[...].astype(BF16)
    m_scr[...] = jnp.zeros_like(m_scr)
    da_scr[...] = jnp.zeros_like(da_scr)
    root = math.sqrt(2.0 / math.pi)
    width = 512

    def chunk(c, carry):
        at = pl.ds(pl.multiple_of(c * width, width), width)
        w1, w2 = w1_ref[at, :], w2_ref[at, :]
        a2, e = a2_scr[...], e_scr[...]
        z = dot_nt(a2, w1) + hb_ref[0:1, at]
        square = z * z
        t = jnp.tanh(z * (root + (root * 0.044715) * square))
        half = 0.5 * z
        f = (half + half * t).astype(BF16)
        slope = 0.5 + 0.5 * t + half * (1.0 - t * t) * (root + (3.0 * root * 0.044715) * square)
        dz = dot_nt(e, w2) * slope
        hsum_ref[0:1, at] += jnp.sum(dz, axis=0, keepdims=True)
        dz = dz.astype(BF16)
        m_scr[...] += dot_nn(f, w2)
        da_scr[...] += dot_nn(dz, w1)
        acc2[at, :] += dot_tn(f, e)
        acc1[at, :] += dot_tn(dz, a2)
        return carry

    lax.fori_loop(0, w1_ref.shape[0] // width, chunk, 0)
    white, inverse = whiten(y_ref[...])
    out_ref[...] = y_ref[...] + m_scr[...] + shift_ref[3:4, :]
    da = da_scr[...]
    t2 = da * gain_ref[1:2, :]
    dy = e_ref[...] + inverse * (t2 - row_mean(t2) - white * row_mean(t2 * white))
    dy_ref[...] = dy
    sums_ref[0:1, :] += jnp.sum(da * white, axis=0, keepdims=True)
    sums_ref[1:2, :] += jnp.sum(da, axis=0, keepdims=True)
    sums_ref[2:3, :] += jnp.sum(dy, axis=0, keepdims=True)
    sums_ref[3:4, :] += jnp.sum(e_ref[...], axis=0, keepdims=True)

    @pl.when(step == pl.num_programs(0) - 1)
    def _():
        g1_ref[...] = acc1[...].astype(BF16)
        g2_ref[...] = acc2[...].astype(BF16)


def attention_backward_kernel(
    dy_ref,
    xs_ref,
    qkv_ref,
    p_ref,
    o_ref,
    wqkv_ref,
    wproj_ref,
    gain_ref,
    shift_ref,
    gin_ref,
    gqkv_ref,
    gproj_ref,
    dbias_ref,
    hsum_ref,
    sums_ref,
    accq,
    accp,
    dy_scr,
    do_scr,
    du_scr,
    mask_scr,
    turn_scr,
    g_scr,
):
    step = pl.program_id(0)

    @pl.when(step == 0)
    def _():
        mask_scr[...] = head_mask(range(OCT))
        turn_scr[...] = head_mask(TURNED)
        accq[...] = jnp.zeros_like(accq)
        accp[...] = jnp.zeros_like(accp)
        dbias_ref[...] = jnp.zeros_like(dbias_ref)
        hsum_ref[...] = jnp.zeros_like(hsum_ref)
        sums_ref[...] = jnp.zeros_like(sums_ref)
        dy_scr[...] = jnp.zeros_like(dy_scr)

    into_slots(dy_ref, dy_scr)
    dr = dy_scr[...].astype(BF16)
    do_scr[...] = dot_nt(dr, wproj_ref[...]).astype(BF16)
    accp[...] += dot_tn(o_ref[...], dr)
    scale = HEAD ** (-0.5)

    def one_window(at, carry):
        rows = pl.ds(pl.multiple_of(at * SLOT, SLOT), SLOT)
        for octet in range(OCTS):
            q = qkv_ref[rows, octet * OCT_W : (octet + 1) * OCT_W]
            k = qkv_ref[rows, D + octet * OCT_W : D + (octet + 1) * OCT_W]
            v = qkv_ref[rows, 2 * D + octet * OCT_W : 2 * D + (octet + 1) * OCT_W]
            do = do_scr[rows, octet * OCT_W : (octet + 1) * OCT_W]
            probs = p_ref[rows, octet * OCT_S : (octet + 1) * OCT_S]
            wide_do = spread(do, mask_scr)
            weighted = probs.astype(F32) * dot_nt(v, wide_do)
            ds = weighted - probs.astype(F32) * jnp.sum(weighted, axis=0, keepdims=True)
            dbias_ref[octet] += ds
            dq = dot_nn(turned(ds).astype(BF16), spread(k, turn_scr)) * scale
            dk = dot_nn(ds.astype(BF16), spread(q, mask_scr))
            dv = dot_nn(probs, wide_do)
            lanes = slice(octet * OCT_W, (octet + 1) * OCT_W)
            hsum_ref[0:1, lanes] += jnp.sum(dq, axis=0, keepdims=True)
            hsum_ref[1:2, lanes] += jnp.sum(dv, axis=0, keepdims=True)
            for part, grad in enumerate((dq, dk, dv)):
                for inner in range(OCT_W // PART):
                    group = octet * (OCT_W // PART) + inner
                    at_col = (group * 3 + part) * PART
                    du_scr[rows, at_col : at_col + PART] = grad[
                        :, inner * PART : (inner + 1) * PART
                    ].astype(BF16)
        return carry

    lax.fori_loop(0, STEP_IMAGES * WINDOWS, one_window, 0)
    white, inverse = whiten(xs_ref[...])
    a1 = (white * gain_ref[0:1, :] + shift_ref[0:1, :]).astype(BF16)
    accq[...] += dot_tn(du_scr[...], a1)
    da = dot_nn(du_scr[...], wqkv_ref[...])
    t1 = da * gain_ref[0:1, :]
    g_scr[...] = dy_scr[...] + inverse * (t1 - row_mean(t1) - white * row_mean(t1 * white))
    out_of_slots(g_scr, gin_ref)
    sums_ref[0:1, :] += jnp.sum(da * white, axis=0, keepdims=True)
    sums_ref[1:2, :] += jnp.sum(da, axis=0, keepdims=True)

    @pl.when(step == pl.num_programs(0) - 1)
    def _():
        gqkv_ref[...] = accq[...].astype(BF16)
        gproj_ref[...] = accp[...].astype(BF16)


def whole(shape):
    return pl.BlockSpec(shape, lambda i: (0,) * len(shape))


def rows_of(rows, columns):
    return pl.BlockSpec((rows, columns), lambda i: (i, 0))


def shape_of(shape, dtype):
    return jax.ShapeDtypeStruct(shape, dtype)


PARAMS = pltpu.CompilerParams(dimension_semantics=("arbitrary",), vmem_limit_bytes=VMEM_LIMIT)


def attention_forward(tokens, wqkv, wproj, gains, shifts, head_biases, table, index, regions):
    steps = tokens.shape[0] // STEP_ROWS
    slots = steps * STEP_SLOTS
    return pl.pallas_call(
        attention_forward_kernel,
        grid=(steps,),
        out_shape=(
            shape_of(tokens.shape, F32),
            shape_of((slots, D), F32),
            shape_of((slots, 3 * D), BF16),
            shape_of((slots, OCTS * OCT_S), BF16),
            shape_of((slots, D), BF16),
        ),
        in_specs=[
            rows_of(STEP_ROWS, D),
            whole(wqkv.shape),
            whole(wproj.shape),
            whole(gains.shape),
            whole(shifts.shape),
            whole(head_biases.shape),
            whole(table.shape),
            whole(index.shape),
            pl.BlockSpec(memory_space=pltpu.SMEM),
        ],
        out_specs=(
            rows_of(STEP_ROWS, D),
            rows_of(STEP_SLOTS, D),
            rows_of(STEP_SLOTS, 3 * D),
            rows_of(STEP_SLOTS, OCTS * OCT_S),
            rows_of(STEP_SLOTS, D),
        ),
        scratch_shapes=[
            pltpu.VMEM((WINDOWS, OCTS, SLOT, OCT_S), F32),
            pltpu.VMEM((LANES, LANES), F32),
            pltpu.VMEM((HEADS, 2 * LANES), F32),
            pltpu.VMEM((OCT_S, OCT_W), BF16),
            pltpu.VMEM((OCT_S, OCT_W), BF16),
            pltpu.VMEM((STEP_SLOTS, D), F32),
        ],
        compiler_params=PARAMS,
        name="attention_forward",
    )(tokens, wqkv, wproj, gains, shifts, head_biases, table, index, regions)


def mlp(middle, out_grad, w1, w2, gains, shifts, hidden_bias):
    steps = middle.shape[0] // STEP_ROWS
    hidden = w1.shape[0]
    return pl.pallas_call(
        mlp_kernel,
        grid=(steps,),
        out_shape=(
            shape_of(middle.shape, F32),
            shape_of(middle.shape, F32),
            shape_of(w1.shape, BF16),
            shape_of(w2.shape, BF16),
            shape_of((1, hidden), F32),
            shape_of((4, D), F32),
        ),
        in_specs=[
            rows_of(STEP_ROWS, D),
            rows_of(STEP_ROWS, D),
            whole(w1.shape),
            whole(w2.shape),
            whole(gains.shape),
            whole(shifts.shape),
            whole((1, hidden)),
        ],
        out_specs=(
            rows_of(STEP_ROWS, D),
            rows_of(STEP_ROWS, D),
            whole(w1.shape),
            whole(w2.shape),
            whole((1, hidden)),
            whole((4, D)),
        ),
        scratch_shapes=[
            pltpu.VMEM(w1.shape, F32),
            pltpu.VMEM(w2.shape, F32),
            pltpu.VMEM((STEP_ROWS, D), F32),
            pltpu.VMEM((STEP_ROWS, D), F32),
            pltpu.VMEM((STEP_ROWS, D), BF16),
            pltpu.VMEM((STEP_ROWS, D), BF16),
        ],
        compiler_params=PARAMS,
        name="mlp",
    )(middle, out_grad, w1, w2, gains, shifts, hidden_bias.reshape(1, hidden))


def attention_backward(dy, xs, qkv, probs, mixed, wqkv, wproj, gains, shifts):
    steps = dy.shape[0] // STEP_ROWS
    return pl.pallas_call(
        attention_backward_kernel,
        grid=(steps,),
        out_shape=(
            shape_of(dy.shape, F32),
            shape_of(wqkv.shape, BF16),
            shape_of(wproj.shape, BF16),
            shape_of((OCTS, SLOT, OCT_S), F32),
            shape_of((2, D), F32),
            shape_of((2, D), F32),
        ),
        in_specs=[
            rows_of(STEP_ROWS, D),
            rows_of(STEP_SLOTS, D),
            rows_of(STEP_SLOTS, 3 * D),
            rows_of(STEP_SLOTS, OCTS * OCT_S),
            rows_of(STEP_SLOTS, D),
            whole(wqkv.shape),
            whole(wproj.shape),
            whole(gains.shape),
            whole(shifts.shape),
        ],
        out_specs=(
            rows_of(STEP_ROWS, D),
            whole(wqkv.shape),
            whole(wproj.shape),
            whole((OCTS, SLOT, OCT_S)),
            whole((2, D)),
            whole((2, D)),
        ),
        scratch_shapes=[
            pltpu.VMEM(wqkv.shape, F32),
            pltpu.VMEM(wproj.shape, F32),
            pltpu.VMEM((STEP_SLOTS, D), F32),
            pltpu.VMEM((STEP_SLOTS, D), BF16),
            pltpu.VMEM((STEP_SLOTS, 3 * D), BF16),
            pltpu.VMEM((OCT_S, OCT_W), BF16),
            pltpu.VMEM((OCT_S, OCT_W), BF16),
            pltpu.VMEM((STEP_SLOTS, D), F32),
        ],
        compiler_params=PARAMS,
        name="attention_backward",
    )(dy, xs, qkv, probs, mixed, wqkv, wproj, gains, shifts)


def newton_schulz_kernel(g_ref, n_ref, w_ref, out_ref, x_scr, a_scr, *, rate):
    first, second, third = QUINTIC
    chunk = 512
    rows = g_ref.shape[0]

    def low(values):
        return values.astype(BF16)

    def gram(src_ref):
        a_scr[...] = jnp.zeros_like(a_scr)

        def add(at, carry):
            part = src_ref[pl.ds(pl.multiple_of(at * chunk, chunk), chunk), :]
            a_scr[...] += dot_tn(part, part)
            return carry

        lax.fori_loop(0, rows // chunk, add, 0)
        return a_scr[...]

    def advance(src_ref, factor, scale):
        factor = low(factor)

        def step(at, carry):
            at = pl.ds(pl.multiple_of(at * chunk, chunk), chunk)
            x_scr[at, :] = low(dot_nn(src_ref[at, :], factor) * scale)
            return carry

        lax.fori_loop(0, rows // chunk, step, 0)

    def bend(a):
        return second * a + third * dot_nn(low(a), low(a))

    diagonal = lax.broadcasted_iota(jnp.int32, (D, D), 0) == lax.broadcasted_iota(jnp.int32, (D, D), 1)

    def two_turns(a):
        b = bend(a)
        q = b + jnp.where(diagonal, first, 0.0)
        r = first * a + dot_nn(low(a), low(b))
        a = first * r + dot_nn(low(r), low(b))
        b = bend(a)
        return first * q + dot_nn(low(b), low(q))

    a = gram(g_ref)
    scale = 1.0 / (jnp.sqrt(jnp.sum(jnp.where(diagonal, a, 0.0))) + MUON_EPSILON)
    q = two_turns(a * scale * scale)
    advance(g_ref, q, scale)
    mine = dot_nn(low(n_ref[...]), low(q)) * scale
    q = two_turns(gram(x_scr))
    advance(x_scr, q, 1.0)
    mine = dot_nn(low(mine), low(q))
    b = bend(gram(x_scr))
    mine = first * mine + dot_nn(low(mine), low(b))
    out_ref[...] = w_ref[...] - rate * mine


def newton_schulz(gathered, slab, weight, factor):
    return pl.pallas_call(
        functools.partial(newton_schulz_kernel, rate=MATRIX_RATE * factor),
        out_shape=shape_of(slab.shape, F32),
        scratch_shapes=[pltpu.VMEM(gathered.shape, BF16), pltpu.VMEM((D, D), F32)],
        compiler_params=pltpu.CompilerParams(vmem_limit_bytes=VMEM_LIMIT),
        name="newton_schulz",
    )(gathered, slab, weight)


ALL = ("tensor", "dp")
WIDE = (True, False, True, False)
FACTORS = (
    math.sqrt(3.0),
    1.0,
    math.sqrt(max(1.0, FF / D)),
    math.sqrt(max(1.0, D / FF)),
)


def as_slab(block, wide):
    return block.reshape(D, -1).T if wide else block.reshape(-1, D)


def as_block(slab, like, wide):
    return (slab.T if wide else slab).reshape(like.shape)


def shards(
    tokens,
    out_grad,
    qkv_weight,
    proj_weight,
    fc1_weight,
    fc2_weight,
    qkv_momentum,
    proj_momentum,
    fc1_momentum,
    fc2_momentum,
    norm_gains,
    shift_biases,
    head_biases,
    hidden_bias,
    position_table,
    gain_momentum,
    shift_momentum,
    head_bias_momentum,
    hidden_bias_momentum,
    table_momentum,
    region_ids,
    position_index,
):
    devices = lax.axis_size("dp") * lax.axis_size("tensor")
    images = tokens.shape[0] // AREA * devices
    blocks = (qkv_weight, proj_weight, fc1_weight, fc2_weight)
    weights = tuple(as_slab(w, wide) for w, wide in zip(blocks, WIDE))
    momenta = tuple(
        as_slab(m, wide)
        for m, wide in zip((qkv_momentum, proj_momentum, fc1_momentum, fc2_momentum), WIDE)
    )
    wqkv, wproj, w1, w2 = (
        lax.all_gather(w.astype(BF16), ALL, axis=0, tiled=True) for w in weights
    )
    middle, xs, qkv, probs, mixed = attention_forward(
        tokens,
        wqkv,
        wproj,
        norm_gains,
        shift_biases,
        head_biases,
        position_table.T,
        position_index,
        region_ids,
    )
    output, dy, g1, g2, hidden_sum, sums2 = mlp(
        middle, out_grad, w1, w2, norm_gains, shift_biases, hidden_bias
    )
    input_grad, gqkv, gproj, dbias, head_sum, sums1 = attention_backward(
        dy, xs, qkv, probs, mixed, wqkv, wproj, norm_gains, shift_biases
    )
    by_head = (
        dbias.reshape(OCTS, SLOT, OCT, SLOT)[:, :SPOTS, :, :SPOTS]
        .transpose(0, 2, 3, 1)
        .reshape(HEADS, SPOTS * SPOTS)
    )
    onehot = (
        position_index.reshape(-1)[:, None]
        == jnp.arange(position_table.shape[0], dtype=jnp.int32)[None, :]
    ).astype(F32)
    table_part = jnp.dot(onehot.T, by_head.T, precision=lax.Precision.HIGHEST)
    smalls = lax.psum(
        (
            jnp.stack([sums1[0], sums2[0]]),
            jnp.stack([sums1[1], sums2[1], sums2[2], sums2[3]]),
            head_sum,
            hidden_sum.reshape(-1),
            table_part,
        ),
        ALL,
    )
    slab_grads = tuple(
        lax.psum_scatter(g, ALL, scatter_dimension=0, tiled=True).astype(F32) / images
        for g in (gqkv, gproj, g1, g2)
    )
    new_momenta = tuple(MOMENTUM * m + g for m, g in zip(momenta, slab_grads))
    new_weights = tuple(
        newton_schulz(lax.all_gather(n.astype(BF16), ALL, axis=0, tiled=True), n, w, factor)
        for n, w, factor in zip(new_momenta, weights, FACTORS)
    )
    small_grads = tuple(s / images for s in smalls)
    small_params = (norm_gains, shift_biases, head_biases, hidden_bias, position_table)
    small_moms = (
        gain_momentum,
        shift_momentum,
        head_bias_momentum,
        hidden_bias_momentum,
        table_momentum,
    )
    small_moms_new = tuple(MOMENTUM * m + g for m, g in zip(small_moms, small_grads))
    small_new = tuple(p - VECTOR_RATE * m for p, m in zip(small_params, small_moms_new))

    def placed(slabs):
        return tuple(as_block(s, like, wide) for s, like, wide in zip(slabs, blocks, WIDE))

    return (
        (output, input_grad)
        + placed(slab_grads)
        + placed(new_weights)
        + placed(new_momenta)
        + small_grads
        + small_new
        + small_moms_new
    )


def solution(mesh):
    rows = P(("dp", "tensor"), None)
    wide, tall = P(None, "tensor", "dp"), P("tensor", "dp", None)
    matrices = (wide, tall, wide, tall)
    return jax.shard_map(
        shards,
        mesh=mesh,
        in_specs=(rows, rows) + matrices * 2 + (P(),) * 12,
        out_specs=(rows, rows) + matrices * 3 + (P(),) * 15,
        check_vma=False,
    )
```

time: 1620 us -> 986 us (0.61)
  local copies, waits for them, and re-layouts: 453 us -> 0.65 us
  matrix products: 189 us -> 0.91 us
  Pallas kernels: 0 us -> 184 us
  other arithmetic: 174 us -> 13.9 us
  waiting for transfers between devices: 428 us -> 586 us
  starting transfers between devices: 84.5 us -> 0.58 us
  blocking collectives: 234 us -> 182 us
  loops' own time: 24.9 us -> 0 us
    dot_general x85 -> x1, matrix products: 189 us -> 0.91 us  [shards(): table_part = jnp.dot(onehot.T, by_head.T, precision=lax.Precision.HIGHEST)]
    pallas_call x0 -> x7, Pallas kernels: none -> 184 us  [the longest x4 53.7 us: newton_schulz(): pl.pallas_call(functools.partial(newton_schulz_kernel, rate=MATRIX_RATE *...]
    reduce_scatter x6 -> x4, waiting for transfers between devices: 272 us -> 448 us  [shards(): lax.psum_scatter(g, ALL, scatter_dimension=0, tiled=True).astype(F32)]
    unnamed x14 -> x10, waiting for transfers between devices: 104 us -> 1.84 us
    all_gather x4 -> x6, waiting for transfers between devices: 34.2 us -> 136 us  [the longest x3 69 us: shards(): lax.all_gather(n.astype(BF16), ALL, axis=0, tiled=True)]
    unnamed x155 -> x40, local copies, waits for them, and re-layouts: 97.7 us -> 0.12 us
    another operation x35 -> x0, local copies, waits for them, and re-layouts: 96.7 us -> none  [the longest x2 44.3 us: from_windows(): layout = windows.reshape((images_in, across, across, WIN, WIN) + trailing)]
    all_to_all x2 -> x0, starting transfers between devices: 83.8 us -> none  [the longest x1 71.7 us: shards(): lax.all_to_all(shortened(results), 'tensor', split_axis=1, concat_axis=0,...]
  transfers between devices with their start and end apart: 14 -> 10, of which waited for: 9 -> 8; matrix products, arithmetic and copies ran while one was open for 11% -> 1% of each run, Pallas kernels for 0% -> 8%
where the time goes in v1:
time: 986 us; the launch traced here: 982 us
  waiting for transfers between devices  586 us (59%)
  Pallas kernels  184 us (19%)
  blocking collectives  182 us (18%)
  between operations  14.5 us (1%)
  other arithmetic  13.9 us (1%)
    reduce_scatter x4, waiting for transfers between devices, shards(): lax.psum_scatter(g, ALL, scatter_dimension=0, tiled=True).astype(F32)  448 us
    all_gather x1, blocking collectives, shards(): lax.all_gather(n.astype(BF16), ALL, axis=0, tiled=True)  71 us
    all_gather x3, waiting for transfers between devices, shards(): lax.all_gather(n.astype(BF16), ALL, axis=0, tiled=True)  69 us
    all_gather x3, waiting for transfers between devices, shards(): lax.all_gather(w.astype(BF16), ALL, axis=0, tiled=True)  66.7 us
    all_gather x1, blocking collectives, shards(): lax.all_gather(w.astype(BF16), ALL, axis=0, tiled=True)  65.8 us
    pallas_call x4, Pallas kernels, newton_schulz(): pl.pallas_call(functools.partial(newton_schulz_kernel, rate=MATRIX_RATE *...  53.7 us
    pallas_call x1, Pallas kernels, attention_backward(): pl.pallas_call(attention_backward_kernel, grid=(steps,), out_shape=(shape...  50.2 us
    psum x1, blocking collectives, shards(): lax.psum((jnp.stack([sums1[0], sums2[0]]), jnp.stack([sums1[1], sums2[1],...  45.4 us
  transfers between devices with their start and end apart: 10, of which 8 were waited for; matrix products, arithmetic and copies ran while one was open for 1% of the time, Pallas kernels for 8%

profile of v1, /device:TPU:17, one launch (start us, length us, event | category | flops | bytes accessed | tf_op | source)
XLA Modules:
  0.0 982.4 jit_solution(3522198595652803535)
XLA Ops:
  7.2 0.0 all-gather.7.cloned.1.call-start
  7.2 1.5 bitcast_convert_fusion.1
  8.8 0.0 all-gather.11.cloned.1.call-start
  8.8 1.5 bitcast_convert_fusion.2
  10.4 0.0 all-gather.9.cloned.1.call-start
  10.5 1.5 bitcast_convert_fusion
  12.0 0.0 reduce-scatter.5.cloned.1.call-start
  12.1 0.8 bitcast_convert_fusion.3
  12.8 65.8 %all_gather.25.wproj_ref = bf16[512,512]{1,0:T(8,128)(2,1)} all-gather(bf16[16,512]{1,0:T(8,128)(2,1)S(1)} %bitcast_convert_fusion.3), channel_id=1, replica_groups=mesh['dp'=8,'tensor'=4] {'tensor','dp'}, dimensions={0}, use_global_device_ids=true | all-gather | bytes 540672 | tf_op jit(solution)/shard_map/all_gather | solution.py:673
  78.6 39.5 %attention_forward.1 = (f32[1568,512]{1,0:T(8,128)}, f32[2048,512]{1,0:T(8,128)}, bf16[2048,1536]{1,0:T(8,128)(2,1)}, bf16[2048,1024]{1,0:T(8,128)(2,1)}, bf16[2048,512]{1,0:T(8,128)(2,1)}) custom-call(f32[1568,512]{1,0:T(8,128)} %x_ref.1, bf16[1536,512]{1,0:T(8,128)(2,1)} %all-gather.7.cloned.1.call-done.wqkv_ref, bf16[512,512]{1,0:T(8,128)(2,1)} %all_gather.25.wproj_ref, ...), custom_call_target="tpu_custom_call" | custom-call | tf_op jit(solution)/shard_map/attention_forward/pallas_call | solution.py:425
  118.1 7.7 all-gather.11.cloned.1.call-done.w2_ref
  125.8 59.0 %all-gather.9.cloned.1.call-done.w1_ref = bf16[2048,512]{1,0:T(8,128)(2,1)} async-done(((bf16[64,512]{1,0:T(8,128)(2,1)}), bf16[2048,512]{1,0:T(8,128)(2,1)}) %all-gather.9.cloned.1.call-update) | async-done | bytes 2097168 | tf_op jit(solution)/shard_map/all_gather | solution.py:673
  184.8 40.2 %mlp.1 = (f32[1568,512]{1,0:T(8,128)}, f32[1568,512]{1,0:T(8,128)}, bf16[2048,512]{1,0:T(8,128)(2,1)}, bf16[2048,512]{1,0:T(8,128)(2,1)}, f32[1,2048]{1,0:T(1,128)}, /*index=5*/f32[4,512]{1,0:T(4,128)}) custom-call(f32[1568,512]{1,0:T(8,128)} %get-tuple-element.46.y_ref, f32[1568,512]{1,0:T(8,128)} %e_ref.1, ...), custom_call_target="tpu_custom_call" | custom-call | tf_op jit(solution)/shard_map/mlp/pallas_call | solution.py:469
  225.0 50.2 %attention_backward.1 = (f32[1568,512]{1,0:T(8,128)}, bf16[1536,512]{1,0:T(8,128)(2,1)}, bf16[512,512]{1,0:T(8,128)(2,1)}, f32[2,64,512]{2,1,0:T(8,128)}, f32[2,512]{1,0:T(2,128)}, /*index=5*/f32[2,512]{1,0:T(2,128)}) custom-call(f32[1568,512]{1,0:T(8,128)} %get-tuple-element.48.dy_ref, f32[2048,512]{1,0:T(8,128)} %get-tuple-element.49.xs_ref, ...), custom_call_target="tpu_custom_call" | custom-call | tf_op jit(solution)/shard_map/attention_backward/pallas_call | solution.py:512
  275.3 0.0 reduce-scatter.5.cloned.1.call-update
  275.3 0.0 reduce-scatter.11.cloned.1.call-start
  275.4 0.5 reduce-scatter.11.cloned.1.call-update
  275.9 0.0 reduce-scatter.9.cloned.1.call-start
  276.0 0.5 reduce-scatter.9.cloned.1.call-update
  276.5 0.0 reduce-scatter.7.cloned.1.call-start
  276.6 0.7 reduce-scatter.7.cloned.1.call-update
  277.4 0.0 all-gather.13.cloned.1.call-start
  277.5 93.2 %reduce-scatter.5.cloned.1.call-done = bf16[48,512]{1,0:T(8,128)(2,1)} async-done(((bf16[1536,512]{1,0:T(8,128)(2,1)}), bf16[48,512]{1,0:T(8,128)(2,1)}) %reduce-scatter.5.cloned.1.call-update) | async-done | bytes 49168 | tf_op jit(solution)/shard_map/reduce_scatter | solution.py:713
  370.7 1.5 fusion.14
  372.2 0.0 all-gather.17.cloned.1.call-start
  372.3 134.7 %reduce-scatter.11.cloned.1.call-done = bf16[64,512]{1,0:T(8,128)(2,1)} async-done(((bf16[2048,512]{1,0:T(8,128)(2,1)}), bf16[64,512]{1,0:T(8,128)(2,1)}) %reduce-scatter.11.cloned.1.call-update) | async-done | bytes 65552 | tf_op jit(solution)/shard_map/reduce_scatter | solution.py:713
  507.0 1.6 fusion.11
  508.6 0.2 all-gather.15.cloned.1.call-start
  508.9 136.3 %reduce-scatter.9.cloned.1.call-done = bf16[64,512]{1,0:T(8,128)(2,1)} async-done(((bf16[2048,512]{1,0:T(8,128)(2,1)}), bf16[64,512]{1,0:T(8,128)(2,1)}) %reduce-scatter.9.cloned.1.call-update) | async-done | bytes 65552 | tf_op jit(solution)/shard_map/reduce_scatter | solution.py:713
  645.2 1.6 fusion.12
  646.8 0.1 eq.15
  647.0 0.2 copy.52
  647.2 0.2 reshape.150
  647.5 0.9 fusion
  648.4 45.4 %all-reduce = (f32[2,512]{1,0:T(2,128)S(1)}, f32[4,512]{1,0:T(4,128)S(1)}, f32[2,512]{1,0:T(2,128)S(1)}, f32[2048]{0:T(1024)S(1)}, f32[169,16]{0,1:T(8,128)S(1)}) all-reduce(f32[2,512]{1,0:T(2,128)S(1)} %pad_maximum_fusion.1, f32[4,512]{1,0:T(4,128)S(1)} %pad_maximum_fusion, ...), channel_id=1, replica_groups=mesh['dp'=8,'tensor'=4] {'tensor','dp'}, use_global_device_ids=true, to_apply=%region_4.0 | all-reduce | flops 8848 | bytes 70784 | tf_op jit(solution)/shard_map/psum | solution.py:702
  693.8 0.6 fusion.7
  694.5 0.6 fusion.9
  695.1 0.6 fusion.8
  695.7 0.6 fusion.6
  696.3 84.2 %reduce-scatter.7.cloned.1.call-done = bf16[16,512]{1,0:T(8,128)(2,1)} async-done(((bf16[512,512]{1,0:T(8,128)(2,1)}), bf16[16,512]{1,0:T(8,128)(2,1)}) %reduce-scatter.7.cloned.1.call-update) | async-done | bytes 16400 | tf_op jit(solution)/shard_map/reduce_scatter | solution.py:713
  780.5 1.4 fusion.13
  781.9 71.0 %all_gather.29.g_ref = bf16[512,512]{1,0:T(8,128)(2,1)} all-gather(bf16[16,512]{1,0:T(8,128)(2,1)S(1)} %get-tuple-element.87), channel_id=1, replica_groups=mesh['dp'=8,'tensor'=4] {'tensor','dp'}, dimensions={0}, use_global_device_ids=true | all-gather | bytes 540672 | tf_op jit(solution)/shard_map/all_gather | solution.py:718
  852.9 7.6 newton_schulz.5
  860.5 13.7 %newton_schulz.4 = f32[48,512]{1,0:T(8,128)} custom-call(bf16[1536,512]{1,0:T(8,128)(2,1)} %all-gather.13.cloned.1.call-done.g_ref, f32[48,512]{1,0:T(8,128)} %get-tuple-element.90.n_ref, f32[48,512]{1,0:T(8,128)} %bitcast.68), custom_call_target="tpu_custom_call" | custom-call | tf_op jit(solution)/shard_map/newton_schulz/pallas_call | solution.py:613
  874.2 26.5 %all-gather.17.cloned.1.call-done.g_ref = bf16[2048,512]{1,0:T(8,128)(2,1)} async-done(((bf16[64,512]{1,0:T(8,128)(2,1)}), bf16[2048,512]{1,0:T(8,128)(2,1)}) %all-gather.17.cloned.1.call-update) | async-done | bytes 2097168 | tf_op jit(solution)/shard_map/all_gather | solution.py:718
  900.7 16.2 %newton_schulz.7 = f32[64,512]{1,0:T(8,128)} custom-call(bf16[2048,512]{1,0:T(8,128)(2,1)} %all-gather.17.cloned.1.call-done.g_ref, f32[64,512]{1,0:T(8,128)} %get-tuple-element.84.n_ref, f32[64,512]{1,0:T(8,128)} %bitcast.64), custom_call_target="tpu_custom_call" | custom-call | tf_op jit(solution)/shard_map/newton_schulz/pallas_call | solution.py:613
  916.9 42.5 %all-gather.15.cloned.1.call-done.g_ref = bf16[2048,512]{1,0:T(8,128)(2,1)} async-done(((bf16[64,512]{1,0:T(8,128)(2,1)}), bf16[2048,512]{1,0:T(8,128)(2,1)}) %all-gather.15.cloned.1.call-update) | async-done | bytes 2097168 | tf_op jit(solution)/shard_map/all_gather | solution.py:718
  959.4 16.2 %newton_schulz.6 = f32[64,512]{1,0:T(8,128)} custom-call(bf16[2048,512]{1,0:T(8,128)(2,1)} %all-gather.15.cloned.1.call-done.g_ref, f32[64,512]{1,0:T(8,128)} %get-tuple-element.86.n_ref, f32[64,512]{1,0:T(8,128)} %bitcast.65), custom_call_target="tpu_custom_call" | custom-call | tf_op jit(solution)/shard_map/newton_schulz/pallas_call | solution.py:613
  (54 shorter events, 0.3 us)
Async XLA Ops:
  7.2 71.4 %all-gather.7.cloned.1.call-start = ((), (), s32[]{:S(2)}) async-start(), calls=%async_computation.4 | async-start | bytes 1622016 | tf_op jit(solution)/shard_map/all_gather | solution.py:673
  8.8 117.0 %all-gather.11.cloned.1.call-start = ((), (), s32[]{:S(2)}) async-start(), calls=%async_computation.6 | async-start | bytes 2162688 | tf_op jit(solution)/shard_map/all_gather | solution.py:673
  10.4 174.4 %all-gather.9.cloned.1.call-start = ((), (), s32[]{:S(2)}) async-start(), calls=%async_computation.5 | async-start | bytes 2162688 | tf_op jit(solution)/shard_map/all_gather | solution.py:673
  12.0 358.7 %reduce-scatter.5.cloned.1.call-start = ((), (), s32[]{:S(2)}) async-start(), calls=%async_computation.7 | async-start | bytes 1622016 | tf_op jit(solution)/shard_map/reduce_scatter | solution.py:713
  275.3 95.4 %copy-start.5 = (f32[512,1,48]{0,2,1:T(8,128)S(1)}, f32[512,1,48]{0,2,1:T(8,128)}, u32[]{:S(2)}) copy-start(f32[512,1,48]{0,2,1:T(8,128)} %param.28) | copy-start | bytes 294916
  275.3 231.7 %reduce-scatter.11.cloned.1.call-start = ((), (), s32[]{:S(2)}) async-start(), calls=%async_computation.10 | async-start | bytes 2162688 | tf_op jit(solution)/shard_map/reduce_scatter | solution.py:713
  275.4 231.7 %copy-start.2 = (f32[1,64,512]{2,1,0:T(8,128)S(1)}, f32[1,64,512]{2,1,0:T(8,128)}, u32[]{:S(2)}) copy-start(f32[1,64,512]{2,1,0:T(8,128)} %param.31) | copy-start | bytes 393220
  275.4 369.8 %copy-start.3 = (f32[512,1,64]{0,2,1:T(8,128)S(1)}, f32[512,1,64]{0,2,1:T(8,128)}, u32[]{:S(2)}) copy-start(f32[512,1,64]{0,2,1:T(8,128)} %param.30) | copy-start | bytes 393220
  275.9 370.9 %copy-start.4 = (s32[49,49]{1,0:T(8,128)S(1)}, s32[49,49]{1,0:T(8,128)}, u32[]{:S(2)}) copy-start(s32[49,49]{1,0:T(8,128)} %index_ref.1) | copy-start | bytes 28816
  275.9 371.1 %copy-start.12 = (f32[4,512]{1,0:T(4,128)S(1)}, f32[4,512]{1,0:T(4,128)}, u32[]{:S(2)}) copy-start(f32[4,512]{1,0:T(4,128)} %get-tuple-element.59) | copy-start | bytes 24580
  275.9 371.1 %copy-start = (f32[2,64,512]{2,1,0:T(8,128)S(1)}, f32[2,64,512]{2,1,0:T(8,128)}, u32[]{:S(2)}) copy-start(f32[2,64,512]{2,1,0:T(8,128)} %get-tuple-element.62) | copy-start | bytes 786436
  275.9 369.3 %reduce-scatter.9.cloned.1.call-start = ((), (), s32[]{:S(2)}) async-start(), calls=%async_computation.9 | async-start | bytes 2162688 | tf_op jit(solution)/shard_map/reduce_scatter | solution.py:713
  276.5 370.9 %copy-start.19 = (f32[2,512]{1,0:T(2,128)S(1)}, f32[2,512]{1,0:T(2,128)}, u32[]{:S(2)}) copy-start(f32[2,512]{1,0:T(2,128)} %get-tuple-element.58) | copy-start | bytes 12292
  276.5 504.0 %reduce-scatter.7.cloned.1.call-start = ((), (), s32[]{:S(2)}) async-start(), calls=%async_computation.8 | async-start | bytes 540672 | tf_op jit(solution)/shard_map/reduce_scatter | solution.py:713
  277.3 371.1 %copy-start.13 = (f32[1,2048]{1,0:T(1,128)S(1)}, f32[1,2048]{1,0:T(1,128)}, u32[]{:S(2)}) copy-start(f32[1,2048]{1,0:T(1,128)} %get-tuple-element.61) | copy-start | bytes 24580
  277.3 371.1 %copy-start.18 = (f32[2,512]{1,0:T(2,128)S(1)}, f32[2,512]{1,0:T(2,128)}, u32[]{:S(2)}) copy-start(f32[2,512]{1,0:T(2,128)} %get-tuple-element.60) | copy-start | bytes 12292
  277.3 416.5 %copy-start.8 = (f32[2048]{0:T(1024)S(1)}, f32[2048]{0:T(1024)}, u32[]{:S(2)}) copy-start(f32[2048]{0:T(1024)} %param.35) | copy-start | bytes 24580
  277.3 416.5 %copy-start.14 = (f32[2048]{0:T(1024)S(1)}, f32[2048]{0:T(1024)}, u32[]{:S(2)}) copy-start(f32[2048]{0:T(1024)} %param.40) | copy-start | bytes 24580
  277.3 417.1 %copy-start.1 = (f32[4,512]{1,0:T(4,128)S(1)}, f32[4,512]{1,0:T(4,128)}, u32[]{:S(2)}) copy-start(f32[4,512]{1,0:T(4,128)} %shift_ref.5) | copy-start | bytes 24580
  277.3 417.1 %copy-start.15 = (f32[4,512]{1,0:T(4,128)S(1)}, f32[4,512]{1,0:T(4,128)}, u32[]{:S(2)}) copy-start(f32[4,512]{1,0:T(4,128)} %param.38) | copy-start | bytes 24580
  277.3 417.7 %copy-start.7 = (f32[2,512]{1,0:T(2,128)S(1)}, f32[2,512]{1,0:T(2,128)}, u32[]{:S(2)}) copy-start(f32[2,512]{1,0:T(2,128)} %gain_ref.5) | copy-start | bytes 12292
  277.3 417.7 %copy-start.10 = (f32[2,512]{1,0:T(2,128)S(1)}, f32[2,512]{1,0:T(2,128)}, u32[]{:S(2)}) copy-start(f32[2,512]{1,0:T(2,128)} %qkvb_ref.1) | copy-start | bytes 12292
  277.4 417.7 %copy-start.16 = (f32[2,512]{1,0:T(2,128)S(1)}, f32[2,512]{1,0:T(2,128)}, u32[]{:S(2)}) copy-start(f32[2,512]{1,0:T(2,128)} %param.39) | copy-start | bytes 12292
  277.4 417.7 %copy-start.17 = (f32[2,512]{1,0:T(2,128)S(1)}, f32[2,512]{1,0:T(2,128)}, u32[]{:S(2)}) copy-start(f32[2,512]{1,0:T(2,128)} %param.37) | copy-start | bytes 12292
  277.4 418.3 %copy-start.6 = (f32[169,16]{0,1:T(8,128)S(1)}, f32[169,16]{0,1:T(8,128)}, u32[]{:S(2)}) copy-start(f32[169,16]{0,1:T(8,128)} %param.36) | copy-start | bytes 32452
  277.4 418.3 %copy-start.11 = (f32[169,16]{0,1:T(8,128)S(1)}, f32[169,16]{0,1:T(8,128)}, u32[]{:S(2)}) copy-start(f32[169,16]{0,1:T(8,128)} %param.41) | copy-start | bytes 32452
  277.4 503.1 %copy-start.9 = (f32[1,16,512]{2,1,0:T(8,128)S(1)}, f32[1,16,512]{2,1,0:T(8,128)}, u32[]{:S(2)}) copy-start(f32[1,16,512]{2,1,0:T(8,128)} %param.29) | copy-start | bytes 98308
  277.4 583.1 %all-gather.13.cloned.1.call-start = ((), (), s32[]{:S(2)}) async-start(), calls=%async_computation.11 | async-start | bytes 1622016 | tf_op jit(solution)/shard_map/all_gather | solution.py:718
  372.2 528.4 %all-gather.17.cloned.1.call-start = ((), (), s32[]{:S(2)}) async-start(), calls=%async_computation.13 | async-start | bytes 2162688 | tf_op jit(solution)/shard_map/all_gather | solution.py:718
  508.6 450.8 %all-gather.15.cloned.1.call-start = ((), (), s32[]{:S(2)}) async-start(), calls=%async_computation.12 | async-start | bytes 2162688 | tf_op jit(solution)/shard_map/all_gather | solution.py:718
Sparse Core Ops, SparseCore 0:
  11.5 55.3 all-gather.6
  70.5 55.3 all-gather.10
  129.4 55.3 all-gather.8
  275.4 95.2 reduce-scatter.4
  372.8 134.1 reduce-scatter.10
  509.1 136.0 reduce-scatter.8
  647.4 133.0 reduce-scatter.6
  784.0 57.4 all-gather.12
  845.0 55.5 all-gather.16
  904.1 55.2 all-gather.14

commit v2 on v1

--- a/solution.py
+++ b/solution.py
@@ -554,10 +554,356 @@
     )(dy, xs, qkv, probs, mixed, wqkv, wproj, gains, shifts)
 
 
-def newton_schulz_kernel(g_ref, n_ref, w_ref, out_ref, x_scr, a_scr, *, rate):
+MESH = pl.DeviceIdType.MESH
+
+
+def flipped(bit, by):
+    return bit + by - 2 * bit * by
+
+
+class Place:
+    def __init__(self, ndp, nt):
+        self.ndp, self.nt = ndp, nt
+        self.nz, self.nx = ndp // 2, nt // 2
+        self.dp, self.t = lax.axis_index("dp"), lax.axis_index("tensor")
+        self.z, self.y = self.dp // 2, self.dp % 2
+        self.x, self.c = self.t // 2, self.t % 2
+
+    def up(self, k):
+        return lax.rem(self.z + k, self.nz)
+
+    def down(self, k):
+        return lax.rem(self.z + self.nz - k, self.nz)
+
+    def device(self, z=None, y=None, x=None, c=None):
+        z, y = self.z if z is None else z, self.y if y is None else y
+        x, c = self.x if x is None else x, self.c if c is None else c
+        return {"dp": z * 2 + y, "tensor": x * 2 + c}
+
+    def block(self, z, y, x, c):
+        return (x * 2 + c) * self.ndp + z * 2 + y
+
+    def across(self, c, a, b):
+        return flipped(self.y, c * a + (1 - c) * b), flipped(self.x, (1 - c) * a + c * b)
+
+    def bit_partner(self, b):
+        size = 2**b
+        return self.z + size * (1 - 2 * lax.rem(self.z // size, 2))
+
+    def greet(self):
+        others = [self.device(c=1 - self.c), self.device(x=1 - self.x)]
+        others += [self.device(x=1 - self.x, c=1 - self.c), self.device(y=1 - self.y)]
+        others += [self.device(z=self.up(k)) for k in range(1, self.nz)]
+        barrier = pltpu.get_barrier_semaphore()
+        for other in others:
+            pl.semaphore_signal(barrier, inc=1, device_id=other, device_id_type=MESH)
+        pl.semaphore_wait(barrier, len(others))
+
+
+class Sender:
+    def __init__(self, send_sem, recv_sem):
+        self.send_sem, self.recv_sem = send_sem, recv_sem
+        self.used, self.copies = 0, {}
+
+    def start(self, key, src, dst, device):
+        at = self.used
+        self.used += 1
+        copy = pltpu.make_async_remote_copy(
+            src_ref=src,
+            dst_ref=dst,
+            send_sem=self.send_sem.at[at],
+            recv_sem=self.recv_sem.at[at],
+            device_id=device,
+            device_id_type=MESH,
+        )
+        copy.start()
+        self.copies[key] = copy
+
+    def arrived(self, key):
+        self.copies[key].wait_recv()
+
+    def finish(self):
+        for copy in self.copies.values():
+            copy.wait_send()
+
+
+def gather_kernel(ndp, nt, count, *refs):
+    slabs, outs = refs[:count], refs[count : 2 * count]
+    lows = refs[2 * count : 3 * count]
+    send_sem, recv_sem, local_sem = refs[3 * count :]
+    place = Place(ndp, nt)
+    nz, c = place.nz, place.c
+    for slab, low in zip(slabs, lows):
+        low[...] = slab[...].astype(BF16)
+    place.greet()
+    sender = Sender(send_sem, recv_sem)
+    here = place.block(place.z, place.y, place.x, c)
+    own = []
+    for m in range(count):
+        own.append(pltpu.make_async_copy(lows[m], outs[m].at[here], local_sem.at[m]))
+        own[m].start()
+
+    def origin(a, b, k):
+        y, x = place.across(1 - c, a, b)
+        return place.block(place.down(k), y, x, c)
+
+    def send(stage, a, b, k, device):
+        for m in range(count):
+            at = origin(a, b, k)
+            src = lows[m] if (a, b, k) == (0, 0, 0) else outs[m].at[at]
+            sender.start((stage, m, a, b, k), src, outs[m].at[at], device)
+
+    def wait(stage, a, b, k):
+        for m in range(count):
+            sender.arrived((stage, m, a, b, k))
+
+    y, x = place.across(1 - c, 1, 0)
+    first = place.device(y=y, x=x)
+    y, x = place.across(1 - c, 0, 1)
+    second = place.device(y=y, x=x)
+    core = place.device(c=1 - c)
+
+    def spread_column(k):
+        send("p", 0, 0, k, first)
+        send("q", 0, 0, k, second)
+        send("c", 0, 0, k, core)
+
+    def spread_first(k):
+        wait("p", 0, 0, k)
+        send("q", 1, 0, k, second)
+        send("c", 1, 0, k, core)
+
+    for k in range(1, nz):
+        for m in range(count):
+            sender.start(("z", m, k), lows[m], outs[m].at[here], place.device(z=place.up(k)))
+    spread_column(0)
+    for k in range(1, nz):
+        for m in range(count):
+            sender.arrived(("z", m, k))
+        spread_column(k)
+        spread_first(k - 1)
+    spread_first(nz - 1)
+    for a in range(2):
+        for k in range(nz):
+            wait("q", a, 0, k)
+            send("c", a, 1, k, core)
+    for b in range(2):
+        for a in range(2):
+            for k in range(nz):
+                wait("c", a, b, k)
+    for copy in own:
+        copy.wait()
+    sender.finish()
+
+
+def gather_weights(slabs, ndp, nt, collective_id):
+    count, n = len(slabs), ndp * nt
+    messages = count * (n - 1)
+    gathered = pl.pallas_call(
+        functools.partial(gather_kernel, ndp, nt, count),
+        out_shape=tuple(shape_of((n,) + s.shape, BF16) for s in slabs),
+        in_specs=[pl.BlockSpec(memory_space=pltpu.VMEM)] * count,
+        out_specs=tuple(pl.BlockSpec(memory_space=pl.ANY) for _ in slabs),
+        scratch_shapes=[pltpu.VMEM(s.shape, BF16) for s in slabs]
+        + [
+            pltpu.SemaphoreType.DMA((messages,)),
+            pltpu.SemaphoreType.DMA((messages,)),
+            pltpu.SemaphoreType.DMA((count,)),
+        ],
+        compiler_params=pltpu.CompilerParams(
+            collective_id=collective_id, has_side_effects=True, vmem_limit_bytes=VMEM_LIMIT
+        ),
+        name="gather_weights",
+    )(*slabs)
+    return tuple(g.reshape(n * s.shape[0], D) for g, s in zip(gathered, slabs))
+
+
+SMALL_ROWS = 32
+TABLE_ROW = 16
+
+
+def update_kernel(ndp, nt, images, tall, *refs):
+    refs = list(refs)
+
+    def take(n):
+        taken = refs[:n]
+        del refs[:n]
+        return taken
+
+    count = nt
+    grads, momenta = take(count), take(count)
+    sums1, sums2, head, hidden, table = take(5)
+    grad_out = take(count)
+    bundle, small_out = take(2)
+    own, from_core, from_p, from_q, from_z = (take(count) for _ in range(5))
+    (fresh, small, small_in) = take(3)
+    send_sem, recv_sem, local_sem, near_sem = take(4)
+    place = Place(ndp, nt)
+    nz, c = place.nz, place.c
+    small[0] = jnp.zeros_like(small[0])
+    small[0, 0:1, :] = sums1[0:1, :]
+    small[0, 1:2, :] = sums2[0:1, :]
+    small[0, 2:3, :] = sums1[1:2, :]
+    small[0, 3:6, :] = sums2[1:4, :]
+    small[0, 6:8, :] = head[...]
+    spans = hidden.shape[1] // D
+    for i in range(spans):
+        small[0, 8 + i : 9 + i, :] = hidden[0:1, i * D : (i + 1) * D]
+    small[0, TABLE_ROW : TABLE_ROW + table.shape[0], 0 : table.shape[1]] = table[...]
+    fresh[...] = jnp.zeros_like(fresh)
+    place.greet()
+    sender = Sender(send_sem, recv_sem)
+    steps = [place.device(c=1 - c), place.device(x=1 - place.x), place.device(y=1 - place.y)]
+    bit = 0
+    while 2**bit < nz:
+        steps.append(place.device(z=place.bit_partner(bit)))
+        bit += 1
+
+    def small_send(i):
+        sender.start(("s", i), small.at[i], small_in.at[i], steps[i])
+
+    def small_add(i):
+        sender.arrived(("s", i))
+        small[i + 1] = small[i] + small_in[i]
+
+    order = [(a, b, k) for a in (1, 0) for b in (1, 0) for k in list(range(1, nz)) + [0]]
+    locals_ = {}
+    for a, b, k in order:
+        y, x = place.across(1 - c, a, b)
+        at = place.block(place.up(k), y, x, 1 - c)
+        for m in range(count):
+            sender.start(("c", m, a, b, k), grads[m].at[at], from_core[m].at[a, b, k], place.device(c=1 - c))
+    small_send(0)
+    for number, (a, b, k) in enumerate(order):
+        y, x = place.across(c, a, b)
+        at = place.block(place.up(k), y, x, c)
+        for m in range(count):
+            copy = pltpu.make_async_copy(
+                grads[m].at[at], own[m].at[a, b, k], local_sem.at[number * count + m]
+            )
+            copy.start()
+            locals_[m, a, b, k] = copy
+    y, x = place.across(c, 1, 0)
+    first = place.device(y=y, x=x)
+    y, x = place.across(c, 0, 1)
+    second = place.device(y=y, x=x)
+    waiting = []
+
+    def flush():
+        for key, src, dst, device in waiting:
+            sender.start(key, src, dst, device)
+        waiting.clear()
+
+    small_at = 0
+    totals = [None] * count
+    for number, (a, b, k) in enumerate(order):
+        ready = []
+        for m in range(count):
+            locals_[m, a, b, k].wait()
+            sender.arrived(("c", m, a, b, k))
+            value = own[m][a, b, k].astype(F32) + from_core[m][a, b, k].astype(F32)
+            if a == 0:
+                sender.arrived(("p", m, b, k))
+                value = value + from_p[m][b, k].astype(F32)
+                if b == 0:
+                    sender.arrived(("q", m, k))
+                    value = value + from_q[m][k].astype(F32)
+            if (a, b, k) == (0, 0, 0):
+                totals[m] = value
+                continue
+            own[m][a, b, k] = value.astype(BF16)
+            src = own[m].at[a, b, k]
+            if a == 1:
+                ready.append((("p", m, b, k), src, from_p[m].at[b, k], first))
+            elif b == 1:
+                ready.append((("q", m, k), src, from_q[m].at[k], second))
+            else:
+                ready.append((("z", m, k), src, from_z[m].at[k - 1], place.device(z=place.up(k))))
+        flush()
+        waiting.extend(ready)
+        if number % 3 == 2 and small_at < len(steps):
+            small_add(small_at)
+            small_at += 1
+            if small_at < len(steps):
+                small_send(small_at)
+    flush()
+    while small_at < len(steps):
+        small_add(small_at)
+        small_at += 1
+        if small_at < len(steps):
+            small_send(small_at)
+    for m in range(count):
+        value = totals[m]
+        for k in range(1, nz):
+            sender.arrived(("z", m, k))
+            value = value + from_z[m][k - 1].astype(F32)
+        value = value / images
+        grad_out[m][...] = value
+        value = MOMENTUM * momenta[m][...] + value
+        fresh[m, 0 : value.shape[0], :] = value.astype(BF16)
+    small_out[...] = small[len(steps)] / images
+    near = pltpu.make_async_copy(fresh.at[place.t], bundle.at[place.dp, place.t], near_sem)
+    near.start()
+    for d in range(1, nt):
+        to = lax.rem(place.t + d, nt)
+        sender.start(
+            ("t", d), fresh.at[to], bundle.at[place.dp, place.t], {"dp": place.dp, "tensor": to}
+        )
+    near.wait()
+    for d in range(1, nt):
+        sender.arrived(("t", d))
+    for k in range(1, nz):
+        sender.start(("bz", k), bundle.at[place.dp], bundle.at[place.dp], place.device(z=place.up(k)))
+    sideways = place.device(y=1 - place.y)
+    for k in range(nz):
+        if k:
+            sender.arrived(("bz", k))
+        at = place.down(k) * 2 + place.y
+        sender.start(("by", k), bundle.at[at], bundle.at[at], sideways)
+    for k in range(nz):
+        sender.arrived(("by", k))
+    sender.finish()
+
+
+def update(grads, momenta, small_sums, ndp, nt, images, collective_id):
+    n, nz = ndp * nt, ndp // 2
+    slabs = [m.shape[0] for m in momenta]
+    tall = max(slabs)
+    grads = tuple(g.reshape(n, r, D) for g, r in zip(grads, slabs))
+    small_steps = 3 + (nz - 1).bit_length()
+    messages = nt * (4 * nz + 2 * nz + nz + nz - 1) + small_steps + (nt - 1) + (nz - 1) + nz
+    vmem, any_ = pl.BlockSpec(memory_space=pltpu.VMEM), pl.BlockSpec(memory_space=pl.ANY)
+    like = lambda arrays: tuple(shape_of(a.shape, F32) for a in arrays)
+    outs = like(momenta) + (shape_of((ndp, nt, tall, D), BF16), shape_of((SMALL_ROWS, D), F32))
+    scratch = []
+    for lead in ((2, 2, nz), (2, 2, nz), (2, nz), (nz,), (nz - 1,)):
+        scratch += [pltpu.VMEM(lead + (r, D), BF16) for r in slabs]
+    scratch += [
+        pltpu.VMEM((nt, tall, D), BF16),
+        pltpu.VMEM((small_steps + 1, SMALL_ROWS, D), F32),
+        pltpu.VMEM((small_steps, SMALL_ROWS, D), F32),
+        pltpu.SemaphoreType.DMA((messages,)),
+        pltpu.SemaphoreType.DMA((messages,)),
+        pltpu.SemaphoreType.DMA((4 * nz * nt,)),
+        pltpu.SemaphoreType.DMA,
+    ]
+    return pl.pallas_call(
+        functools.partial(update_kernel, ndp, nt, images, tall),
+        out_shape=outs,
+        in_specs=[any_] * nt + [vmem] * (nt + 5),
+        out_specs=(vmem,) * nt + (any_, vmem),
+        scratch_shapes=scratch,
+        compiler_params=pltpu.CompilerParams(
+            collective_id=collective_id, has_side_effects=True, vmem_limit_bytes=VMEM_LIMIT
+        ),
+        name="update",
+    )(*grads, *momenta, *small_sums)
+
+
+def newton_schulz_kernel(g_ref, out_ref, x_scr, a_scr):
     first, second, third = QUINTIC
     chunk = 512
-    rows = g_ref.shape[0]
+    rows, mine = g_ref.shape[0], out_ref.shape[0]
 
     def low(values):
         return values.astype(BF16)
@@ -598,28 +944,100 @@
 
     a = gram(g_ref)
     scale = 1.0 / (jnp.sqrt(jnp.sum(jnp.where(diagonal, a, 0.0))) + MUON_EPSILON)
-    q = two_turns(a * scale * scale)
-    advance(g_ref, q, scale)
-    mine = dot_nn(low(n_ref[...]), low(q)) * scale
+    advance(g_ref, two_turns(a * scale * scale), scale)
     q = two_turns(gram(x_scr))
+    at = pl.ds(pl.multiple_of(lax.axis_index("dp") * mine, mine), mine)
+    here = dot_nn(x_scr[at, :], low(q))
     advance(x_scr, q, 1.0)
-    mine = dot_nn(low(mine), low(q))
     b = bend(gram(x_scr))
-    mine = first * mine + dot_nn(low(mine), low(b))
-    out_ref[...] = w_ref[...] - rate * mine
-
-
-def newton_schulz(gathered, slab, weight, factor):
+    out_ref[...] = first * here + dot_nn(low(here), low(b))
+
+
+def newton_schulz(bundle):
+    ndp, nt, tall, _ = bundle.shape
+    rows = ndp * nt * tall
     return pl.pallas_call(
-        functools.partial(newton_schulz_kernel, rate=MATRIX_RATE * factor),
-        out_shape=shape_of(slab.shape, F32),
-        scratch_shapes=[pltpu.VMEM(gathered.shape, BF16), pltpu.VMEM((D, D), F32)],
+        newton_schulz_kernel,
+        out_shape=shape_of((nt * tall, D), F32),
+        scratch_shapes=[pltpu.VMEM((rows, D), BF16), pltpu.VMEM((D, D), F32)],
         compiler_params=pltpu.CompilerParams(vmem_limit_bytes=VMEM_LIMIT),
         name="newton_schulz",
-    )(gathered, slab, weight)
-
-
-ALL = ("tensor", "dp")
+    )(bundle.reshape(rows, D)).reshape(nt, tall, D)
+
+
+def return_kernel(ndp, nt, x_ref, landed, send_sem, recv_sem):
+    dp, t = lax.axis_index("dp"), lax.axis_index("tensor")
+    barrier = pltpu.get_barrier_semaphore()
+    for d in range(1, nt):
+        other = {"dp": dp, "tensor": lax.rem(t + d, nt)}
+        pl.semaphore_signal(barrier, inc=1, device_id=other, device_id_type=MESH)
+    pl.semaphore_wait(barrier, nt - 1)
+    sender = Sender(send_sem, recv_sem)
+    for d in range(1, nt):
+        to = lax.rem(t + d, nt)
+        sender.start(d, x_ref.at[to], landed.at[t], {"dp": dp, "tensor": to})
+    landed[t] = x_ref[t]
+    for d in range(1, nt):
+        sender.arrived(d)
+    sender.finish()
+
+
+def return_updates(x, ndp, nt, collective_id):
+    return pl.pallas_call(
+        functools.partial(return_kernel, ndp, nt),
+        out_shape=shape_of(x.shape, F32),
+        in_specs=[pl.BlockSpec(memory_space=pltpu.VMEM)],
+        out_specs=pl.BlockSpec(memory_space=pltpu.VMEM),
+        scratch_shapes=[pltpu.SemaphoreType.DMA((nt - 1,)), pltpu.SemaphoreType.DMA((nt - 1,))],
+        compiler_params=pltpu.CompilerParams(collective_id=collective_id, has_side_effects=True),
+        name="return_updates",
+    )(x)
+
+
+def finish_kernel(nt, rates, *refs):
+    refs = list(refs)
+
+    def take(n):
+        taken = refs[:n]
+        del refs[:n]
+        return taken
+
+    landed, total = take(2)
+    grads, momenta, weights = take(nt), take(nt), take(nt)
+    small_par, small_mom = take(5), take(5)
+    grad_out, new_out, mom_out = take(nt), take(nt), take(nt)
+    small_grad_out, small_new_out, small_mom_out = take(5), take(5), take(5)
+    for m in range(nt):
+        grad = grads[m][...]
+        grad_out[m][...] = grad
+        mom_out[m][...] = MOMENTUM * momenta[m][...] + grad
+        new_out[m][...] = weights[m][...] - rates[m] * landed[m, 0 : grad.shape[0], :]
+
+    def small_update(i, at, grad):
+        small_grad_out[i][at] = grad
+        grad = MOMENTUM * small_mom[i][at] + grad
+        small_mom_out[i][at] = grad
+        small_new_out[i][at] = small_par[i][at] - VECTOR_RATE * grad
+
+    for i, (low, high) in enumerate(((0, 2), (2, 6), (6, 8))):
+        small_update(i, (slice(None), slice(None)), total[low:high, :])
+    for i in range(small_par[3].shape[1] // D):
+        small_update(3, (slice(0, 1), slice(i * D, (i + 1) * D)), total[8 + i : 9 + i, :])
+    heads, rows = small_par[4].shape
+    small_update(4, (slice(None), slice(None)), total[TABLE_ROW : TABLE_ROW + heads, 0:rows])
+
+
+def finish(landed, total, grads, momenta, weights, small_params, small_moms, rates):
+    nt = len(grads)
+    like = lambda arrays: tuple(shape_of(a.shape, F32) for a in arrays)
+    return pl.pallas_call(
+        functools.partial(finish_kernel, nt, rates),
+        out_shape=like(grads) * 3 + like(small_params) * 3,
+        compiler_params=pltpu.CompilerParams(vmem_limit_bytes=VMEM_LIMIT),
+        name="finish",
+    )(landed, total, *grads, *momenta, *weights, *small_params, *small_moms)
+
+
 WIDE = (True, False, True, False)
 FACTORS = (
     math.sqrt(3.0),
@@ -669,9 +1087,8 @@
         as_slab(m, wide)
         for m, wide in zip((qkv_momentum, proj_momentum, fc1_momentum, fc2_momentum), WIDE)
     )
-    wqkv, wproj, w1, w2 = (
-        lax.all_gather(w.astype(BF16), ALL, axis=0, tiled=True) for w in weights
-    )
+    ndp, nt = lax.axis_size("dp"), lax.axis_size("tensor")
+    wqkv, wproj, w1, w2 = gather_weights(weights, ndp, nt, 0)
     middle, xs, qkv, probs, mixed = attention_forward(
         tokens,
         wqkv,
@@ -699,36 +1116,32 @@
         == jnp.arange(position_table.shape[0], dtype=jnp.int32)[None, :]
     ).astype(F32)
     table_part = jnp.dot(onehot.T, by_head.T, precision=lax.Precision.HIGHEST)
-    smalls = lax.psum(
-        (
-            jnp.stack([sums1[0], sums2[0]]),
-            jnp.stack([sums1[1], sums2[1], sums2[2], sums2[3]]),
-            head_sum,
-            hidden_sum.reshape(-1),
-            table_part,
-        ),
-        ALL,
-    )
-    slab_grads = tuple(
-        lax.psum_scatter(g, ALL, scatter_dimension=0, tiled=True).astype(F32) / images
-        for g in (gqkv, gproj, g1, g2)
-    )
-    new_momenta = tuple(MOMENTUM * m + g for m, g in zip(momenta, slab_grads))
-    new_weights = tuple(
-        newton_schulz(lax.all_gather(n.astype(BF16), ALL, axis=0, tiled=True), n, w, factor)
-        for n, w, factor in zip(new_momenta, weights, FACTORS)
-    )
-    small_grads = tuple(s / images for s in smalls)
-    small_params = (norm_gains, shift_biases, head_biases, hidden_bias, position_table)
+    small_params = (norm_gains, shift_biases, head_biases, hidden_bias.reshape(1, -1), position_table.T)
     small_moms = (
         gain_momentum,
         shift_momentum,
         head_bias_momentum,
-        hidden_bias_momentum,
-        table_momentum,
+        hidden_bias_momentum.reshape(1, -1),
+        table_momentum.T,
     )
-    small_moms_new = tuple(MOMENTUM * m + g for m, g in zip(small_moms, small_grads))
-    small_new = tuple(p - VECTOR_RATE * m for p, m in zip(small_params, small_moms_new))
+    results = update(
+        (gqkv, gproj, g1, g2),
+        momenta,
+        (sums1, sums2, head_sum, hidden_sum, table_part.T),
+        ndp,
+        nt,
+        images,
+        1,
+    )
+    slab_grads, bundle, total = results[:nt], results[nt], results[nt + 1]
+    landed = return_updates(newton_schulz(bundle), ndp, nt, 2)
+    rates = tuple(MATRIX_RATE * factor for factor in FACTORS)
+    results = finish(landed, total, slab_grads, momenta, weights, small_params, small_moms, rates)
+    slab_grads, new_weights, new_momenta = (results[i * nt : (i + 1) * nt] for i in range(3))
+    smalls = tuple(
+        s.reshape(-1) if i % 5 == 3 else s.T if i % 5 == 4 else s
+        for i, s in enumerate(results[3 * nt :])
+    )
 
     def placed(slabs):
         return tuple(as_block(s, like, wide) for s, like, wide in zip(slabs, blocks, WIDE))
@@ -738,9 +1151,7 @@
         + placed(slab_grads)
         + placed(new_weights)
         + placed(new_momenta)
-        + small_grads
-        + small_new
-        + small_moms_new
+        + smalls
     )
 
 

time: 986 us -> 301 us (0.31)
  waiting for transfers between devices: 586 us -> 0 us
  blocking collectives: 182 us -> 0 us
  Pallas kernels: 184 us -> 296 us
  other arithmetic: 13.9 us -> 0 us
  between operations: 14.5 us -> 0.91 us
    reduce_scatter x4 -> x0, waiting for transfers between devices: 448 us -> none  [shards(): lax.psum_scatter(g, ALL, scatter_dimension=0, tiled=True).astype(F32)]
    all_gather x2 -> x0, blocking collectives: 137 us -> none  [the longest x1 71 us: shards(): lax.all_gather(n.astype(BF16), ALL, axis=0, tiled=True)]
    all_gather x6 -> x0, waiting for transfers between devices: 136 us -> none  [the longest x3 69 us: shards(): lax.all_gather(n.astype(BF16), ALL, axis=0, tiled=True)]
    pallas_call x4 -> x5, Pallas kernels: 53.7 us -> 166 us  [the longest x1 94.3 us: update(): pl.pallas_call(functools.partial(update_kernel, ndp, nt, images, tall), o...]
    psum x1 -> x0, blocking collectives: 45.4 us -> none  [shards(): lax.psum((jnp.stack([sums1[0], sums2[0]]), jnp.stack([sums1[1], sums2[1],...]
    convert_element_type x8 -> x0, other arithmetic: 11.4 us -> none  [the longest x4 6.05 us: shards(): n.astype(BF16)]
  transfers between devices with their start and end apart: 10 -> 0, of which waited for: 8 -> 0; matrix products, arithmetic and copies ran while one was open for 1% -> 0% of each run, Pallas kernels for 8% -> 0%
where the time goes in v2:
time: 301 us; the launch traced here: 300 us
  Pallas kernels  296 us (98%)
    pallas_call x1, Pallas kernels, update(): pl.pallas_call(functools.partial(update_kernel, ndp, nt, images, tall), o...  94.3 us
    pallas_call x1, Pallas kernels, attention_backward(): pl.pallas_call(attention_backward_kernel, grid=(steps,), out_shape=(shape...  50.3 us
    pallas_call x1, Pallas kernels, gather_weights(): pl.pallas_call(functools.partial(gather_kernel, ndp, nt, count), out_shap...  42.4 us
    pallas_call x1, Pallas kernels, mlp(): pl.pallas_call(mlp_kernel, grid=(steps,), out_shape=(shape_of(middle.shap...  40.3 us
    pallas_call x1, Pallas kernels, attention_forward(): pl.pallas_call(attention_forward_kernel, grid=(steps,), out_shape=(shape_...  39.5 us
    pallas_call x1, Pallas kernels, newton_schulz(): pl.pallas_call(newton_schulz_kernel, out_shape=shape_of((nt * tall, D), F...  16.2 us
    pallas_call x1, Pallas kernels, return_updates(): pl.pallas_call(functools.partial(return_kernel, ndp, nt), out_shape=shape...  10.6 us

profile of v2, /device:TPU:17, one launch (start us, length us, event | category | flops | bytes accessed | tf_op | source)
XLA Modules:
  0.0 300.3 jit_solution(7699986595198032139)
XLA Ops:
  0.7 42.4 %gather_weights.1 = (bf16[32,48,512]{2,1,0:T(8,128)(2,1)}, bf16[32,16,512]{2,1,0:T(8,128)(2,1)}, bf16[32,64,512]{2,1,0:T(8,128)(2,1)}, bf16[32,64,512]{2,1,0:T(8,128)(2,1)}) custom-call(f32[48,512]{1,0:T(8,128)} %bitcast.85, f32[16,512]{1,0:T(8,128)} %bitcast.91, f32[64,512]{1,0:T(8,128)} %bitcast.76, f32[64,512]{1,0:T(8,128)} %bitcast.78), custom_call_target="tpu_custom_call" | custom-call | tf_op jit(solution)/shard_map/gather_weights/pallas_call | solution.py:702
  43.1 39.5 %attention_forward.1 = (f32[1568,512]{1,0:T(8,128)}, f32[2048,512]{1,0:T(8,128)}, bf16[2048,1536]{1,0:T(8,128)(2,1)}, bf16[2048,1024]{1,0:T(8,128)(2,1)}, bf16[2048,512]{1,0:T(8,128)(2,1)}) custom-call(f32[1568,512]{1,0:T(8,128)} %x_ref.1, bf16[1536,512]{1,0:T(8,128)(2,1)} %bitcast.64, bf16[512,512]{1,0:T(8,128)(2,1)} %bitcast.68, f32[2,512]{1,0:T(2,128)} %refs_14_.1, ...), custom_call_target="tpu_custom_call" | custom-call | tf_op jit(solution)/shard_map/attention_forward/pallas_call | solution.py:425
  82.6 40.3 %mlp.1 = (f32[1568,512]{1,0:T(8,128)}, f32[1568,512]{1,0:T(8,128)}, bf16[2048,512]{1,0:T(8,128)(2,1)}, bf16[2048,512]{1,0:T(8,128)(2,1)}, f32[1,2048]{1,0:T(1,128)}, /*index=5*/f32[4,512]{1,0:T(4,128)}) custom-call(f32[1568,512]{1,0:T(8,128)} %get-tuple-element.85.y_ref, f32[1568,512]{1,0:T(8,128)} %e_ref.1, bf16[2048,512]{1,0:T(8,128)(2,1)} %bitcast.66, ...), custom_call_target="tpu_custom_call" | custom-call | tf_op jit(solution)/shard_map/mlp/pallas_call | solution.py:469
  122.8 0.0 copy-start
  122.9 50.3 %attention_backward.1 = (f32[1568,512]{1,0:T(8,128)}, bf16[1536,512]{1,0:T(8,128)(2,1)}, bf16[512,512]{1,0:T(8,128)(2,1)}, f32[2,64,512]{2,1,0:T(8,128)}, f32[2,512]{1,0:T(2,128)}, /*index=5*/f32[2,512]{1,0:T(2,128)}) custom-call(f32[1568,512]{1,0:T(8,128)} %get-tuple-element.89.dy_ref, f32[2048,512]{1,0:T(8,128)} %get-tuple-element.90.xs_ref, ...), custom_call_target="tpu_custom_call" | custom-call | tf_op jit(solution)/shard_map/attention_backward/pallas_call | solution.py:512
  173.2 1.1 copy.52
  174.4 0.2 reshape.189
  174.5 0.0 copy-done
  174.5 0.1 eq.15
  174.7 1.5 fusion.refs_12_
  176.2 94.3 %update.1 = (f32[48,512]{1,0:T(8,128)}, f32[16,512]{1,0:T(8,128)}, f32[64,512]{1,0:T(8,128)}, f32[64,512]{1,0:T(8,128)}, bf16[8,4,64,512]{3,2,1,0:T(8,128)(2,1)}, /*index=5*/f32[32,512]{1,0:T(8,128)}) custom-call(bf16[32,48,512]{2,1,0:T(8,128)(2,1)} %bitcast.75, bf16[32,16,512]{2,1,0:T(8,128)(2,1)} %bitcast.84, bf16[32,64,512]{2,1,0:T(8,128)(2,1)} %bitcast.72, ...), custom_call_target="tpu_custom_call" | custom-call | tf_op jit(solution)/shard_map/update/pallas_call | solution.py:890
  270.5 16.2 %newton_schulz.1 = f32[256,512]{1,0:T(8,128)} custom-call(bf16[2048,512]{1,0:T(8,128)(2,1)} %bitcast.70), custom_call_target="tpu_custom_call" | custom-call | tf_op jit(solution)/shard_map/newton_schulz/pallas_call | solution.py:959
  286.7 10.6 %return_updates.1.refs_0_ = f32[4,64,512]{2,1,0:T(8,128)} custom-call(f32[4,64,512]{2,1,0:T(8,128)} %bitcast.71), custom_call_target="tpu_custom_call" | custom-call | tf_op jit(solution)/shard_map/return_updates/pallas_call | solution.py:986
  297.3 2.8 finish.1
  (1 shorter events, 0.0 us)
Async XLA Ops:
  122.8 51.7 %copy-start = (s32[49,49]{1,0:T(8,128)S(1)}, s32[49,49]{1,0:T(8,128)}, u32[]{:S(2)}) copy-start(s32[49,49]{1,0:T(8,128)} %index_ref.1) | copy-start | bytes 28816

commit v3 on v1

--- a/solution.py
+++ b/solution.py
@@ -172,7 +172,715 @@
     return jnp.concatenate(tiles, axis=1)
 
 
+MESH = pl.DeviceIdType.MESH
+
+
+def flipped(bit, by):
+    return bit + by - 2 * bit * by
+
+
+class Place:
+    def __init__(self, ndp, nt):
+        self.ndp, self.nt = ndp, nt
+        self.nz = ndp // 2
+        self.dp, self.t = lax.axis_index("dp"), lax.axis_index("tensor")
+        self.z, self.y = self.dp // 2, self.dp % 2
+        self.x, self.c = self.t // 2, self.t % 2
+
+    def up(self, k):
+        return lax.rem(self.z + k, self.nz)
+
+    def down(self, k):
+        return lax.rem(self.z + self.nz - k, self.nz)
+
+    def device(self, z=None, y=None, x=None, c=None):
+        z, y = self.z if z is None else z, self.y if y is None else y
+        x, c = self.x if x is None else x, self.c if c is None else c
+        return {"dp": z * 2 + y, "tensor": x * 2 + c}
+
+    def block(self, z, y, x, c):
+        return (x * 2 + c) * self.ndp + z * 2 + y
+
+    def across(self, c, a, b):
+        return flipped(self.y, c * a + (1 - c) * b), flipped(self.x, (1 - c) * a + c * b)
+
+    def chip(self, c, a, b):
+        y, x = self.across(c, a, b)
+        return self.device(y=y, x=x)
+
+    def bit_partner(self, b):
+        size = 2**b
+        return self.z + size * (1 - 2 * lax.rem(self.z // size, 2))
+
+    def greet(self):
+        others = [self.device(c=1 - self.c), self.device(x=1 - self.x)]
+        others += [self.device(x=1 - self.x, c=1 - self.c), self.device(y=1 - self.y)]
+        others += [self.device(z=self.up(k)) for k in range(1, self.nz)]
+        barrier = pltpu.get_barrier_semaphore()
+        for other in others:
+            pl.semaphore_signal(barrier, inc=1, device_id=other, device_id_type=MESH)
+        pl.semaphore_wait(barrier, len(others))
+
+
+def remote(src, dst, send_sem, recv_sem, device):
+    return pltpu.make_async_remote_copy(
+        src_ref=src,
+        dst_ref=dst,
+        send_sem=send_sem,
+        recv_sem=recv_sem,
+        device_id=device,
+        device_id_type=MESH,
+    )
+
+
+class Gather:
+    def __init__(self, place, slabs, outs, scratch):
+        count = len(slabs)
+        self.place, self.slabs, self.outs, self.count = place, slabs, outs, count
+        self.lows = scratch[:count]
+        self.send_sem, self.recv_sem, self.local_sem = scratch[count:]
+
+    @staticmethod
+    def scratch(shapes, n):
+        messages = len(shapes) * (n - 1)
+        return [pltpu.VMEM(s, BF16) for s in shapes] + [
+            pltpu.SemaphoreType.DMA((messages,)),
+            pltpu.SemaphoreType.DMA((messages,)),
+            pltpu.SemaphoreType.DMA((len(shapes),)),
+        ]
+
+    def copy(self, stage, m, a, b, k):
+        place, nz = self.place, self.place.nz
+        order = 1 - place.c
+        base = {"z": -1, "p": nz - 1, "q": 2 * nz - 1, "c": 4 * nz - 1}[stage]
+        at = m * (8 * nz - 1) + base + (b * 2 + a) * nz + k
+        y, x = place.across(order, a, b)
+        where = place.block(place.down(k), y, x, place.c)
+        device = {
+            "p": lambda: place.chip(order, 1, 0),
+            "q": lambda: place.chip(order, 0, 1),
+            "c": lambda: place.device(c=1 - place.c),
+            "z": lambda: place.device(z=place.up(k)),
+        }[stage]()
+        if stage == "z":
+            where = place.block(place.z, place.y, place.x, place.c)
+        mine = stage == "z" or (a, b, k) == (0, 0, 0)
+        src = self.lows[m] if mine else self.outs[m].at[where]
+        return remote(src, self.outs[m].at[where], self.send_sem.at[at], self.recv_sem.at[at], device)
+
+    def local(self, m):
+        place = self.place
+        where = place.block(place.z, place.y, place.x, place.c)
+        return pltpu.make_async_copy(self.lows[m], self.outs[m].at[where], self.local_sem.at[m])
+
+    def send(self, stage, a, b, k):
+        for m in range(self.count):
+            self.copy(stage, m, a, b, k).start()
+
+    def wait(self, stage, a, b, k):
+        for m in range(self.count):
+            self.copy(stage, m, a, b, k).wait_recv()
+
+    def column(self, k):
+        if k:
+            self.wait("z", 0, 0, k)
+        self.send("p", 0, 0, k)
+        self.send("q", 0, 0, k)
+        self.send("c", 0, 0, k)
+
+    def first(self, k):
+        self.wait("p", 0, 0, k)
+        self.send("q", 1, 0, k)
+        self.send("c", 1, 0, k)
+
+    def second(self, a, k):
+        self.wait("q", a, 0, k)
+        self.send("c", a, 1, k)
+
+    def round(self):
+        return range(self.place.nz)
+
+    def begin(self):
+        for slab, low in zip(self.slabs, self.lows):
+            low[...] = slab[...].astype(BF16)
+        self.place.greet()
+        for m in range(self.count):
+            self.local(m).start()
+        for k in self.round()[1:]:
+            self.send("z", 0, 0, k)
+        self.column(0)
+
+    def end(self):
+        everything = [("z", 0, 0, k) for k in self.round()[1:]]
+        everything += [("p", 0, 0, k) for k in self.round()]
+        everything += [("q", a, 0, k) for a in range(2) for k in self.round()]
+        last = [("c", a, b, k) for b in range(2) for a in range(2) for k in self.round()]
+        for key in last:
+            self.wait(*key)
+        for m in range(self.count):
+            self.local(m).wait()
+            for stage, a, b, k in everything + last:
+                self.copy(stage, m, a, b, k).wait_send()
+
+    def at_once(self):
+        self.begin()
+        for k in self.round()[1:]:
+            self.column(k)
+            self.first(k - 1)
+        self.first(self.place.nz - 1)
+        for a in range(2):
+            for k in self.round():
+                self.second(a, k)
+        self.end()
+
+
+class Reduce:
+    def __init__(self, place, grads, scratch):
+        count = len(grads)
+        self.place, self.grads, self.count = place, grads, count
+        self.own, self.from_core, self.from_p, self.from_q, self.from_z = (
+            scratch[i * count : (i + 1) * count] for i in range(5)
+        )
+        self.send_sem, self.recv_sem, self.local_sem = scratch[5 * count :]
+
+    @staticmethod
+    def scratch(rows, n):
+        nz, count = n // 8, len(rows)
+        shapes = []
+        for lead in ((2, 2, nz), (2, 2, nz), (2, nz), (nz,), (nz - 1,)):
+            shapes += [pltpu.VMEM(lead + (r, D), BF16) for r in rows]
+        return shapes + [
+            pltpu.SemaphoreType.DMA((count * (8 * nz - 1),)),
+            pltpu.SemaphoreType.DMA((count * (8 * nz - 1),)),
+            pltpu.SemaphoreType.DMA((count * 4 * nz,)),
+        ]
+
+    def ks(self):
+        return list(range(1, self.place.nz)) + [0]
+
+    def copy(self, stage, m, a, b, k):
+        place, nz = self.place, self.place.nz
+        base = {"c": 0, "p": 4 * nz, "q": 6 * nz, "z": 7 * nz - 1}[stage]
+        at = m * (8 * nz - 1) + base + {"c": (a * 2 + b) * nz + k, "p": b * nz + k}.get(stage, k)
+        sems = self.send_sem.at[at], self.recv_sem.at[at]
+        if stage == "c":
+            y, x = place.across(1 - place.c, a, b)
+            where = place.block(place.up(k), y, x, 1 - place.c)
+            return remote(
+                self.grads[m].at[where], self.from_core[m].at[a, b, k], *sems, place.device(c=1 - place.c)
+            )
+        src = self.own[m].at[a, b, k]
+        if stage == "p":
+            return remote(src, self.from_p[m].at[b, k], *sems, place.chip(place.c, 1, 0))
+        if stage == "q":
+            return remote(src, self.from_q[m].at[k], *sems, place.chip(place.c, 0, 1))
+        return remote(src, self.from_z[m].at[k - 1], *sems, place.device(z=place.up(k)))
+
+    def local(self, m, a, b, k):
+        place, nz = self.place, self.place.nz
+        y, x = place.across(place.c, a, b)
+        where = place.block(place.up(k), y, x, place.c)
+        at = m * 4 * nz + (a * 2 + b) * nz + k
+        return pltpu.make_async_copy(
+            self.grads[m].at[where], self.own[m].at[a, b, k], self.local_sem.at[at]
+        )
+
+    def order(self):
+        return [(a, b, k) for a in (1, 0) for b in (1, 0) for k in self.ks()]
+
+    def begin(self):
+        for a, b, k in self.order():
+            for m in range(self.count):
+                self.copy("c", m, a, b, k).start()
+        for a, b, k in self.order():
+            for m in range(self.count):
+                self.local(m, a, b, k).start()
+
+    def value(self, m, a, b, k):
+        self.local(m, a, b, k).wait()
+        self.copy("c", m, a, b, k).wait_recv()
+        value = self.own[m][a, b, k].astype(F32) + self.from_core[m][a, b, k].astype(F32)
+        if a == 0:
+            self.copy("p", m, 1, b, k).wait_recv()
+            value = value + self.from_p[m][b, k].astype(F32)
+            if b == 0:
+                self.copy("q", m, 0, 1, k).wait_recv()
+                value = value + self.from_q[m][k].astype(F32)
+        return value
+
+    def pass_on(self, a, b, between=None):
+        stage = "p" if a else "q" if b else "z"
+        waiting = []
+        for k in self.ks():
+            if stage == "z" and k == 0:
+                continue
+            for m in range(self.count):
+                self.own[m][a, b, k] = self.value(m, a, b, k).astype(BF16)
+            for copy in waiting:
+                copy.start()
+            waiting = [self.copy(stage, m, a, b, k) for m in range(self.count)]
+        if between is not None:
+            between()
+        for copy in waiting:
+            copy.start()
+
+    def totals(self):
+        values = [self.value(m, 0, 0, 0) for m in range(self.count)]
+        for m in range(self.count):
+            for k in self.ks()[:-1]:
+                self.copy("z", m, 0, 0, k).wait_recv()
+                values[m] = values[m] + self.from_z[m][k - 1].astype(F32)
+        return values
+
+    def end(self):
+        for m in range(self.count):
+            for a, b, k in self.order():
+                self.copy("c", m, a, b, k).wait_send()
+                if a:
+                    self.copy("p", m, a, b, k).wait_send()
+                elif b:
+                    self.copy("q", m, a, b, k).wait_send()
+                elif k:
+                    self.copy("z", m, a, b, k).wait_send()
+
+
+class Share:
+    def __init__(self, place, core, fresh, bundle, scratch):
+        self.place, self.core, self.fresh, self.bundle = place, core, fresh, bundle
+        self.send_sem, self.recv_sem, self.near_sem = scratch
+
+    @staticmethod
+    def scratch(n, nt):
+        messages = 2 + (nt - 1) + (n // 8 - 1) + n // 8
+        return [
+            pltpu.SemaphoreType.DMA((messages,)),
+            pltpu.SemaphoreType.DMA((messages,)),
+            pltpu.SemaphoreType.DMA,
+        ]
+
+    def near(self, i):
+        place = self.place
+        return pltpu.make_async_copy(self.fresh.at[i], self.bundle.at[place.dp, place.t], self.near_sem)
+
+    def handed(self, i, label):
+        place = self.place
+        to = self.core + 2 * i
+        return remote(
+            self.fresh.at[i],
+            self.bundle.at[place.dp, place.t],
+            self.send_sem.at[i],
+            self.recv_sem.at[label],
+            {"dp": place.dp, "tensor": to},
+        )
+
+    def each(self, then):
+        for i in range(2):
+            to = self.core + 2 * i
+
+            @pl.when(self.place.t != to)
+            def _(i=i, to=to):
+                then(self.handed(i, lax.rem(self.place.t + self.place.nt - to, self.place.nt) - 1))
+
+    def hand(self):
+        self.each(lambda copy: copy.start())
+        for i in range(2):
+
+            @pl.when(self.place.t == self.core + 2 * i)
+            def _(i=i):
+                self.near(i).start()
+
+    def move(self, stage, k):
+        place, nz = self.place, self.place.nz
+        at = self.place.nt - 1 + (k - 1 if stage == "z" else nz - 1 + k)
+        sems = self.send_sem.at[2 + at], self.recv_sem.at[at]
+        if stage == "z":
+            where, device = place.dp, place.device(z=place.up(k))
+        else:
+            where, device = place.down(k) * 2 + place.y, place.device(y=1 - place.y)
+        return remote(self.bundle.at[where], self.bundle.at[where], *sems, device)
+
+    def mine(self):
+        return pl.when(self.place.c == self.core)
+
+    def along_z(self):
+        @self.mine()
+        def _():
+            self.near(0).wait()
+            for label in range(self.place.nt - 1):
+                self.handed(0, label).wait_recv()
+            for k in range(1, self.place.nz):
+                self.move("z", k).start()
+            self.move("y", 0).start()
+
+    def along_y(self):
+        @self.mine()
+        def _():
+            for k in range(1, self.place.nz):
+                self.move("z", k).wait_recv()
+                self.move("y", k).start()
+
+    def end(self):
+        self.each(lambda copy: copy.wait_send())
+
+        @self.mine()
+        def _():
+            for k in range(self.place.nz):
+                self.move("y", k).wait_recv()
+            for k in range(self.place.nz):
+                self.move("y", k).wait_send()
+                if k:
+                    self.move("z", k).wait_send()
+
+
+def renew(totals, momenta, grad_out, fresh, images):
+    values = []
+    for total, momentum, out in zip(totals, momenta, grad_out):
+        grad = total / images
+        out[...] = grad
+        values.append(MOMENTUM * momentum[...] + grad)
+    for i, value in enumerate(values):
+        fresh[i, 0 : value.shape[0], :] = value.astype(BF16)
+
+
+def gather_kernel(ndp, nt, count, *refs):
+    Gather(Place(ndp, nt), refs[:count], refs[count : 2 * count], refs[2 * count :]).at_once()
+
+
+def gather_weights(slabs, ndp, nt, collective_id):
+    count, n = len(slabs), ndp * nt
+    gathered = pl.pallas_call(
+        functools.partial(gather_kernel, ndp, nt, count),
+        out_shape=tuple(shape_of((n,) + s.shape, BF16) for s in slabs),
+        in_specs=[pl.BlockSpec(memory_space=pltpu.VMEM)] * count,
+        out_specs=tuple(pl.BlockSpec(memory_space=pl.ANY) for _ in slabs),
+        scratch_shapes=Gather.scratch([s.shape for s in slabs], n),
+        compiler_params=pltpu.CompilerParams(
+            collective_id=collective_id, has_side_effects=True, vmem_limit_bytes=VMEM_LIMIT
+        ),
+        name="gather_weights",
+    )(*slabs)
+    return tuple(g.reshape(n * s.shape[0], D) for g, s in zip(gathered, slabs))
+
+
+SMALL_ROWS = 32
+TABLE_ROW = 16
+
+
+class SmallSum:
+    def __init__(self, place, values, arrived, send_sem, recv_sem):
+        self.values, self.arrived = values, arrived
+        self.send_sem, self.recv_sem = send_sem, recv_sem
+        self.steps = [
+            place.device(c=1 - place.c),
+            place.device(x=1 - place.x),
+            place.device(y=1 - place.y),
+        ]
+        bit = 0
+        while 2**bit < place.nz:
+            self.steps.append(place.device(z=place.bit_partner(bit)))
+            bit += 1
+        self.done = 0
+
+    def copy(self, i):
+        return remote(
+            self.values.at[i], self.arrived.at[i], self.send_sem.at[i], self.recv_sem.at[i], self.steps[i]
+        )
+
+    def begin(self):
+        self.copy(0).start()
+
+    def step(self):
+        i = self.done
+        if i < len(self.steps):
+            self.copy(i).wait_recv()
+            self.values[i + 1] = self.values[i] + self.arrived[i]
+            self.done += 1
+
+    def go_on(self):
+        if 0 < self.done < len(self.steps):
+            self.copy(self.done).start()
+
+    def end(self):
+        while self.done < len(self.steps):
+            self.step()
+            self.go_on()
+        for i in range(len(self.steps)):
+            self.copy(i).wait_send()
+        return self.values[len(self.steps)]
+
+
+def update_kernel(ndp, nt, images, *refs):
+    refs = list(refs)
+
+    def take(n):
+        taken = refs[:n]
+        del refs[:n]
+        return taken
+
+    grads, momenta = take(2), take(2)
+    sums1, sums2, head, hidden, table = take(5)
+    grad_out = take(2)
+    bundle, small_out = take(2)
+    fresh, small, small_in, small_send, small_recv = take(5)
+    share_scratch = take(3)
+    place = Place(ndp, nt)
+    small[0] = jnp.zeros_like(small[0])
+    small[0, 0:1, :] = sums1[0:1, :]
+    small[0, 1:2, :] = sums2[0:1, :]
+    small[0, 2:3, :] = sums1[1:2, :]
+    small[0, 3:6, :] = sums2[1:4, :]
+    small[0, 6:8, :] = head[...]
+    for i in range(hidden.shape[1] // D):
+        small[0, 8 + i : 9 + i, :] = hidden[0:1, i * D : (i + 1) * D]
+    small[0, TABLE_ROW : TABLE_ROW + table.shape[0], 0 : table.shape[1]] = table[...]
+    fresh[...] = jnp.zeros_like(fresh)
+    place.greet()
+    reduce = Reduce(place, grads, refs)
+    tiny = SmallSum(place, small, small_in, small_send, small_recv)
+    tiny.begin()
+    reduce.begin()
+    for a, b in ((1, 1), (1, 0), (0, 1), (0, 0)):
+        reduce.pass_on(a, b, tiny.step)
+        tiny.go_on()
+    renew(reduce.totals(), momenta, grad_out, fresh, images)
+    tiny.step()
+    share = Share(place, 0, fresh, bundle, share_scratch)
+    share.hand()
+    small_out[...] = tiny.end() / images
+    share.along_z()
+    share.along_y()
+    share.end()
+    reduce.end()
+
+
+def padded(rows):
+    return -(-max(rows) // 16) * 16
+
+
+def update(grads, momenta, small_sums, ndp, nt, images, collective_id):
+    n = ndp * nt
+    slabs = [m.shape[0] for m in momenta]
+    grads = tuple(g.reshape(n, r, D) for g, r in zip(grads, slabs))
+    small_steps = 3 + (ndp // 2 - 1).bit_length()
+    vmem, any_ = pl.BlockSpec(memory_space=pltpu.VMEM), pl.BlockSpec(memory_space=pl.ANY)
+    return pl.pallas_call(
+        functools.partial(update_kernel, ndp, nt, images),
+        out_shape=tuple(shape_of(m.shape, F32) for m in momenta)
+        + (shape_of((ndp, nt, padded(slabs), D), BF16), shape_of((SMALL_ROWS, D), F32)),
+        in_specs=[any_] * 2 + [vmem] * 7,
+        out_specs=(vmem, vmem, any_, vmem),
+        scratch_shapes=[
+            pltpu.VMEM((2, padded(slabs), D), BF16),
+            pltpu.VMEM((small_steps + 1, SMALL_ROWS, D), F32),
+            pltpu.VMEM((small_steps, SMALL_ROWS, D), F32),
+            pltpu.SemaphoreType.DMA((small_steps,)),
+            pltpu.SemaphoreType.DMA((small_steps,)),
+        ]
+        + Share.scratch(n, nt)
+        + Reduce.scratch(slabs, n),
+        compiler_params=pltpu.CompilerParams(
+            collective_id=collective_id, has_side_effects=True, vmem_limit_bytes=VMEM_LIMIT
+        ),
+        name="update",
+    )(*grads, *momenta, *small_sums)
+
+
+def newton_schulz_kernel(first_ref, second_ref, out_ref, g_scr, x_scr, a_scr, sem):
+    first, second, third = QUINTIC
+    chunk = 512
+    core = lax.axis_index("tensor") % 2
+    dp = lax.axis_index("dp")
+    sources = (first_ref, second_ref)
+    for which, ref in enumerate(sources):
+
+        @pl.when(core == which)
+        def _(ref=ref):
+            copy = pltpu.make_async_copy(ref, g_scr.at[0 : ref.shape[0]], sem)
+            copy.start()
+            copy.wait()
+
+    chunks = jnp.where(core == 0, first_ref.shape[0] // chunk, second_ref.shape[0] // chunk)
+
+    def low(values):
+        return values.astype(BF16)
+
+    def gram(src_ref):
+        a_scr[...] = jnp.zeros_like(a_scr)
+
+        def add(at, carry):
+            part = src_ref[pl.ds(pl.multiple_of(at * chunk, chunk), chunk), :]
+            a_scr[...] += dot_tn(part, part)
+            return carry
+
+        lax.fori_loop(0, chunks, add, 0)
+        return a_scr[...]
+
+    def advance(src_ref, factor, scale):
+        factor = low(factor)
+
+        def step(at, carry):
+            at = pl.ds(pl.multiple_of(at * chunk, chunk), chunk)
+            x_scr[at, :] = low(dot_nn(src_ref[at, :], factor) * scale)
+            return carry
+
+        lax.fori_loop(0, chunks, step, 0)
+
+    def bend(a):
+        return second * a + third * dot_nn(low(a), low(a))
+
+    diagonal = lax.broadcasted_iota(jnp.int32, (D, D), 0) == lax.broadcasted_iota(jnp.int32, (D, D), 1)
+
+    def two_turns(a):
+        b = bend(a)
+        q = b + jnp.where(diagonal, first, 0.0)
+        r = first * a + dot_nn(low(a), low(b))
+        a = first * r + dot_nn(low(r), low(b))
+        b = bend(a)
+        return first * q + dot_nn(low(b), low(q))
+
+    a = gram(g_scr)
+    scale = 1.0 / (jnp.sqrt(jnp.sum(jnp.where(diagonal, a, 0.0))) + MUON_EPSILON)
+    advance(g_scr, two_turns(a * scale * scale), scale)
+    q = two_turns(gram(x_scr))
+    for which, ref in enumerate(sources):
+
+        @pl.when(core == which)
+        def _(ref=ref):
+            mine = ref.shape[0] // lax.axis_size("dp")
+            at = pl.ds(pl.multiple_of(dp * mine, mine), mine)
+            out_ref[0:mine, :] = dot_nn(x_scr[at, :], low(q))
+
+    advance(x_scr, q, 1.0)
+    b = bend(gram(x_scr))
+    here = out_ref[...]
+    out_ref[...] = first * here + dot_nn(low(here), low(b))
+
+
+def newton_schulz(bundles):
+    ndp, nt = bundles[0].shape[:2]
+    rows = [ndp * nt * b.shape[2] for b in bundles]
+    tall = max(rows)
+    any_ = pl.BlockSpec(memory_space=pl.ANY)
+    return pl.pallas_call(
+        newton_schulz_kernel,
+        out_shape=shape_of((tall // ndp, D), F32),
+        in_specs=[any_, any_],
+        out_specs=pl.BlockSpec(memory_space=pltpu.VMEM),
+        scratch_shapes=[
+            pltpu.VMEM((tall, D), BF16),
+            pltpu.VMEM((tall, D), BF16),
+            pltpu.VMEM((D, D), F32),
+            pltpu.SemaphoreType.DMA,
+        ],
+        compiler_params=pltpu.CompilerParams(vmem_limit_bytes=VMEM_LIMIT),
+        name="newton_schulz",
+    )(*(b.reshape(r, D) for b, r in zip(bundles, rows)))
+
+
+def return_kernel(ndp, nt, heights, x_ref, *refs):
+    outs = refs[:2]
+    send_sem, recv_sem = refs[2:]
+    dp, t = lax.axis_index("dp"), lax.axis_index("tensor")
+    barrier = pltpu.get_barrier_semaphore()
+    for d in range(1, nt):
+        other = {"dp": dp, "tensor": lax.rem(t + d, nt)}
+        pl.semaphore_signal(barrier, inc=1, device_id=other, device_id_type=MESH)
+    pl.semaphore_wait(barrier, nt - 1)
+
+    def copy(which, d):
+        to = lax.rem(t + d, nt)
+        height = heights[which]
+        return remote(
+            x_ref.at[pl.ds(pl.multiple_of(to * height, height), height)],
+            outs[which].at[t // 2],
+            send_sem.at[d - 1],
+            recv_sem.at[d - 1],
+            {"dp": dp, "tensor": to},
+        )
+
+    for which in range(2):
+
+        @pl.when(t % 2 == which)
+        def _(which=which):
+            for d in range(1, nt):
+                copy(which, d).start()
+            height = heights[which]
+            outs[which][t // 2] = x_ref[pl.ds(pl.multiple_of(t * height, height), height), :]
+
+    for d in range(1, nt):
+        for which in range(2):
+
+            @pl.when(lax.rem(t + nt - d, nt) % 2 == which)
+            def _(d=d, which=which):
+                copy(which, d).wait_recv()
+
+    for which in range(2):
+
+        @pl.when(t % 2 == which)
+        def _(which=which):
+            for d in range(1, nt):
+                copy(which, d).wait_send()
+
+
+def return_updates(x, heights, ndp, nt, collective_id):
+    return pl.pallas_call(
+        functools.partial(return_kernel, ndp, nt, heights),
+        out_shape=tuple(shape_of((nt // 2, h, D), F32) for h in heights),
+        in_specs=[pl.BlockSpec(memory_space=pltpu.VMEM)],
+        out_specs=(pl.BlockSpec(memory_space=pltpu.VMEM),) * 2,
+        scratch_shapes=[pltpu.SemaphoreType.DMA((nt - 1,)), pltpu.SemaphoreType.DMA((nt - 1,))],
+        compiler_params=pltpu.CompilerParams(collective_id=collective_id, has_side_effects=True),
+        name="return_updates",
+    )(x)
+
+
+def finish_kernel(nt, rates, *refs):
+    refs = list(refs)
+
+    def take(n):
+        taken = refs[:n]
+        del refs[:n]
+        return taken
+
+    landed, (total,) = take(2), take(1)
+    grads, momenta, weights = take(nt), take(nt), take(nt)
+    small_par, small_mom = take(5), take(5)
+    grad_out, new_out, mom_out = take(nt), take(nt), take(nt)
+    small_grad_out, small_new_out, small_mom_out = take(5), take(5), take(5)
+    for m in range(nt):
+        grad = grads[m][...]
+        grad_out[m][...] = grad
+        mom_out[m][...] = MOMENTUM * momenta[m][...] + grad
+        new_out[m][...] = weights[m][...] - rates[m] * landed[m % 2][m // 2, 0 : grad.shape[0], :]
+
+    def small_update(i, at, grad):
+        small_grad_out[i][at] = grad
+        grad = MOMENTUM * small_mom[i][at] + grad
+        small_mom_out[i][at] = grad
+        small_new_out[i][at] = small_par[i][at] - VECTOR_RATE * grad
+
+    for i, (low, high) in enumerate(((0, 2), (2, 6), (6, 8))):
+        small_update(i, (slice(None), slice(None)), total[low:high, :])
+    for i in range(small_par[3].shape[1] // D):
+        small_update(3, (slice(0, 1), slice(i * D, (i + 1) * D)), total[8 + i : 9 + i, :])
+    heads, rows = small_par[4].shape
+    small_update(4, (slice(None), slice(None)), total[TABLE_ROW : TABLE_ROW + heads, 0:rows])
+
+
+def finish(landed, total, grads, momenta, weights, small_params, small_moms, rates):
+    nt = len(grads)
+    like = lambda arrays: tuple(shape_of(a.shape, F32) for a in arrays)
+    return pl.pallas_call(
+        functools.partial(finish_kernel, nt, rates),
+        out_shape=like(grads) * 3 + like(small_params) * 3,
+        compiler_params=pltpu.CompilerParams(vmem_limit_bytes=VMEM_LIMIT),
+        name="finish",
+    )(*landed, total, *grads, *momenta, *weights, *small_params, *small_moms)
+
+
 def attention_forward_kernel(
+    ndp,
+    nt,
     x_ref,
     wqkv_ref,
     wproj_ref,
@@ -182,20 +890,29 @@
     table_ref,
     index_ref,
     region_ref,
+    slab1_ref,
+    slab2_ref,
     y_ref,
     xs_ref,
     qkv_ref,
     p_ref,
     o_ref,
+    all1_ref,
+    all2_ref,
     bias_scr,
     idx_scr,
     tab_scr,
     mask_scr,
     turn_scr,
     y_scr,
+    *gather_scr,
 ):
-    @pl.when(pl.program_id(0) == 0)
+    step, last = pl.program_id(0), pl.num_programs(0) - 1
+    gather = Gather(Place(ndp, nt), (slab1_ref, slab2_ref), (all1_ref, all2_ref), gather_scr)
+
+    @pl.when(step == 0)
     def _():
+        gather.begin()
         build_bias(region_ref, index_ref, table_ref, bias_scr, idx_scr, tab_scr)
         mask_scr[...] = head_mask(range(OCT))
         turn_scr[...] = head_mask(TURNED)
@@ -239,6 +956,26 @@
     lax.fori_loop(0, STEP_IMAGES * WINDOWS, one_window, 0)
     y_scr[...] = xs_ref[...] + dot_nn(o_ref[...], wproj_ref[...]) + shift_ref[2:3, :]
     out_of_slots(y_scr, y_ref)
+
+    @pl.when(step == 0)
+    def _():
+        for k in gather.round()[1:]:
+            gather.column(k)
+
+    @pl.when(step == 1)
+    def _():
+        for k in gather.round():
+            gather.first(k)
+
+    @pl.when(step == 2)
+    def _():
+        for a in range(2):
+            for k in gather.round():
+                gather.second(a, k)
+
+    @pl.when(step == last)
+    def _():
+        gather.end()
 
 
 def mlp_kernel(
@@ -317,6 +1054,9 @@
 
 
 def attention_backward_kernel(
+    ndp,
+    nt,
+    images,
     dy_ref,
     xs_ref,
     qkv_ref,
@@ -326,12 +1066,19 @@
     wproj_ref,
     gain_ref,
     shift_ref,
+    g1_ref,
+    g2_ref,
+    m1_ref,
+    m2_ref,
     gin_ref,
     gqkv_ref,
     gproj_ref,
     dbias_ref,
     hsum_ref,
     sums_ref,
+    slab1_ref,
+    slab2_ref,
+    bundle_ref,
     accq,
     accp,
     dy_scr,
@@ -340,11 +1087,19 @@
     mask_scr,
     turn_scr,
     g_scr,
+    fresh,
+    *comm_scr,
 ):
-    step = pl.program_id(0)
+    step, last = pl.program_id(0), pl.num_programs(0) - 1
+    place = Place(ndp, nt)
+    share = Share(place, 1, fresh, bundle_ref, comm_scr[:3])
+    reduce = Reduce(place, (g1_ref, g2_ref), comm_scr[3:])
 
     @pl.when(step == 0)
     def _():
+        place.greet()
+        reduce.begin()
+        fresh[...] = jnp.zeros_like(fresh)
         mask_scr[...] = head_mask(range(OCT))
         turn_scr[...] = head_mask(TURNED)
         accq[...] = jnp.zeros_like(accq)
@@ -353,6 +1108,14 @@
         hsum_ref[...] = jnp.zeros_like(hsum_ref)
         sums_ref[...] = jnp.zeros_like(sums_ref)
         dy_scr[...] = jnp.zeros_like(dy_scr)
+
+    @pl.when(step == 2)
+    def _():
+        reduce.pass_on(0, 0)
+
+    @pl.when(step == last)
+    def _():
+        share.along_z()
 
     into_slots(dy_ref, dy_scr)
     dr = dy_scr[...].astype(BF16)
@@ -388,6 +1151,25 @@
         return carry
 
     lax.fori_loop(0, STEP_IMAGES * WINDOWS, one_window, 0)
+
+    @pl.when(step == 0)
+    def _():
+        reduce.pass_on(1, 1)
+        reduce.pass_on(1, 0)
+
+    @pl.when(step == 1)
+    def _():
+        reduce.pass_on(0, 1)
+
+    @pl.when(step == 2)
+    def _():
+        renew(reduce.totals(), (m1_ref, m2_ref), (slab1_ref, slab2_ref), fresh, images)
+        share.hand()
+
+    @pl.when(step == last)
+    def _():
+        share.along_y()
+
     white, inverse = whiten(xs_ref[...])
     a1 = (white * gain_ref[0:1, :] + shift_ref[0:1, :]).astype(BF16)
     accq[...] += dot_tn(du_scr[...], a1)
@@ -402,6 +1184,8 @@
     def _():
         gqkv_ref[...] = accq[...].astype(BF16)
         gproj_ref[...] = accp[...].astype(BF16)
+        share.end()
+        reduce.end()
 
 
 def whole(shape):
@@ -419,11 +1203,23 @@
 PARAMS = pltpu.CompilerParams(dimension_semantics=("arbitrary",), vmem_limit_bytes=VMEM_LIMIT)
 
 
-def attention_forward(tokens, wqkv, wproj, gains, shifts, head_biases, table, index, regions):
+def remote_params(collective_id):
+    return pltpu.CompilerParams(
+        dimension_semantics=("arbitrary",),
+        vmem_limit_bytes=VMEM_LIMIT,
+        collective_id=collective_id,
+        has_side_effects=True,
+    )
+
+
+def attention_forward(
+    tokens, wqkv, wproj, gains, shifts, head_biases, table, index, regions, slabs, ndp, nt, collective_id
+):
+    n = ndp * nt
     steps = tokens.shape[0] // STEP_ROWS
     slots = steps * STEP_SLOTS
     return pl.pallas_call(
-        attention_forward_kernel,
+        functools.partial(attention_forward_kernel, ndp, nt),
         grid=(steps,),
         out_shape=(
             shape_of(tokens.shape, F32),
@@ -431,7 +1227,8 @@
             shape_of((slots, 3 * D), BF16),
             shape_of((slots, OCTS * OCT_S), BF16),
             shape_of((slots, D), BF16),
-        ),
+        )
+        + tuple(shape_of((n,) + s.shape, BF16) for s in slabs),
         in_specs=[
             rows_of(STEP_ROWS, D),
             whole(wqkv.shape),
@@ -442,6 +1239,8 @@
             whole(table.shape),
             whole(index.shape),
             pl.BlockSpec(memory_space=pltpu.SMEM),
+            whole(slabs[0].shape),
+            whole(slabs[1].shape),
         ],
         out_specs=(
             rows_of(STEP_ROWS, D),
@@ -449,6 +1248,8 @@
             rows_of(STEP_SLOTS, 3 * D),
             rows_of(STEP_SLOTS, OCTS * OCT_S),
             rows_of(STEP_SLOTS, D),
+            pl.BlockSpec(memory_space=pl.ANY),
+            pl.BlockSpec(memory_space=pl.ANY),
         ),
         scratch_shapes=[
             pltpu.VMEM((WINDOWS, OCTS, SLOT, OCT_S), F32),
@@ -457,10 +1258,11 @@
             pltpu.VMEM((OCT_S, OCT_W), BF16),
             pltpu.VMEM((OCT_S, OCT_W), BF16),
             pltpu.VMEM((STEP_SLOTS, D), F32),
-        ],
-        compiler_params=PARAMS,
+        ]
+        + Gather.scratch([s.shape for s in slabs], n),
+        compiler_params=remote_params(collective_id),
         name="attention_forward",
-    )(tokens, wqkv, wproj, gains, shifts, head_biases, table, index, regions)
+    )(tokens, wqkv, wproj, gains, shifts, head_biases, table, index, regions, *slabs)
 
 
 def mlp(middle, out_grad, w1, w2, gains, shifts, hidden_bias):
@@ -507,10 +1309,16 @@
     )(middle, out_grad, w1, w2, gains, shifts, hidden_bias.reshape(1, hidden))
 
 
-def attention_backward(dy, xs, qkv, probs, mixed, wqkv, wproj, gains, shifts):
+def attention_backward(
+    dy, xs, qkv, probs, mixed, wqkv, wproj, gains, shifts, grads, momenta, ndp, nt, images, collective_id
+):
+    n = ndp * nt
+    slabs = [m.shape[0] for m in momenta]
+    grads = tuple(g.reshape(n, r, D) for g, r in zip(grads, slabs))
+    any_ = pl.BlockSpec(memory_space=pl.ANY)
     steps = dy.shape[0] // STEP_ROWS
     return pl.pallas_call(
-        attention_backward_kernel,
+        functools.partial(attention_backward_kernel, ndp, nt, images),
         grid=(steps,),
         out_shape=(
             shape_of(dy.shape, F32),
@@ -519,7 +1327,9 @@
             shape_of((OCTS, SLOT, OCT_S), F32),
             shape_of((2, D), F32),
             shape_of((2, D), F32),
-        ),
+        )
+        + tuple(shape_of(m.shape, F32) for m in momenta)
+        + (shape_of((ndp, nt, padded(slabs), D), BF16),),
         in_specs=[
             rows_of(STEP_ROWS, D),
             rows_of(STEP_SLOTS, D),
@@ -530,6 +1340,10 @@
             whole(wproj.shape),
             whole(gains.shape),
             whole(shifts.shape),
+            any_,
+            any_,
+            whole(momenta[0].shape),
+            whole(momenta[1].shape),
         ],
         out_specs=(
             rows_of(STEP_ROWS, D),
@@ -538,6 +1352,9 @@
             whole((OCTS, SLOT, OCT_S)),
             whole((2, D)),
             whole((2, D)),
+            whole(momenta[0].shape),
+            whole(momenta[1].shape),
+            any_,
         ),
         scratch_shapes=[
             pltpu.VMEM(wqkv.shape, F32),
@@ -548,83 +1365,21 @@
             pltpu.VMEM((OCT_S, OCT_W), BF16),
             pltpu.VMEM((OCT_S, OCT_W), BF16),
             pltpu.VMEM((STEP_SLOTS, D), F32),
-        ],
-        compiler_params=PARAMS,
+            pltpu.VMEM((2, padded(slabs), D), BF16),
+        ]
+        + Share.scratch(n, nt)
+        + Reduce.scratch(slabs, n),
+        compiler_params=remote_params(collective_id),
         name="attention_backward",
-    )(dy, xs, qkv, probs, mixed, wqkv, wproj, gains, shifts)
-
-
-def newton_schulz_kernel(g_ref, n_ref, w_ref, out_ref, x_scr, a_scr, *, rate):
-    first, second, third = QUINTIC
-    chunk = 512
-    rows = g_ref.shape[0]
-
-    def low(values):
-        return values.astype(BF16)
-
-    def gram(src_ref):
-        a_scr[...] = jnp.zeros_like(a_scr)
-
-        def add(at, carry):
-            part = src_ref[pl.ds(pl.multiple_of(at * chunk, chunk), chunk), :]
-            a_scr[...] += dot_tn(part, part)
-            return carry
-
-        lax.fori_loop(0, rows // chunk, add, 0)
-        return a_scr[...]
-
-    def advance(src_ref, factor, scale):
-        factor = low(factor)
-
-        def step(at, carry):
-            at = pl.ds(pl.multiple_of(at * chunk, chunk), chunk)
-            x_scr[at, :] = low(dot_nn(src_ref[at, :], factor) * scale)
-            return carry
-
-        lax.fori_loop(0, rows // chunk, step, 0)
-
-    def bend(a):
-        return second * a + third * dot_nn(low(a), low(a))
-
-    diagonal = lax.broadcasted_iota(jnp.int32, (D, D), 0) == lax.broadcasted_iota(jnp.int32, (D, D), 1)
-
-    def two_turns(a):
-        b = bend(a)
-        q = b + jnp.where(diagonal, first, 0.0)
-        r = first * a + dot_nn(low(a), low(b))
-        a = first * r + dot_nn(low(r), low(b))
-        b = bend(a)
-        return first * q + dot_nn(low(b), low(q))
-
-    a = gram(g_ref)
-    scale = 1.0 / (jnp.sqrt(jnp.sum(jnp.where(diagonal, a, 0.0))) + MUON_EPSILON)
-    q = two_turns(a * scale * scale)
-    advance(g_ref, q, scale)
-    mine = dot_nn(low(n_ref[...]), low(q)) * scale
-    q = two_turns(gram(x_scr))
-    advance(x_scr, q, 1.0)
-    mine = dot_nn(low(mine), low(q))
-    b = bend(gram(x_scr))
-    mine = first * mine + dot_nn(low(mine), low(b))
-    out_ref[...] = w_ref[...] - rate * mine
-
-
-def newton_schulz(gathered, slab, weight, factor):
-    return pl.pallas_call(
-        functools.partial(newton_schulz_kernel, rate=MATRIX_RATE * factor),
-        out_shape=shape_of(slab.shape, F32),
-        scratch_shapes=[pltpu.VMEM(gathered.shape, BF16), pltpu.VMEM((D, D), F32)],
-        compiler_params=pltpu.CompilerParams(vmem_limit_bytes=VMEM_LIMIT),
-        name="newton_schulz",
-    )(gathered, slab, weight)
-
-
-ALL = ("tensor", "dp")
-WIDE = (True, False, True, False)
+    )(dy, xs, qkv, probs, mixed, wqkv, wproj, gains, shifts, *grads, *momenta)
+
+
+ORDER = (0, 2, 1, 3)
+WIDE = (True, True, False, False)
 FACTORS = (
     math.sqrt(3.0),
+    math.sqrt(max(1.0, FF / D)),
     1.0,
-    math.sqrt(max(1.0, FF / D)),
     math.sqrt(max(1.0, D / FF)),
 )
 
@@ -663,16 +1418,15 @@
 ):
     devices = lax.axis_size("dp") * lax.axis_size("tensor")
     images = tokens.shape[0] // AREA * devices
-    blocks = (qkv_weight, proj_weight, fc1_weight, fc2_weight)
+    blocks = (qkv_weight, fc1_weight, proj_weight, fc2_weight)
     weights = tuple(as_slab(w, wide) for w, wide in zip(blocks, WIDE))
     momenta = tuple(
         as_slab(m, wide)
-        for m, wide in zip((qkv_momentum, proj_momentum, fc1_momentum, fc2_momentum), WIDE)
+        for m, wide in zip((qkv_momentum, fc1_momentum, proj_momentum, fc2_momentum), WIDE)
     )
-    wqkv, wproj, w1, w2 = (
-        lax.all_gather(w.astype(BF16), ALL, axis=0, tiled=True) for w in weights
-    )
-    middle, xs, qkv, probs, mixed = attention_forward(
+    ndp, nt = lax.axis_size("dp"), lax.axis_size("tensor")
+    wqkv, wproj = gather_weights(weights[0::2], ndp, nt, 0)
+    middle, xs, qkv, probs, mixed, w1, w2 = attention_forward(
         tokens,
         wqkv,
         wproj,
@@ -682,12 +1436,31 @@
         position_table.T,
         position_index,
         region_ids,
+        weights[1::2],
+        ndp,
+        nt,
+        1,
     )
+    w1, w2 = w1.reshape(-1, D), w2.reshape(-1, D)
     output, dy, g1, g2, hidden_sum, sums2 = mlp(
         middle, out_grad, w1, w2, norm_gains, shift_biases, hidden_bias
     )
-    input_grad, gqkv, gproj, dbias, head_sum, sums1 = attention_backward(
-        dy, xs, qkv, probs, mixed, wqkv, wproj, norm_gains, shift_biases
+    input_grad, gqkv, gproj, dbias, head_sum, sums1, slab1, slab2, bundle1 = attention_backward(
+        dy,
+        xs,
+        qkv,
+        probs,
+        mixed,
+        wqkv,
+        wproj,
+        norm_gains,
+        shift_biases,
+        (g1, g2),
+        momenta[1::2],
+        ndp,
+        nt,
+        images,
+        2,
     )
     by_head = (
         dbias.reshape(OCTS, SLOT, OCT, SLOT)[:, :SPOTS, :, :SPOTS]
@@ -699,48 +1472,46 @@
         == jnp.arange(position_table.shape[0], dtype=jnp.int32)[None, :]
     ).astype(F32)
     table_part = jnp.dot(onehot.T, by_head.T, precision=lax.Precision.HIGHEST)
-    smalls = lax.psum(
-        (
-            jnp.stack([sums1[0], sums2[0]]),
-            jnp.stack([sums1[1], sums2[1], sums2[2], sums2[3]]),
-            head_sum,
-            hidden_sum.reshape(-1),
-            table_part,
-        ),
-        ALL,
-    )
-    slab_grads = tuple(
-        lax.psum_scatter(g, ALL, scatter_dimension=0, tiled=True).astype(F32) / images
-        for g in (gqkv, gproj, g1, g2)
-    )
-    new_momenta = tuple(MOMENTUM * m + g for m, g in zip(momenta, slab_grads))
-    new_weights = tuple(
-        newton_schulz(lax.all_gather(n.astype(BF16), ALL, axis=0, tiled=True), n, w, factor)
-        for n, w, factor in zip(new_momenta, weights, FACTORS)
-    )
-    small_grads = tuple(s / images for s in smalls)
-    small_params = (norm_gains, shift_biases, head_biases, hidden_bias, position_table)
+    small_params = (norm_gains, shift_biases, head_biases, hidden_bias.reshape(1, -1), position_table.T)
     small_moms = (
         gain_momentum,
         shift_momentum,
         head_bias_momentum,
-        hidden_bias_momentum,
-        table_momentum,
+        hidden_bias_momentum.reshape(1, -1),
+        table_momentum.T,
     )
-    small_moms_new = tuple(MOMENTUM * m + g for m, g in zip(small_moms, small_grads))
-    small_new = tuple(p - VECTOR_RATE * m for p, m in zip(small_params, small_moms_new))
+    slab0, slab3, bundle0, total = update(
+        (gqkv, gproj),
+        momenta[0::2],
+        (sums1, sums2, head_sum, hidden_sum, table_part.T),
+        ndp,
+        nt,
+        images,
+        3,
+    )
+    slab_grads = (slab0, slab1, slab3, slab2)
+    bundles = (bundle0, bundle1)
+    landed = return_updates(
+        newton_schulz(bundles), tuple(b.shape[2] for b in bundles), ndp, nt, 4
+    )
+    rates = tuple(MATRIX_RATE * factor for factor in FACTORS)
+    results = finish(landed, total, slab_grads, momenta, weights, small_params, small_moms, rates)
+    slab_grads, new_weights, new_momenta = (results[i * nt : (i + 1) * nt] for i in range(3))
+    smalls = tuple(
+        s.reshape(-1) if i % 5 == 3 else s.T if i % 5 == 4 else s
+        for i, s in enumerate(results[3 * nt :])
+    )
 
     def placed(slabs):
-        return tuple(as_block(s, like, wide) for s, like, wide in zip(slabs, blocks, WIDE))
+        placed = tuple(as_block(s, like, wide) for s, like, wide in zip(slabs, blocks, WIDE))
+        return tuple(placed[i] for i in ORDER)
 
     return (
         (output, input_grad)
         + placed(slab_grads)
         + placed(new_weights)
         + placed(new_momenta)
-        + small_grads
-        + small_new
-        + small_moms_new
+        + smalls
     )
 
 

time: 986 us -> 262 us (0.27)
  waiting for transfers between devices: 586 us -> 0 us
  blocking collectives: 182 us -> 0 us
  Pallas kernels: 184 us -> 253 us
  other arithmetic: 13.9 us -> 0 us
  between operations: 14.5 us -> 0.79 us
    reduce_scatter x4 -> x0, waiting for transfers between devices: 448 us -> none  [shards(): lax.psum_scatter(g, ALL, scatter_dimension=0, tiled=True).astype(F32)]
    all_gather x2 -> x0, blocking collectives: 137 us -> none  [the longest x1 71 us: shards(): lax.all_gather(n.astype(BF16), ALL, axis=0, tiled=True)]
    all_gather x6 -> x0, waiting for transfers between devices: 136 us -> none  [the longest x3 69 us: shards(): lax.all_gather(n.astype(BF16), ALL, axis=0, tiled=True)]
    pallas_call x6 -> x7, Pallas kernels: 143 us -> 213 us  [the longest x1 75.1 us: attention_backward(): pl.pallas_call(functools.partial(attention_backward_kernel, ndp, nt, imag...]
    psum x1 -> x0, blocking collectives: 45.4 us -> none  [shards(): lax.psum((jnp.stack([sums1[0], sums2[0]]), jnp.stack([sums1[1], sums2[1],...]
    convert_element_type x8 -> x0, other arithmetic: 11.4 us -> none  [the longest x4 6.05 us: shards(): n.astype(BF16)]
  transfers between devices with their start and end apart: 10 -> 0, of which waited for: 8 -> 0; matrix products, arithmetic and copies ran while one was open for 1% -> 0% of each run, Pallas kernels for 8% -> 0%
where the time goes in v3:
time: 262 us; the launch traced here: 259 us
  Pallas kernels  253 us (97%)
  local copies, waits for them, and re-layouts  3.16 us (1%)
    pallas_call x1, Pallas kernels, attention_backward(): pl.pallas_call(functools.partial(attention_backward_kernel, ndp, nt, imag...  75.1 us
    pallas_call x1, Pallas kernels, attention_forward(): pl.pallas_call(functools.partial(attention_forward_kernel, ndp, nt), grid...  44 us
    pallas_call x1, Pallas kernels, mlp(): pl.pallas_call(mlp_kernel, grid=(steps,), out_shape=(shape_of(middle.shap...  40.3 us
    pallas_call x1, Pallas kernels, return_updates(): pl.pallas_call(functools.partial(return_kernel, ndp, nt, heights), out_sh...  28.9 us
    pallas_call x1, Pallas kernels, gather_weights(): pl.pallas_call(functools.partial(gather_kernel, ndp, nt, count), out_shap...  23 us
    pallas_call x1, Pallas kernels, update(): pl.pallas_call(functools.partial(update_kernel, ndp, nt, images), out_sha...  22.6 us
    pallas_call x1, Pallas kernels, newton_schulz(): pl.pallas_call(newton_schulz_kernel, out_shape=shape_of((tall // ndp, D),...  16.7 us

profile of v3, /device:TPU:17, one launch (start us, length us, event | category | flops | bytes accessed | tf_op | source)
XLA Modules:
  0.0 258.8 jit_solution(15879163069044990178)
XLA Ops:
  0.7 23.0 %gather_weights.1 = (bf16[32,48,512]{2,1,0:T(8,128)(2,1)}, bf16[32,16,512]{2,1,0:T(8,128)(2,1)}) custom-call(f32[48,512]{1,0:T(8,128)} %bitcast.87, f32[16,512]{1,0:T(8,128)} %bitcast.91), custom_call_target="tpu_custom_call" | custom-call | tf_op jit(solution)/shard_map/gather_weights/pallas_call | solution.py:551
  23.7 44.0 %attention_forward.1 = (f32[1568,512]{1,0:T(8,128)}, f32[2048,512]{1,0:T(8,128)}, bf16[2048,1536]{1,0:T(8,128)(2,1)}, bf16[2048,1024]{1,0:T(8,128)(2,1)}, bf16[2...) custom-call(f32[1568,512]{1,0:T(8,128)} %x_ref.1, bf16[1536,512]{1,0:T(8,128)(2,1)} %bitcast.64, ...), custom_call_target="tpu_custom_call" | custom-call | tf_op jit(solution)/shard_map/attention_forward/pallas_call | solution.py:1221
  67.6 40.3 %mlp.1 = (f32[1568,512]{1,0:T(8,128)}, f32[1568,512]{1,0:T(8,128)}, bf16[2048,512]{1,0:T(8,128)(2,1)}, bf16[2048,512]{1,0:T(8,128)(2,1)}, f32[1,2048]{1,0:T(1,128)}, /*index=5*/f32[4,512]{1,0:T(4,128)}) custom-call(f32[1568,512]{1,0:T(8,128)} %get-tuple-element.88.y_ref, f32[1568,512]{1,0:T(8,128)} %e_ref.1, bf16[2048,512]{1,0:T(8,128)(2,1)} %bitcast.66, ...), custom_call_target="tpu_custom_call" | custom-call | tf_op jit(solution)/shard_map/mlp/pallas_call | solution.py:1271
  108.0 0.0 copy-start.1
  108.0 75.1 %attention_backward.1 = (f32[1568,512]{1,0:T(8,128)}, bf16[1536,512]{1,0:T(8,128)(2,1)}, bf16[512,512]{1,0:T(8,128)(2,1)}, f32[2,64,512]{2,1,0:T(8,128)}, f32[2,...) custom-call(f32[1568,512]{1,0:T(8,128)} %get-tuple-element.92.dy_ref, ...), custom_call_target="tpu_custom_call" | custom-call | tf_op jit(solution)/shard_map/attention_backward/pallas_call | solution.py:1320
  183.1 1.1 copy.52
  184.3 0.2 reshape.189
  184.5 0.0 copy-done.1
  184.5 0.1 eq.15
  184.6 1.5 fusion.refs_8_
  186.1 22.6 %update.1 = (f32[48,512]{1,0:T(8,128)}, f32[16,512]{1,0:T(8,128)}, bf16[8,4,48,512]{3,2,1,0:T(8,128)(2,1)}, f32[32,512]{1,0:T(8,128)}) custom-call(bf16[32,48,512]{2,1,0:T(8,128)(2,1)} %bitcast.74, bf16[32,16,512]{2,1,0:T(8,128)(2,1)} %bitcast.76, f32[48,512]{1,0:T(8,128)} %bitcast.85, f32[16,512]{1,0:T(8,128)} %bitcast.89, ...), custom_call_target="tpu_custom_call" | custom-call | tf_op jit(solution)/shard_map/update/pallas_call | solution.py:666
  208.8 0.0 copy-start
  208.8 16.7 %newton_schulz.1.x_ref = f32[256,512]{1,0:T(8,128)} custom-call(bf16[1536,512]{1,0:T(8,128)(2,1)} %bitcast.75, bf16[2048,512]{1,0:T(8,128)(2,1)} %bitcast.68), custom_call_target="tpu_custom_call" | custom-call | tf_op jit(solution)/shard_map/newton_schulz/pallas_call | solution.py:764
  225.5 28.9 %return_updates.1 = (f32[2,48,512]{2,1,0:T(8,128)}, f32[2,64,512]{2,1,0:T(8,128)}) custom-call(f32[256,512]{1,0:T(8,128)} %newton_schulz.1.x_ref), custom_call_target="tpu_custom_call" | custom-call | tf_op jit(solution)/shard_map/return_updates/pallas_call | solution.py:826
  254.4 2.7 %finish.1 = (f32[48,512]{1,0:T(8,128)}, f32[64,512]{1,0:T(8,128)}, f32[16,512]{1,0:T(8,128)}, f32[64,512]{1,0:T(8,128)}, f32[48,512]{1,0:T(8,128)}, /*index=5*/f...) custom-call(f32[2,48,512]{2,1,0:T(8,128)} %get-tuple-element.109.ref, ...), custom_call_target="tpu_custom_call" | custom-call | tf_op jit(solution)/shard_map/finish/pallas_call | solution.py:873
  257.1 0.0 copy-done
  257.2 1.7 copy.54
  (1 shorter events, 0.0 us)
Async XLA Ops:
  108.0 76.5 %copy-start.1 = (s32[49,49]{1,0:T(8,128)S(1)}, s32[49,49]{1,0:T(8,128)}, u32[]{:S(2)}) copy-start(s32[49,49]{1,0:T(8,128)} %index_ref.1) | copy-start | bytes 28816
  208.8 48.4 %copy-start = (f32[1568,512]{1,0:T(8,128)S(1)}, f32[1568,512]{1,0:T(8,128)}, u32[]{:S(2)}) copy-start(f32[1568,512]{1,0:T(8,128)} %get-tuple-element.173) | copy-start | bytes 9633796

commit v4 on v3

--- a/solution.py
+++ b/solution.py
@@ -34,7 +34,8 @@
 OCT = 8
 OCTS = HEADS // OCT
 OCT_W = OCT * HEAD
-OCT_S = OCT * SLOT
+PAIRS = OCT // 2
+ROWS_S = PAIRS * SLOT
 PAD_SCORE = -1e30
 STEP_IMAGES = 2
 STEP_ROWS = STEP_IMAGES * AREA
@@ -103,13 +104,35 @@
             ]
 
 
-def head_mask(order):
-    rows = lax.broadcasted_iota(jnp.int32, (SLOT, OCT_W), 1) // HEAD
-    return jnp.concatenate([(rows == head).astype(F32) for head in order], axis=0).astype(BF16)
+def pair_mask():
+    pair = lax.broadcasted_iota(jnp.int32, (SLOT, OCT_W), 1) // (2 * HEAD)
+    return jnp.concatenate([(pair == at).astype(F32) for at in range(PAIRS)], axis=0).astype(BF16)
+
+
+def side_mask():
+    side = lax.broadcasted_iota(jnp.int32, (SLOT, OCT_W), 1) // HEAD % 2
+    return jnp.concatenate([(side == at).astype(F32) for at in range(2)], axis=0).astype(BF16)
 
 
 def spread(values, mask_ref):
-    return jnp.concatenate([values] * OCT, axis=0) * mask_ref[...]
+    return jnp.concatenate([values] * (mask_ref.shape[0] // SLOT), axis=0) * mask_ref[...]
+
+
+def turned(values):
+    return jnp.concatenate([values[at : at + LANES].T for at in range(0, ROWS_S, LANES)], axis=1)
+
+
+def by_side(values, first_side):
+    return jnp.where(first_side, values[0:SLOT], values[SLOT:])
+
+
+def by_pair(weights, side_values):
+    tiles = []
+    first = lane_iota(SLOT) < SLOT
+    for at in range(0, OCT_W, LANES):
+        tile = dot_nn(weights[at : at + LANES], side_values[:, at : at + LANES])
+        tiles.append(jnp.where(first, tile[0:SLOT], tile[SLOT:]))
+    return jnp.concatenate(tiles, axis=1)
 
 
 def lane_iota(rows):
@@ -117,15 +140,12 @@
 
 
 def build_bias(region_ref, index_ref, table_ref, bias_ref, idx_scr, tab_scr):
-    idx_scr[...] = jnp.zeros_like(idx_scr)
-    idx_scr[0:SPOTS, 0:SPOTS] = index_ref[...].astype(F32)
     heads, rows = table_ref.shape
     tab_scr[...] = jnp.zeros_like(tab_scr)
     tab_scr[:, 0:rows] = table_ref[...]
     by_head = tab_scr[...]
-    index = idx_scr[...].T[0:SLOT, :]
     lanes = lane_iota(SLOT)
-    index = jnp.where(lanes < SLOT, index, pltpu.roll(index, SLOT, 1)).astype(jnp.int32)
+    index = key_by_query(index_ref, idx_scr).astype(jnp.int32)
     sublanes = lax.broadcasted_iota(jnp.int32, (SLOT, LANES), 0)
     spot = lanes % SLOT
     masks = []
@@ -154,22 +174,11 @@
         )
 
     for octet in range(OCTS):
-        for pair in range(OCT // 2):
+        for pair in range(PAIRS):
             head = octet * OCT + 2 * pair
             tile = jnp.where(lanes < SLOT, gathered(head), gathered(head + 1))
             for window in range(WINDOWS):
-                bias_ref[window, octet, :, pair * LANES : (pair + 1) * LANES] = tile + masks[window]
-
-
-TURNED = (0, 2, 1, 3, 4, 6, 5, 7)
-
-
-def turned(values):
-    tiles = []
-    for at in range(0, OCT_S, 2 * LANES):
-        both = jnp.concatenate([values[:, at : at + LANES], values[:, at + LANES : at + 2 * LANES]], axis=0).T
-        tiles += [both[0:SLOT, :], both[SLOT:, :]]
-    return jnp.concatenate(tiles, axis=1)
+                bias_ref[window, octet, pair * SLOT : (pair + 1) * SLOT, :] = tile + masks[window]
 
 
 MESH = pl.DeviceIdType.MESH
@@ -303,7 +312,6 @@
     def begin(self):
         for slab, low in zip(self.slabs, self.lows):
             low[...] = slab[...].astype(BF16)
-        self.place.greet()
         for m in range(self.count):
             self.local(m).start()
         for k in self.round()[1:]:
@@ -323,6 +331,7 @@
                 self.copy(stage, m, a, b, k).wait_send()
 
     def at_once(self):
+        self.place.greet()
         self.begin()
         for k in self.round()[1:]:
             self.column(k)
@@ -538,8 +547,8 @@
         grad = total / images
         out[...] = grad
         values.append(MOMENTUM * momentum[...] + grad)
-    for i, value in enumerate(values):
-        fresh[i, 0 : value.shape[0], :] = value.astype(BF16)
+    for value, ref in zip(values, fresh):
+        ref[0 : value.shape[0], :] = value.astype(BF16)
 
 
 def gather_kernel(ndp, nt, count, *refs):
@@ -609,21 +618,11 @@
         return self.values[len(self.steps)]
 
 
-def update_kernel(ndp, nt, images, *refs):
-    refs = list(refs)
-
-    def take(n):
-        taken = refs[:n]
-        del refs[:n]
-        return taken
-
-    grads, momenta = take(2), take(2)
-    sums1, sums2, head, hidden, table = take(5)
-    grad_out = take(2)
-    bundle, small_out = take(2)
-    fresh, small, small_in, small_send, small_recv = take(5)
-    share_scratch = take(3)
-    place = Place(ndp, nt)
+def padded(rows):
+    return -(-max(rows) // 16) * 16
+
+
+def pack_small(small, sums1, sums2, head, hidden, table):
     small[0] = jnp.zeros_like(small[0])
     small[0, 0:1, :] = sums1[0:1, :]
     small[0, 1:2, :] = sums2[0:1, :]
@@ -633,64 +632,19 @@
     for i in range(hidden.shape[1] // D):
         small[0, 8 + i : 9 + i, :] = hidden[0:1, i * D : (i + 1) * D]
     small[0, TABLE_ROW : TABLE_ROW + table.shape[0], 0 : table.shape[1]] = table[...]
-    fresh[...] = jnp.zeros_like(fresh)
-    place.greet()
-    reduce = Reduce(place, grads, refs)
-    tiny = SmallSum(place, small, small_in, small_send, small_recv)
-    tiny.begin()
-    reduce.begin()
-    for a, b in ((1, 1), (1, 0), (0, 1), (0, 0)):
-        reduce.pass_on(a, b, tiny.step)
-        tiny.go_on()
-    renew(reduce.totals(), momenta, grad_out, fresh, images)
-    tiny.step()
-    share = Share(place, 0, fresh, bundle, share_scratch)
-    share.hand()
-    small_out[...] = tiny.end() / images
-    share.along_z()
-    share.along_y()
-    share.end()
-    reduce.end()
-
-
-def padded(rows):
-    return -(-max(rows) // 16) * 16
-
-
-def update(grads, momenta, small_sums, ndp, nt, images, collective_id):
-    n = ndp * nt
-    slabs = [m.shape[0] for m in momenta]
-    grads = tuple(g.reshape(n, r, D) for g, r in zip(grads, slabs))
-    small_steps = 3 + (ndp // 2 - 1).bit_length()
-    vmem, any_ = pl.BlockSpec(memory_space=pltpu.VMEM), pl.BlockSpec(memory_space=pl.ANY)
-    return pl.pallas_call(
-        functools.partial(update_kernel, ndp, nt, images),
-        out_shape=tuple(shape_of(m.shape, F32) for m in momenta)
-        + (shape_of((ndp, nt, padded(slabs), D), BF16), shape_of((SMALL_ROWS, D), F32)),
-        in_specs=[any_] * 2 + [vmem] * 7,
-        out_specs=(vmem, vmem, any_, vmem),
-        scratch_shapes=[
-            pltpu.VMEM((2, padded(slabs), D), BF16),
-            pltpu.VMEM((small_steps + 1, SMALL_ROWS, D), F32),
-            pltpu.VMEM((small_steps, SMALL_ROWS, D), F32),
-            pltpu.SemaphoreType.DMA((small_steps,)),
-            pltpu.SemaphoreType.DMA((small_steps,)),
-        ]
-        + Share.scratch(n, nt)
-        + Reduce.scratch(slabs, n),
-        compiler_params=pltpu.CompilerParams(
-            collective_id=collective_id, has_side_effects=True, vmem_limit_bytes=VMEM_LIMIT
-        ),
-        name="update",
-    )(*grads, *momenta, *small_sums)
-
-
-def newton_schulz_kernel(first_ref, second_ref, out_ref, g_scr, x_scr, a_scr, sem):
+
+
+def newton_schulz_kernel(nt, heights, first_ref, second_ref, landed0, landed1, g_scr, x_scr, a_scr, y_scr, back, sem, send_sem, recv_sem):
     first, second, third = QUINTIC
     chunk = 512
-    core = lax.axis_index("tensor") % 2
-    dp = lax.axis_index("dp")
+    t, dp = lax.axis_index("tensor"), lax.axis_index("dp")
+    core = t % 2
     sources = (first_ref, second_ref)
+    landed = (landed0, landed1)
+    barrier = pltpu.get_barrier_semaphore()
+    for d in range(1, nt):
+        other = {"dp": dp, "tensor": lax.rem(t + d, nt)}
+        pl.semaphore_signal(barrier, inc=1, device_id=other, device_id_type=MESH)
     for which, ref in enumerate(sources):
 
         @pl.when(core == which)
@@ -746,92 +700,77 @@
 
         @pl.when(core == which)
         def _(ref=ref):
-            mine = ref.shape[0] // lax.axis_size("dp")
+            mine = nt * heights[which]
             at = pl.ds(pl.multiple_of(dp * mine, mine), mine)
-            out_ref[0:mine, :] = dot_nn(x_scr[at, :], low(q))
+            y_scr[0:mine, :] = dot_nn(x_scr[at, :], low(q))
 
     advance(x_scr, q, 1.0)
     b = bend(gram(x_scr))
-    here = out_ref[...]
-    out_ref[...] = first * here + dot_nn(low(here), low(b))
-
-
-def newton_schulz(bundles):
+    here = y_scr[...]
+    back[...] = low(first * here + dot_nn(low(here), low(b)))
+    pl.semaphore_wait(barrier, nt - 1)
+
+    def copy(which, d):
+        to = lax.rem(t + d, nt)
+        height = heights[which]
+        return remote(
+            back.at[pl.ds(pl.multiple_of(to * height, height), height)],
+            landed[which].at[t // 2],
+            send_sem.at[d - 1],
+            recv_sem.at[d - 1],
+            {"dp": dp, "tensor": to},
+        )
+
+    for which in range(2):
+
+        @pl.when(core == which)
+        def _(which=which):
+            for d in range(1, nt):
+                copy(which, d).start()
+            height = heights[which]
+            landed[which][t // 2] = back[pl.ds(pl.multiple_of(t * height, height), height), :]
+
+    for d in range(1, nt):
+        for which in range(2):
+
+            @pl.when(lax.rem(t + nt - d, nt) % 2 == which)
+            def _(d=d, which=which):
+                copy(which, d).wait_recv()
+
+    for which in range(2):
+
+        @pl.when(core == which)
+        def _(which=which):
+            for d in range(1, nt):
+                copy(which, d).wait_send()
+
+
+def newton_schulz(bundles, collective_id):
     ndp, nt = bundles[0].shape[:2]
-    rows = [ndp * nt * b.shape[2] for b in bundles]
+    heights = tuple(b.shape[2] for b in bundles)
+    rows = [ndp * nt * h for h in heights]
     tall = max(rows)
-    any_ = pl.BlockSpec(memory_space=pl.ANY)
+    any_, vmem = pl.BlockSpec(memory_space=pl.ANY), pl.BlockSpec(memory_space=pltpu.VMEM)
     return pl.pallas_call(
-        newton_schulz_kernel,
-        out_shape=shape_of((tall // ndp, D), F32),
+        functools.partial(newton_schulz_kernel, nt, heights),
+        out_shape=tuple(shape_of((nt // 2, h, D), BF16) for h in heights),
         in_specs=[any_, any_],
-        out_specs=pl.BlockSpec(memory_space=pltpu.VMEM),
+        out_specs=(vmem, vmem),
         scratch_shapes=[
             pltpu.VMEM((tall, D), BF16),
             pltpu.VMEM((tall, D), BF16),
             pltpu.VMEM((D, D), F32),
+            pltpu.VMEM((tall // ndp, D), F32),
+            pltpu.VMEM((tall // ndp, D), BF16),
             pltpu.SemaphoreType.DMA,
+            pltpu.SemaphoreType.DMA((nt - 1,)),
+            pltpu.SemaphoreType.DMA((nt - 1,)),
         ],
-        compiler_params=pltpu.CompilerParams(vmem_limit_bytes=VMEM_LIMIT),
+        compiler_params=pltpu.CompilerParams(
+            collective_id=collective_id, has_side_effects=True, vmem_limit_bytes=VMEM_LIMIT
+        ),
         name="newton_schulz",
     )(*(b.reshape(r, D) for b, r in zip(bundles, rows)))
-
-
-def return_kernel(ndp, nt, heights, x_ref, *refs):
-    outs = refs[:2]
-    send_sem, recv_sem = refs[2:]
-    dp, t = lax.axis_index("dp"), lax.axis_index("tensor")
-    barrier = pltpu.get_barrier_semaphore()
-    for d in range(1, nt):
-        other = {"dp": dp, "tensor": lax.rem(t + d, nt)}
-        pl.semaphore_signal(barrier, inc=1, device_id=other, device_id_type=MESH)
-    pl.semaphore_wait(barrier, nt - 1)
-
-    def copy(which, d):
-        to = lax.rem(t + d, nt)
-        height = heights[which]
-        return remote(
-            x_ref.at[pl.ds(pl.multiple_of(to * height, height), height)],
-            outs[which].at[t // 2],
-            send_sem.at[d - 1],
-            recv_sem.at[d - 1],
-            {"dp": dp, "tensor": to},
-        )
-
-    for which in range(2):
-
-        @pl.when(t % 2 == which)
-        def _(which=which):
-            for d in range(1, nt):
-                copy(which, d).start()
-            height = heights[which]
-            outs[which][t // 2] = x_ref[pl.ds(pl.multiple_of(t * height, height), height), :]
-
-    for d in range(1, nt):
-        for which in range(2):
-
-            @pl.when(lax.rem(t + nt - d, nt) % 2 == which)
-            def _(d=d, which=which):
-                copy(which, d).wait_recv()
-
-    for which in range(2):
-
-        @pl.when(t % 2 == which)
-        def _(which=which):
-            for d in range(1, nt):
-                copy(which, d).wait_send()
-
-
-def return_updates(x, heights, ndp, nt, collective_id):
-    return pl.pallas_call(
-        functools.partial(return_kernel, ndp, nt, heights),
-        out_shape=tuple(shape_of((nt // 2, h, D), F32) for h in heights),
-        in_specs=[pl.BlockSpec(memory_space=pltpu.VMEM)],
-        out_specs=(pl.BlockSpec(memory_space=pltpu.VMEM),) * 2,
-        scratch_shapes=[pltpu.SemaphoreType.DMA((nt - 1,)), pltpu.SemaphoreType.DMA((nt - 1,))],
-        compiler_params=pltpu.CompilerParams(collective_id=collective_id, has_side_effects=True),
-        name="return_updates",
-    )(x)
 
 
 def finish_kernel(nt, rates, *refs):
@@ -851,7 +790,7 @@
         grad = grads[m][...]
         grad_out[m][...] = grad
         mom_out[m][...] = MOMENTUM * momenta[m][...] + grad
-        new_out[m][...] = weights[m][...] - rates[m] * landed[m % 2][m // 2, 0 : grad.shape[0], :]
+        new_out[m][...] = weights[m][...] - rates[m] * landed[m % 2][m // 2, 0 : grad.shape[0], :].astype(F32)
 
     def small_update(i, at, grad):
         small_grad_out[i][at] = grad
@@ -878,65 +817,145 @@
     )(*landed, total, *grads, *momenta, *weights, *small_params, *small_moms)
 
 
-def attention_forward_kernel(
-    ndp,
-    nt,
-    x_ref,
-    wqkv_ref,
-    wproj_ref,
-    gain_ref,
-    shift_ref,
-    qkvb_ref,
-    table_ref,
-    index_ref,
-    region_ref,
-    slab1_ref,
-    slab2_ref,
-    y_ref,
-    xs_ref,
-    qkv_ref,
-    p_ref,
-    o_ref,
-    all1_ref,
-    all2_ref,
-    bias_scr,
-    idx_scr,
-    tab_scr,
-    mask_scr,
-    turn_scr,
-    y_scr,
-    *gather_scr,
-):
+def key_by_query(index_ref, idx_scr):
+    idx_scr[...] = jnp.zeros_like(idx_scr)
+    idx_scr[0:SPOTS, 0:SPOTS] = index_ref[...].astype(F32)
+    index = idx_scr[...].T[0:SLOT, :]
+    return jnp.where(lane_iota(SLOT) < SLOT, index, pltpu.roll(index, SLOT, 1))
+
+
+def table_sums(dbias_ref, index_ref, table_scr, idx_scr, turned_idx):
+    turned_idx[...] = key_by_query(index_ref, idx_scr)
+    table_scr[...] = jnp.zeros_like(table_scr)
+    lanes = lane_iota(PAIRS)
+    entries = lax.broadcasted_iota(jnp.int32, (2 * LANES, LANES), 0).astype(F32)
+    count = OCTS * OCT
+
+    def one_key(key, carry):
+        picks = (entries == turned_idx[pl.ds(key, 1), :]).astype(F32).astype(BF16)
+        values = []
+        for octet in range(OCTS):
+            pairs = dbias_ref[octet, pl.ds(key, PAIRS, SLOT), :]
+            values += [jnp.where(lanes < SLOT, pairs, 0.0), jnp.where(lanes < SLOT, 0.0, pairs)]
+        values = jnp.concatenate(values, axis=0)
+        parts = []
+        for _ in range(3):
+            low = values.astype(BF16).astype(F32)
+            parts.append(low)
+            values = values - low
+        sums = dot_nt(jnp.concatenate(parts, axis=0).astype(BF16), picks)
+        table_scr[...] += sums[0:count] + sums[count : 2 * count] + sums[2 * count :]
+        return carry
+
+    lax.fori_loop(0, SPOTS, one_key, 0)
+    sums = table_scr[...]
+    for octet in range(OCTS):
+        for head in range(OCT):
+            at = octet * OCT + head % 2 * PAIRS + head // 2
+            table_scr[octet * OCT + head : octet * OCT + head + 1, :] = sums[at : at + 1]
+
+
+def attention_forward_kernel(ndp, nt, steps, fused, *refs):
+    refs = list(refs)
+
+    def take(n):
+        taken = refs[:n]
+        del refs[:n]
+        return taken
+
+    x_ref, gain_ref, shift_ref, qkvb_ref, table_ref, index_ref, region_ref = take(7)
+    slabs, (wqkv_in,) = take(3), take(1)
+    xs_ref, a1_ref, qkv_ref, p_ref, o_ref = take(5)
+    gathered = take(3)
+    wqkv_all = take(1) if fused else None
+    bias_scr, idx_scr, tab_scr, pair_scr, side_scr, a1_scr = take(6)
+    place = Place(ndp, nt)
+    rest = Gather(place, slabs, gathered, take(6))
     step, last = pl.program_id(0), pl.num_programs(0) - 1
-    gather = Gather(Place(ndp, nt), (slab1_ref, slab2_ref), (all1_ref, all2_ref), gather_scr)
+    if fused:
+        qkv_gather = Gather(place, (wqkv_in,), wqkv_all, take(4))
+        wqkv_ref, load_sem = take(2)
+    else:
+        wqkv_ref = wqkv_in
 
     @pl.when(step == 0)
     def _():
-        gather.begin()
+        place.greet()
+        if fused:
+            qkv_gather.begin()
+
+    @pl.when(step < steps)
+    def _():
+        xs_ref[...] = jnp.zeros_like(xs_ref)
+        into_slots(x_ref, xs_ref)
+        white, _ = whiten(xs_ref[...])
+        a1 = (white * gain_ref[0:1, :] + shift_ref[0:1, :]).astype(BF16)
+        a1_ref[...] = a1
+        a1_scr[pl.ds(pl.multiple_of(step * STEP_SLOTS, STEP_SLOTS), STEP_SLOTS), :] = a1
+
+    @pl.when(step == 0)
+    def _():
+        if fused:
+            for k in qkv_gather.round()[1:]:
+                qkv_gather.column(k)
         build_bias(region_ref, index_ref, table_ref, bias_scr, idx_scr, tab_scr)
-        mask_scr[...] = head_mask(range(OCT))
-        turn_scr[...] = head_mask(TURNED)
-
-    xs_ref[...] = jnp.zeros_like(xs_ref)
-    into_slots(x_ref, xs_ref)
-    white, _ = whiten(xs_ref[...])
-    a1 = (white * gain_ref[0:1, :] + shift_ref[0:1, :]).astype(BF16)
-    scale = HEAD ** (-0.5)
-    for half in range(2):
-        columns = 3 * PART * GROUPS // 2
-        u = dot_nt(a1, wqkv_ref[half * columns : (half + 1) * columns, :])
-        for inner in range(GROUPS // 2):
-            group = half * (GROUPS // 2) + inner
-            for part in range(3):
-                piece = u[:, (inner * 3 + part) * PART : (inner * 3 + part + 1) * PART]
-                if part == 0:
-                    piece = (piece + qkvb_ref[0:1, group * PART : (group + 1) * PART]) * scale
-                elif part == 2:
-                    piece = piece + qkvb_ref[1:2, group * PART : (group + 1) * PART]
-                at = part * D + group * PART
-                qkv_ref[:, at : at + PART] = piece.astype(BF16)
-
-    real_query = (lax.broadcasted_iota(jnp.int32, (1, OCT_S), 1) % SLOT < SPOTS).astype(F32)
+        pair_scr[...] = pair_mask()
+        side_scr[...] = side_mask()
+
+    if fused:
+
+        @pl.when(step == 1)
+        def _():
+            for k in qkv_gather.round():
+                qkv_gather.first(k)
+
+        @pl.when(step == 2)
+        def _():
+            for a in range(2):
+                for k in qkv_gather.round():
+                    qkv_gather.second(a, k)
+
+    @pl.when(step == 2)
+    def _():
+        rest.begin()
+
+    @pl.when(step == steps - 1)
+    def _():
+        if fused:
+            qkv_gather.end()
+            copies = []
+            for i in range(ndp * nt):
+                rows = wqkv_in.shape[0]
+                copies.append(
+                    pltpu.make_async_copy(
+                        wqkv_all[0].at[i], wqkv_ref.at[i * rows : (i + 1) * rows], load_sem.at[i]
+                    )
+                )
+                copies[i].start()
+            for copy in copies:
+                copy.wait()
+
+    @pl.when(step >= steps)
+    def _():
+        at = pl.multiple_of((step - steps) * STEP_SLOTS, STEP_SLOTS)
+        a1 = a1_scr[pl.ds(at, STEP_SLOTS), :]
+        scale = HEAD ** (-0.5)
+        for half in range(2):
+            columns = 3 * PART * GROUPS // 2
+            u = dot_nt(a1, wqkv_ref[half * columns : (half + 1) * columns, :])
+            for inner in range(GROUPS // 2):
+                group = half * (GROUPS // 2) + inner
+                for part in range(3):
+                    piece = u[:, (inner * 3 + part) * PART : (inner * 3 + part + 1) * PART]
+                    if part == 0:
+                        piece = (piece + qkvb_ref[0:1, group * PART : (group + 1) * PART]) * scale
+                    elif part == 2:
+                        piece = piece + qkvb_ref[1:2, group * PART : (group + 1) * PART]
+                    lanes = part * D + group * PART
+                    qkv_ref[:, lanes : lanes + PART] = piece.astype(BF16)
+
+    real_query = (lane_iota(1) % SLOT < SPOTS).astype(F32)
+    first_side = lax.broadcasted_iota(jnp.int32, (SLOT, OCT_W), 1) // HEAD % 2 == 0
 
     def one_window(at, carry):
         rows = pl.ds(pl.multiple_of(at * SLOT, SLOT), SLOT)
@@ -944,43 +963,54 @@
             q = qkv_ref[rows, octet * OCT_W : (octet + 1) * OCT_W]
             k = qkv_ref[rows, D + octet * OCT_W : D + (octet + 1) * OCT_W]
             v = qkv_ref[rows, 2 * D + octet * OCT_W : 2 * D + (octet + 1) * OCT_W]
-            scores = dot_nt(k, spread(q, mask_scr)) + bias_scr[lax.rem(at, WINDOWS), octet]
-            grown = jnp.exp(scores - jnp.max(scores, axis=0, keepdims=True))
-            probs = grown * (real_query / jnp.sum(grown, axis=0, keepdims=True))
-            p_ref[rows, octet * OCT_S : (octet + 1) * OCT_S] = probs.astype(BF16)
-            o_ref[rows, octet * OCT_W : (octet + 1) * OCT_W] = dot_nn(
-                turned(probs).astype(BF16), spread(v, turn_scr)
-            ).astype(BF16)
+            scores = dot_nt(spread(k, pair_scr), spread(q, side_scr)) + bias_scr[lax.rem(at, WINDOWS), octet]
+            probs = []
+            for pair in range(PAIRS):
+                part = scores[pair * SLOT : (pair + 1) * SLOT]
+                grown = jnp.exp(part - jnp.max(part, axis=0, keepdims=True))
+                probs.append(grown * (real_query / jnp.sum(grown, axis=0, keepdims=True)))
+            probs = jnp.concatenate(probs, axis=0)
+            p_ref[pl.ds(pl.multiple_of((at * OCTS + octet) * ROWS_S, ROWS_S), ROWS_S), :] = probs.astype(BF16)
+            mixed = dot_nn(turned(probs).astype(BF16), spread(v, pair_scr))
+            o_ref[rows, octet * OCT_W : (octet + 1) * OCT_W] = by_side(mixed, first_side).astype(BF16)
         return carry
 
-    lax.fori_loop(0, STEP_IMAGES * WINDOWS, one_window, 0)
-    y_scr[...] = xs_ref[...] + dot_nn(o_ref[...], wproj_ref[...]) + shift_ref[2:3, :]
-    out_of_slots(y_scr, y_ref)
-
-    @pl.when(step == 0)
-    def _():
-        for k in gather.round()[1:]:
-            gather.column(k)
-
-    @pl.when(step == 1)
-    def _():
-        for k in gather.round():
-            gather.first(k)
-
-    @pl.when(step == 2)
+    half_loop = STEP_IMAGES * WINDOWS // 2
+
+    @pl.when(step >= steps)
+    def _():
+        lax.fori_loop(0, half_loop, one_window, 0, unroll=4)
+
+    @pl.when(step == steps + 1)
+    def _():
+        for k in rest.round()[1:]:
+            rest.column(k)
+
+    @pl.when(step == steps + 2)
+    def _():
+        for k in rest.round():
+            rest.first(k)
+
+    @pl.when(step == last)
     def _():
         for a in range(2):
-            for k in gather.round():
-                gather.second(a, k)
+            for k in rest.round():
+                rest.second(a, k)
+
+    @pl.when(step >= steps)
+    def _():
+        lax.fori_loop(half_loop, 2 * half_loop, one_window, 0, unroll=4)
 
     @pl.when(step == last)
     def _():
-        gather.end()
+        rest.end()
 
 
 def mlp_kernel(
-    y_ref,
+    xs_ref,
+    o_ref,
     e_ref,
+    wproj_ref,
     w1_ref,
     w2_ref,
     gain_ref,
@@ -990,14 +1020,18 @@
     dy_ref,
     g1_ref,
     g2_ref,
+    gproj_ref,
     hsum_ref,
     sums_ref,
     acc1,
     acc2,
+    accp,
     m_scr,
     da_scr,
     a2_scr,
     e_scr,
+    slot_scr,
+    y_ref,
 ):
     step = pl.program_id(0)
 
@@ -1005,9 +1039,12 @@
     def _():
         acc1[...] = jnp.zeros_like(acc1)
         acc2[...] = jnp.zeros_like(acc2)
+        accp[...] = jnp.zeros_like(accp)
         hsum_ref[...] = jnp.zeros_like(hsum_ref)
         sums_ref[...] = jnp.zeros_like(sums_ref)
 
+    slot_scr[...] = xs_ref[...] + dot_nn(o_ref[...], wproj_ref[...]) + shift_ref[2:3, :]
+    out_of_slots(slot_scr, y_ref)
     white, inverse = whiten(y_ref[...])
     a2_scr[...] = (white * gain_ref[1:2, :] + shift_ref[1:2, :]).astype(BF16)
     e_scr[...] = e_ref[...].astype(BF16)
@@ -1041,7 +1078,10 @@
     da = da_scr[...]
     t2 = da * gain_ref[1:2, :]
     dy = e_ref[...] + inverse * (t2 - row_mean(t2) - white * row_mean(t2 * white))
-    dy_ref[...] = dy
+    m_scr[...] = dy
+    dy_ref[...] = jnp.zeros_like(dy_ref)
+    into_slots(m_scr, dy_ref)
+    accp[...] += dot_tn(o_ref[...], dy_ref[...].astype(BF16))
     sums_ref[0:1, :] += jnp.sum(da * white, axis=0, keepdims=True)
     sums_ref[1:2, :] += jnp.sum(da, axis=0, keepdims=True)
     sums_ref[2:3, :] += jnp.sum(dy, axis=0, keepdims=True)
@@ -1051,93 +1091,78 @@
     def _():
         g1_ref[...] = acc1[...].astype(BF16)
         g2_ref[...] = acc2[...].astype(BF16)
-
-
-def attention_backward_kernel(
-    ndp,
-    nt,
-    images,
-    dy_ref,
-    xs_ref,
-    qkv_ref,
-    p_ref,
-    o_ref,
-    wqkv_ref,
-    wproj_ref,
-    gain_ref,
-    shift_ref,
-    g1_ref,
-    g2_ref,
-    m1_ref,
-    m2_ref,
-    gin_ref,
-    gqkv_ref,
-    gproj_ref,
-    dbias_ref,
-    hsum_ref,
-    sums_ref,
-    slab1_ref,
-    slab2_ref,
-    bundle_ref,
-    accq,
-    accp,
-    dy_scr,
-    do_scr,
-    du_scr,
-    mask_scr,
-    turn_scr,
-    g_scr,
-    fresh,
-    *comm_scr,
-):
+        gproj_ref[...] = accp[...].astype(BF16)
+
+
+def attention_backward_kernel(ndp, nt, images, steps, *refs):
+    refs = list(refs)
+
+    def take(n):
+        taken = refs[:n]
+        del refs[:n]
+        return taken
+
+    dy_ref, xs_ref, a1_ref, qkv_ref, p_ref, wqkv_ref, wproj_ref, gain_ref, index_ref = take(9)
+    hidden_ref, sums2_ref = take(2)
+    grads, momenta, (qkv_momentum,) = take(3), take(3), take(1)
+    (gin_ref,) = take(1)
+    slabs, (qkv_slab,) = take(3), take(1)
+    bundle0, bundle1, small_out = take(3)
+    accq, gq, do_scr, du_scr, pair_scr, side_scr, g_scr, dbias_ref, hsum_ref, sums_ref = take(10)
+    idx_scr, turned_idx, table_scr, fresh0, fresh1 = take(5)
+    small, small_in, small_send, small_recv = take(4)
+    place = Place(ndp, nt)
     step, last = pl.program_id(0), pl.num_programs(0) - 1
-    place = Place(ndp, nt)
-    share = Share(place, 1, fresh, bundle_ref, comm_scr[:3])
-    reduce = Reduce(place, (g1_ref, g2_ref), comm_scr[3:])
+    share0 = Share(place, 0, fresh0, bundle0, take(3))
+    share1 = Share(place, 1, fresh1, bundle1, take(3))
+    early = Reduce(place, grads, take(18))
+    late = Reduce(place, (gq,), take(8))
+    tiny = SmallSum(place, small, small_in, small_send, small_recv)
 
     @pl.when(step == 0)
     def _():
         place.greet()
-        reduce.begin()
-        fresh[...] = jnp.zeros_like(fresh)
-        mask_scr[...] = head_mask(range(OCT))
-        turn_scr[...] = head_mask(TURNED)
+        early.begin()
+        fresh0[...] = jnp.zeros_like(fresh0)
+        fresh1[...] = jnp.zeros_like(fresh1)
+        pair_scr[...] = pair_mask()
+        side_scr[...] = side_mask()
         accq[...] = jnp.zeros_like(accq)
-        accp[...] = jnp.zeros_like(accp)
         dbias_ref[...] = jnp.zeros_like(dbias_ref)
         hsum_ref[...] = jnp.zeros_like(hsum_ref)
         sums_ref[...] = jnp.zeros_like(sums_ref)
-        dy_scr[...] = jnp.zeros_like(dy_scr)
-
-    @pl.when(step == 2)
-    def _():
-        reduce.pass_on(0, 0)
-
-    @pl.when(step == last)
-    def _():
-        share.along_z()
-
-    into_slots(dy_ref, dy_scr)
-    dr = dy_scr[...].astype(BF16)
-    do_scr[...] = dot_nt(dr, wproj_ref[...]).astype(BF16)
-    accp[...] += dot_tn(o_ref[...], dr)
+
+    first_row = pl.multiple_of(lax.rem(step, steps) * STEP_SLOTS, STEP_SLOTS)
+    step_rows = pl.ds(first_row, STEP_SLOTS)
+
+    @pl.when(step < steps)
+    def _():
+        do_scr[...] = dot_nt(dy_ref[...].astype(BF16), wproj_ref[...]).astype(BF16)
+
     scale = HEAD ** (-0.5)
+    first_side = lax.broadcasted_iota(jnp.int32, (SLOT, OCT_W), 1) // HEAD % 2 == 0
 
     def one_window(at, carry):
         rows = pl.ds(pl.multiple_of(at * SLOT, SLOT), SLOT)
+        out_rows = pl.ds(pl.multiple_of(first_row + at * SLOT, SLOT), SLOT)
         for octet in range(OCTS):
             q = qkv_ref[rows, octet * OCT_W : (octet + 1) * OCT_W]
             k = qkv_ref[rows, D + octet * OCT_W : D + (octet + 1) * OCT_W]
             v = qkv_ref[rows, 2 * D + octet * OCT_W : 2 * D + (octet + 1) * OCT_W]
             do = do_scr[rows, octet * OCT_W : (octet + 1) * OCT_W]
-            probs = p_ref[rows, octet * OCT_S : (octet + 1) * OCT_S]
-            wide_do = spread(do, mask_scr)
-            weighted = probs.astype(F32) * dot_nt(v, wide_do)
-            ds = weighted - probs.astype(F32) * jnp.sum(weighted, axis=0, keepdims=True)
+            probs = p_ref[pl.ds(pl.multiple_of((at * OCTS + octet) * ROWS_S, ROWS_S), ROWS_S), :]
+            side_do = spread(do, side_scr)
+            weighted = probs.astype(F32) * dot_nt(spread(v, pair_scr), side_do)
+            ds = []
+            for pair in range(PAIRS):
+                part = slice(pair * SLOT, (pair + 1) * SLOT)
+                total = jnp.sum(weighted[part], axis=0, keepdims=True)
+                ds.append(weighted[part] - probs[part].astype(F32) * total)
+            ds = jnp.concatenate(ds, axis=0)
             dbias_ref[octet] += ds
-            dq = dot_nn(turned(ds).astype(BF16), spread(k, turn_scr)) * scale
-            dk = dot_nn(ds.astype(BF16), spread(q, mask_scr))
-            dv = dot_nn(probs, wide_do)
+            dq = by_side(dot_nn(turned(ds).astype(BF16), spread(k, pair_scr)), first_side) * scale
+            dk = by_pair(ds.astype(BF16), spread(q, side_scr))
+            dv = by_pair(probs, side_do)
             lanes = slice(octet * OCT_W, (octet + 1) * OCT_W)
             hsum_ref[0:1, lanes] += jnp.sum(dq, axis=0, keepdims=True)
             hsum_ref[1:2, lanes] += jnp.sum(dv, axis=0, keepdims=True)
@@ -1145,47 +1170,96 @@
                 for inner in range(OCT_W // PART):
                     group = octet * (OCT_W // PART) + inner
                     at_col = (group * 3 + part) * PART
-                    du_scr[rows, at_col : at_col + PART] = grad[
+                    du_scr[out_rows, at_col : at_col + PART] = grad[
                         :, inner * PART : (inner + 1) * PART
                     ].astype(BF16)
         return carry
 
-    lax.fori_loop(0, STEP_IMAGES * WINDOWS, one_window, 0)
+    half_loop = STEP_IMAGES * WINDOWS // 2
+
+    @pl.when(step < steps)
+    def _():
+        lax.fori_loop(0, half_loop, one_window, 0, unroll=4)
 
     @pl.when(step == 0)
     def _():
-        reduce.pass_on(1, 1)
-        reduce.pass_on(1, 0)
+        early.pass_on(1, 1)
+        early.pass_on(1, 0)
+
+    @pl.when(step == 2)
+    def _():
+        early.pass_on(0, 0)
+
+    @pl.when(step < steps)
+    def _():
+        lax.fori_loop(half_loop, 2 * half_loop, one_window, 0, unroll=4)
 
     @pl.when(step == 1)
     def _():
-        reduce.pass_on(0, 1)
-
-    @pl.when(step == 2)
-    def _():
-        renew(reduce.totals(), (m1_ref, m2_ref), (slab1_ref, slab2_ref), fresh, images)
-        share.hand()
+        early.pass_on(0, 1)
+
+    @pl.when(step == steps - 1)
+    def _():
+        renew(early.totals(), momenta, slabs, (fresh0.at[1], fresh1.at[0], fresh1.at[1]), images)
+        share1.hand()
+
+    @pl.when(step < steps)
+    def _():
+        accq[...] += dot_tn(du_scr[step_rows, :], a1_ref[...])
+
+    @pl.when(step == steps - 1)
+    def _():
+        rows = gq.shape[1]
+        for i in range(gq.shape[0]):
+            gq[i] = accq[i * rows : (i + 1) * rows, :].astype(BF16)
+        share1.along_z()
+        late.begin()
+
+    @pl.when(step >= steps)
+    def _():
+        white, inverse = whiten(xs_ref[...])
+        da = dot_nn(du_scr[step_rows, :], wqkv_ref[...])
+        t1 = da * gain_ref[0:1, :]
+        g_scr[...] = dy_ref[...] + inverse * (t1 - row_mean(t1) - white * row_mean(t1 * white))
+        out_of_slots(g_scr, gin_ref)
+        sums_ref[0:1, :] += jnp.sum(da * white, axis=0, keepdims=True)
+        sums_ref[1:2, :] += jnp.sum(da, axis=0, keepdims=True)
+
+    @pl.when(step == steps)
+    def _():
+        late.pass_on(1, 1)
+        late.pass_on(1, 0)
+
+    @pl.when(step == steps + 1)
+    def _():
+        table_sums(dbias_ref, index_ref, table_scr, idx_scr, turned_idx)
+        share1.along_y()
+
+    @pl.when(step == steps + 2)
+    def _():
+        late.pass_on(0, 1)
 
     @pl.when(step == last)
     def _():
-        share.along_y()
-
-    white, inverse = whiten(xs_ref[...])
-    a1 = (white * gain_ref[0:1, :] + shift_ref[0:1, :]).astype(BF16)
-    accq[...] += dot_tn(du_scr[...], a1)
-    da = dot_nn(du_scr[...], wqkv_ref[...])
-    t1 = da * gain_ref[0:1, :]
-    g_scr[...] = dy_scr[...] + inverse * (t1 - row_mean(t1) - white * row_mean(t1 * white))
-    out_of_slots(g_scr, gin_ref)
-    sums_ref[0:1, :] += jnp.sum(da * white, axis=0, keepdims=True)
-    sums_ref[1:2, :] += jnp.sum(da, axis=0, keepdims=True)
-
-    @pl.when(step == pl.num_programs(0) - 1)
-    def _():
-        gqkv_ref[...] = accq[...].astype(BF16)
-        gproj_ref[...] = accp[...].astype(BF16)
-        share.end()
-        reduce.end()
+        pack_small(small, sums_ref, sums2_ref, hsum_ref, hidden_ref, table_scr)
+        late.pass_on(0, 0, tiny.begin)
+        tiny.step()
+        tiny.go_on()
+        renew(late.totals(), (qkv_momentum,), (qkv_slab,), (fresh0.at[0],), images)
+        tiny.step()
+        share0.hand()
+        tiny.go_on()
+        tiny.step()
+        tiny.go_on()
+        share0.along_z()
+        tiny.step()
+        tiny.go_on()
+        share0.along_y()
+        small_out[...] = tiny.end() / images
+        share1.end()
+        share0.end()
+        early.end()
+        late.end()
 
 
 def whole(shape):
@@ -1213,75 +1287,92 @@
 
 
 def attention_forward(
-    tokens, wqkv, wproj, gains, shifts, head_biases, table, index, regions, slabs, ndp, nt, collective_id
+    tokens, gains, shifts, head_biases, table, index, regions, slabs, qkv_slab, ndp, nt, collective_ids
 ):
     n = ndp * nt
     steps = tokens.shape[0] // STEP_ROWS
     slots = steps * STEP_SLOTS
-    return pl.pallas_call(
-        functools.partial(attention_forward_kernel, ndp, nt),
-        grid=(steps,),
+    fused = qkv_slab.shape[0] % 16 == 0
+    if not fused:
+        (qkv_slab,) = gather_weights((qkv_slab,), ndp, nt, collective_ids[1])
+    early = lambda i: (jnp.minimum(i, steps - 1), 0)
+    late = lambda i: (jnp.maximum(i - steps, 0), 0)
+    any_ = pl.BlockSpec(memory_space=pl.ANY)
+    gathered = tuple(slabs) + ((qkv_slab,) if fused else ())
+    results = pl.pallas_call(
+        functools.partial(attention_forward_kernel, ndp, nt, steps, fused),
+        grid=(2 * steps,),
         out_shape=(
-            shape_of(tokens.shape, F32),
             shape_of((slots, D), F32),
+            shape_of((slots, D), BF16),
             shape_of((slots, 3 * D), BF16),
-            shape_of((slots, OCTS * OCT_S), BF16),
+            shape_of((slots * OCTS * PAIRS, LANES), BF16),
             shape_of((slots, D), BF16),
         )
-        + tuple(shape_of((n,) + s.shape, BF16) for s in slabs),
+        + tuple(shape_of((n,) + s.shape, BF16) for s in gathered),
         in_specs=[
-            rows_of(STEP_ROWS, D),
-            whole(wqkv.shape),
-            whole(wproj.shape),
+            pl.BlockSpec((STEP_ROWS, D), early),
             whole(gains.shape),
             whole(shifts.shape),
             whole(head_biases.shape),
             whole(table.shape),
             whole(index.shape),
             pl.BlockSpec(memory_space=pltpu.SMEM),
-            whole(slabs[0].shape),
-            whole(slabs[1].shape),
-        ],
+        ]
+        + [whole(s.shape) for s in slabs]
+        + [whole(qkv_slab.shape)],
         out_specs=(
-            rows_of(STEP_ROWS, D),
-            rows_of(STEP_SLOTS, D),
-            rows_of(STEP_SLOTS, 3 * D),
-            rows_of(STEP_SLOTS, OCTS * OCT_S),
-            rows_of(STEP_SLOTS, D),
-            pl.BlockSpec(memory_space=pl.ANY),
-            pl.BlockSpec(memory_space=pl.ANY),
-        ),
+            pl.BlockSpec((STEP_SLOTS, D), early),
+            pl.BlockSpec((STEP_SLOTS, D), early),
+            pl.BlockSpec((STEP_SLOTS, 3 * D), late),
+            pl.BlockSpec((STEP_SLOTS * OCTS * PAIRS, LANES), late),
+            pl.BlockSpec((STEP_SLOTS, D), late),
+        )
+        + (any_,) * len(gathered),
         scratch_shapes=[
-            pltpu.VMEM((WINDOWS, OCTS, SLOT, OCT_S), F32),
+            pltpu.VMEM((WINDOWS, OCTS, ROWS_S, LANES), F32),
             pltpu.VMEM((LANES, LANES), F32),
             pltpu.VMEM((HEADS, 2 * LANES), F32),
-            pltpu.VMEM((OCT_S, OCT_W), BF16),
-            pltpu.VMEM((OCT_S, OCT_W), BF16),
-            pltpu.VMEM((STEP_SLOTS, D), F32),
+            pltpu.VMEM((ROWS_S, OCT_W), BF16),
+            pltpu.VMEM((2 * SLOT, OCT_W), BF16),
+            pltpu.VMEM((slots, D), BF16),
         ]
-        + Gather.scratch([s.shape for s in slabs], n),
-        compiler_params=remote_params(collective_id),
+        + Gather.scratch([s.shape for s in slabs], n)
+        + (
+            Gather.scratch([qkv_slab.shape], n)
+            + [pltpu.VMEM((n * qkv_slab.shape[0], D), BF16), pltpu.SemaphoreType.DMA((n,))]
+            if fused
+            else []
+        ),
+        compiler_params=remote_params(collective_ids[0]),
         name="attention_forward",
-    )(tokens, wqkv, wproj, gains, shifts, head_biases, table, index, regions, *slabs)
-
-
-def mlp(middle, out_grad, w1, w2, gains, shifts, hidden_bias):
-    steps = middle.shape[0] // STEP_ROWS
+    )(tokens, gains, shifts, head_biases, table, index, regions, *slabs, qkv_slab)
+    weights = [g.reshape(-1, D) for g in results[5:]]
+    if not fused:
+        weights.append(qkv_slab)
+    return results[:5], weights
+
+
+def mlp(xs, mixed, out_grad, wproj, w1, w2, gains, shifts, hidden_bias):
+    steps = out_grad.shape[0] // STEP_ROWS
     hidden = w1.shape[0]
     return pl.pallas_call(
         mlp_kernel,
         grid=(steps,),
         out_shape=(
-            shape_of(middle.shape, F32),
-            shape_of(middle.shape, F32),
+            shape_of(out_grad.shape, F32),
+            shape_of(xs.shape, F32),
             shape_of(w1.shape, BF16),
             shape_of(w2.shape, BF16),
+            shape_of(wproj.shape, BF16),
             shape_of((1, hidden), F32),
             shape_of((4, D), F32),
         ),
         in_specs=[
+            rows_of(STEP_SLOTS, D),
+            rows_of(STEP_SLOTS, D),
             rows_of(STEP_ROWS, D),
-            rows_of(STEP_ROWS, D),
+            whole(wproj.shape),
             whole(w1.shape),
             whole(w2.shape),
             whole(gains.shape),
@@ -1290,88 +1381,133 @@
         ],
         out_specs=(
             rows_of(STEP_ROWS, D),
-            rows_of(STEP_ROWS, D),
+            rows_of(STEP_SLOTS, D),
             whole(w1.shape),
             whole(w2.shape),
+            whole(wproj.shape),
             whole((1, hidden)),
             whole((4, D)),
         ),
         scratch_shapes=[
             pltpu.VMEM(w1.shape, F32),
             pltpu.VMEM(w2.shape, F32),
+            pltpu.VMEM(wproj.shape, F32),
             pltpu.VMEM((STEP_ROWS, D), F32),
             pltpu.VMEM((STEP_ROWS, D), F32),
             pltpu.VMEM((STEP_ROWS, D), BF16),
             pltpu.VMEM((STEP_ROWS, D), BF16),
+            pltpu.VMEM((STEP_SLOTS, D), F32),
+            pltpu.VMEM((STEP_ROWS, D), F32),
         ],
         compiler_params=PARAMS,
         name="mlp",
-    )(middle, out_grad, w1, w2, gains, shifts, hidden_bias.reshape(1, hidden))
+    )(xs, mixed, out_grad, wproj, w1, w2, gains, shifts, hidden_bias.reshape(1, hidden))
 
 
 def attention_backward(
-    dy, xs, qkv, probs, mixed, wqkv, wproj, gains, shifts, grads, momenta, ndp, nt, images, collective_id
+    dy,
+    xs,
+    a1,
+    qkv,
+    probs,
+    wqkv,
+    wproj,
+    gains,
+    index,
+    hidden_sum,
+    sums2,
+    grads,
+    momenta,
+    qkv_momentum,
+    ndp,
+    nt,
+    images,
+    collective_id,
 ):
     n = ndp * nt
-    slabs = [m.shape[0] for m in momenta]
-    grads = tuple(g.reshape(n, r, D) for g, r in zip(grads, slabs))
+    rows = [m.shape[0] for m in momenta]
+    qkv_rows = qkv_momentum.shape[0]
+    steps = dy.shape[0] // STEP_SLOTS
+    grads = tuple(g.reshape(n, r, D) for g, r in zip(grads, rows))
     any_ = pl.BlockSpec(memory_space=pl.ANY)
-    steps = dy.shape[0] // STEP_ROWS
+    early = lambda i: (jnp.minimum(i, steps - 1), 0)
+    late = lambda i: (jnp.maximum(i - steps, 0), 0)
+    both = lambda i: (lax.rem(i, steps), 0)
+    tall0, tall1 = padded((qkv_rows, rows[0])), padded(rows[1:])
+    small_steps = 3 + (ndp // 2 - 1).bit_length()
     return pl.pallas_call(
-        functools.partial(attention_backward_kernel, ndp, nt, images),
-        grid=(steps,),
-        out_shape=(
-            shape_of(dy.shape, F32),
-            shape_of(wqkv.shape, BF16),
-            shape_of(wproj.shape, BF16),
-            shape_of((OCTS, SLOT, OCT_S), F32),
-            shape_of((2, D), F32),
-            shape_of((2, D), F32),
-        )
-        + tuple(shape_of(m.shape, F32) for m in momenta)
-        + (shape_of((ndp, nt, padded(slabs), D), BF16),),
+        functools.partial(attention_backward_kernel, ndp, nt, images, steps),
+        grid=(2 * steps,),
+        out_shape=(shape_of((steps * STEP_ROWS, D), F32),)
+        + tuple(shape_of((r, D), F32) for r in rows + [qkv_rows])
+        + (
+            shape_of((ndp, nt, tall0, D), BF16),
+            shape_of((ndp, nt, tall1, D), BF16),
+            shape_of((SMALL_ROWS, D), F32),
+        ),
         in_specs=[
-            rows_of(STEP_ROWS, D),
-            rows_of(STEP_SLOTS, D),
-            rows_of(STEP_SLOTS, 3 * D),
-            rows_of(STEP_SLOTS, OCTS * OCT_S),
-            rows_of(STEP_SLOTS, D),
+            pl.BlockSpec((STEP_SLOTS, D), both),
+            pl.BlockSpec((STEP_SLOTS, D), late),
+            pl.BlockSpec((STEP_SLOTS, D), early),
+            pl.BlockSpec((STEP_SLOTS, 3 * D), early),
+            pl.BlockSpec((STEP_SLOTS * OCTS * PAIRS, LANES), early),
             whole(wqkv.shape),
             whole(wproj.shape),
             whole(gains.shape),
-            whole(shifts.shape),
+            whole(index.shape),
+            whole(hidden_sum.shape),
+            whole(sums2.shape),
             any_,
             any_,
-            whole(momenta[0].shape),
-            whole(momenta[1].shape),
-        ],
-        out_specs=(
-            rows_of(STEP_ROWS, D),
-            whole(wqkv.shape),
-            whole(wproj.shape),
-            whole((OCTS, SLOT, OCT_S)),
-            whole((2, D)),
-            whole((2, D)),
-            whole(momenta[0].shape),
-            whole(momenta[1].shape),
             any_,
-        ),
+        ]
+        + [whole((r, D)) for r in rows + [qkv_rows]],
+        out_specs=(pl.BlockSpec((STEP_ROWS, D), late),)
+        + tuple(whole((r, D)) for r in rows + [qkv_rows])
+        + (any_, any_, whole((SMALL_ROWS, D))),
         scratch_shapes=[
             pltpu.VMEM(wqkv.shape, F32),
-            pltpu.VMEM(wproj.shape, F32),
+            pltpu.VMEM((n, qkv_rows, D), BF16),
+            pltpu.VMEM((STEP_SLOTS, D), BF16),
+            pltpu.VMEM((steps * STEP_SLOTS, 3 * D), BF16),
+            pltpu.VMEM((ROWS_S, OCT_W), BF16),
+            pltpu.VMEM((2 * SLOT, OCT_W), BF16),
             pltpu.VMEM((STEP_SLOTS, D), F32),
-            pltpu.VMEM((STEP_SLOTS, D), BF16),
-            pltpu.VMEM((STEP_SLOTS, 3 * D), BF16),
-            pltpu.VMEM((OCT_S, OCT_W), BF16),
-            pltpu.VMEM((OCT_S, OCT_W), BF16),
-            pltpu.VMEM((STEP_SLOTS, D), F32),
-            pltpu.VMEM((2, padded(slabs), D), BF16),
+            pltpu.VMEM((OCTS, ROWS_S, LANES), F32),
+            pltpu.VMEM((2, D), F32),
+            pltpu.VMEM((2, D), F32),
+            pltpu.VMEM((LANES, LANES), F32),
+            pltpu.VMEM((SLOT, LANES), F32),
+            pltpu.VMEM((HEADS, 2 * LANES), F32),
+            pltpu.VMEM((2, tall0, D), BF16),
+            pltpu.VMEM((2, tall1, D), BF16),
+            pltpu.VMEM((small_steps + 1, SMALL_ROWS, D), F32),
+            pltpu.VMEM((small_steps, SMALL_ROWS, D), F32),
+            pltpu.SemaphoreType.DMA((small_steps,)),
+            pltpu.SemaphoreType.DMA((small_steps,)),
         ]
         + Share.scratch(n, nt)
-        + Reduce.scratch(slabs, n),
+        + Share.scratch(n, nt)
+        + Reduce.scratch(rows, n)
+        + Reduce.scratch([qkv_rows], n),
         compiler_params=remote_params(collective_id),
         name="attention_backward",
-    )(dy, xs, qkv, probs, mixed, wqkv, wproj, gains, shifts, *grads, *momenta)
+    )(
+        dy,
+        xs,
+        a1,
+        qkv,
+        probs,
+        wqkv,
+        wproj,
+        gains,
+        index,
+        hidden_sum,
+        sums2,
+        *grads,
+        *momenta,
+        qkv_momentum,
+    )
 
 
 ORDER = (0, 2, 1, 3)
@@ -1425,53 +1561,45 @@
         for m, wide in zip((qkv_momentum, fc1_momentum, proj_momentum, fc2_momentum), WIDE)
     )
     ndp, nt = lax.axis_size("dp"), lax.axis_size("tensor")
-    wqkv, wproj = gather_weights(weights[0::2], ndp, nt, 0)
-    middle, xs, qkv, probs, mixed, w1, w2 = attention_forward(
+    forward, gathered = attention_forward(
         tokens,
-        wqkv,
-        wproj,
         norm_gains,
         shift_biases,
         head_biases,
         position_table.T,
         position_index,
         region_ids,
-        weights[1::2],
+        weights[1:],
+        weights[0],
         ndp,
         nt,
-        1,
+        (1, 0),
     )
-    w1, w2 = w1.reshape(-1, D), w2.reshape(-1, D)
-    output, dy, g1, g2, hidden_sum, sums2 = mlp(
-        middle, out_grad, w1, w2, norm_gains, shift_biases, hidden_bias
+    xs, a1, qkv, probs, mixed = forward
+    w1, wproj, w2, wqkv = gathered
+    output, dy, g1, g2, gproj, hidden_sum, sums2 = mlp(
+        xs, mixed, out_grad, wproj, w1, w2, norm_gains, shift_biases, hidden_bias
     )
-    input_grad, gqkv, gproj, dbias, head_sum, sums1, slab1, slab2, bundle1 = attention_backward(
+    input_grad, slab2, slab1, slab3, slab0, bundle0, bundle1, total = attention_backward(
         dy,
         xs,
+        a1,
         qkv,
         probs,
-        mixed,
         wqkv,
         wproj,
         norm_gains,
-        shift_biases,
-        (g1, g2),
-        momenta[1::2],
+        position_index,
+        hidden_sum,
+        sums2,
+        (gproj, g1, g2),
+        (momenta[2], momenta[1], momenta[3]),
+        momenta[0],
         ndp,
         nt,
         images,
         2,
     )
-    by_head = (
-        dbias.reshape(OCTS, SLOT, OCT, SLOT)[:, :SPOTS, :, :SPOTS]
-        .transpose(0, 2, 3, 1)
-        .reshape(HEADS, SPOTS * SPOTS)
-    )
-    onehot = (
-        position_index.reshape(-1)[:, None]
-        == jnp.arange(position_table.shape[0], dtype=jnp.int32)[None, :]
-    ).astype(F32)
-    table_part = jnp.dot(onehot.T, by_head.T, precision=lax.Precision.HIGHEST)
     small_params = (norm_gains, shift_biases, head_biases, hidden_bias.reshape(1, -1), position_table.T)
     small_moms = (
         gain_momentum,
@@ -1480,20 +1608,8 @@
         hidden_bias_momentum.reshape(1, -1),
         table_momentum.T,
     )
-    slab0, slab3, bundle0, total = update(
-        (gqkv, gproj),
-        momenta[0::2],
-        (sums1, sums2, head_sum, hidden_sum, table_part.T),
-        ndp,
-        nt,
-        images,
-        3,
-    )
-    slab_grads = (slab0, slab1, slab3, slab2)
-    bundles = (bundle0, bundle1)
-    landed = return_updates(
-        newton_schulz(bundles), tuple(b.shape[2] for b in bundles), ndp, nt, 4
-    )
+    slab_grads = (slab0, slab1, slab2, slab3)
+    landed = newton_schulz((bundle0, bundle1), 3)
     rates = tuple(MATRIX_RATE * factor for factor in FACTORS)
     results = finish(landed, total, slab_grads, momenta, weights, small_params, small_moms, rates)
     slab_grads, new_weights, new_momenta = (results[i * nt : (i + 1) * nt] for i in range(3))

time: 262 us -> 220 us (0.84)
  Pallas kernels: 253 us -> 216 us
    pallas_call x6 -> x3, Pallas kernels: 176 us -> 130 us  [the longest x1 57.9 us: attention_forward(): pl.pallas_call(functools.partial(attention_forward_kernel, ndp, nt, steps...]
    pallas_call x1, Pallas kernels: 75.1 us -> 82.6 us  [attention_backward(): pl.pallas_call(functools.partial(attention_backward_kernel, ndp, nt, imag...]
where the time goes in v4:
time: 220 us; the launch traced here: 218 us
  Pallas kernels  216 us (98%)
    pallas_call x1, Pallas kernels, attention_backward(): pl.pallas_call(functools.partial(attention_backward_kernel, ndp, nt, imag...  82.6 us
    pallas_call x1, Pallas kernels, attention_forward(): pl.pallas_call(functools.partial(attention_forward_kernel, ndp, nt, steps...  57.9 us
    pallas_call x1, Pallas kernels, mlp(): pl.pallas_call(mlp_kernel, grid=(steps,), out_shape=(shape_of(out_grad.sh...  45.8 us
    pallas_call x1, Pallas kernels, newton_schulz(): pl.pallas_call(functools.partial(newton_schulz_kernel, nt, heights), out_...  26.7 us

profile of v4, /device:TPU:17, one launch (start us, length us, event | category | flops | bytes accessed | tf_op | source)
XLA Modules:
  0.0 218.1 jit_solution(9512495014829460117)
XLA Ops:
  0.7 57.9 %attention_forward.1 = (f32[2048,512]{1,0:T(8,128)}, bf16[2048,512]{1,0:T(8,128)(2,1)}, bf16[2048,1536]{1,0:T(8,128)(2,1)}, bf16[16384,128]{1,0:T(8,128)(2,1)}, ...) custom-call(f32[1568,512]{1,0:T(8,128)} %refs_0_.1, ...), custom_call_target="tpu_custom_call" | custom-call | tf_op jit(solution)/shard_map/attention_forward/pallas_call | solution.py:1302
  58.6 45.8 %mlp.1 = (f32[1568,512]{1,0:T(8,128)}, f32[2048,512]{1,0:T(8,128)}, bf16[2048,512]{1,0:T(8,128)(2,1)}, bf16[2048,512]{1,0:T(8,128)(2,1)}, bf16[512,512]{1,0:T(8,...) custom-call(f32[2048,512]{1,0:T(8,128)} %get-tuple-element.82.xs_ref.refs_1_, bf16[2048,512]{1,0:T(8,128)(2,1)} %get-tuple-element.83.o_ref, ...), custom_call_target="tpu_custom_call" | custom-call | tf_op jit(solution)/shard_map/mlp/pallas_call | solution.py:1359
  104.4 82.6 %attention_backward.1 = (f32[1568,512]{1,0:T(8,128)}, f32[16,512]{1,0:T(8,128)}, f32[64,512]{1,0:T(8,128)}, f32[64,512]{1,0:T(8,128)}, f32[48,512]{1,0:T(8,128)}...) custom-call(f32[2048,512]{1,0:T(8,128)} %get-tuple-element.88.refs_0_, ...), custom_call_target="tpu_custom_call" | custom-call | tf_op jit(solution)/shard_map/attention_backward/pallas_call | solution.py:1438
  187.0 0.0 copy-start
  187.0 26.7 %newton_schulz.1 = (bf16[2,48,512]{2,1,0:T(8,128)(2,1)}, bf16[2,64,512]{2,1,0:T(8,128)(2,1)}) custom-call(bf16[1536,512]{1,0:T(8,128)(2,1)} %bitcast.66, bf16[2048,512]{1,0:T(8,128)(2,1)} %bitcast.61), custom_call_target="tpu_custom_call" | custom-call | tf_op jit(solution)/shard_map/newton_schulz/pallas_call | solution.py:754
  213.7 2.7 %finish.1 = (f32[48,512]{1,0:T(8,128)}, f32[64,512]{1,0:T(8,128)}, f32[16,512]{1,0:T(8,128)}, f32[64,512]{1,0:T(8,128)}, f32[48,512]{1,0:T(8,128)}, /*index=5*/f...) custom-call(bf16[2,48,512]{2,1,0:T(8,128)(2,1)} %get-tuple-element.1, ...), custom_call_target="tpu_custom_call" | custom-call | tf_op jit(solution)/shard_map/finish/pallas_call | solution.py:812
  216.4 0.0 copy-done
  216.4 1.7 copy.52
Async XLA Ops:
  187.0 29.4 %copy-start = (f32[1568,512]{1,0:T(8,128)S(1)}, f32[1568,512]{1,0:T(8,128)}, u32[]{:S(2)}) copy-start(f32[1568,512]{1,0:T(8,128)} %get-tuple-element.165) | copy-start | bytes 9633796

commit v5 on v4

--- a/solution.py
+++ b/solution.py
@@ -316,7 +316,6 @@
             self.local(m).start()
         for k in self.round()[1:]:
             self.send("z", 0, 0, k)
-        self.column(0)
 
     def end(self):
         everything = [("z", 0, 0, k) for k in self.round()[1:]]
@@ -333,6 +332,11 @@
     def at_once(self):
         self.place.greet()
         self.begin()
+        self.column(0)
+        self.spread()
+        self.end()
+
+    def spread(self):
         for k in self.round()[1:]:
             self.column(k)
             self.first(k - 1)
@@ -340,7 +344,6 @@
         for a in range(2):
             for k in self.round():
                 self.second(a, k)
-        self.end()
 
 
 class Reduce:
@@ -883,6 +886,7 @@
         place.greet()
         if fused:
             qkv_gather.begin()
+            qkv_gather.column(0)
 
     @pl.when(step < steps)
     def _():
@@ -918,6 +922,7 @@
     @pl.when(step == 2)
     def _():
         rest.begin()
+        rest.column(0)
 
     @pl.when(step == steps - 1)
     def _():
@@ -1181,27 +1186,22 @@
     def _():
         lax.fori_loop(0, half_loop, one_window, 0, unroll=4)
 
+    @pl.when(step == 2)
+    def _():
+        early.pass_on(0, 1)
+
+    @pl.when(step == 3)
+    def _():
+        early.pass_on(0, 0)
+
+    @pl.when(step < steps)
+    def _():
+        lax.fori_loop(half_loop, 2 * half_loop, one_window, 0, unroll=4)
+
     @pl.when(step == 0)
     def _():
         early.pass_on(1, 1)
         early.pass_on(1, 0)
-
-    @pl.when(step == 2)
-    def _():
-        early.pass_on(0, 0)
-
-    @pl.when(step < steps)
-    def _():
-        lax.fori_loop(half_loop, 2 * half_loop, one_window, 0, unroll=4)
-
-    @pl.when(step == 1)
-    def _():
-        early.pass_on(0, 1)
-
-    @pl.when(step == steps - 1)
-    def _():
-        renew(early.totals(), momenta, slabs, (fresh0.at[1], fresh1.at[0], fresh1.at[1]), images)
-        share1.hand()
 
     @pl.when(step < steps)
     def _():
@@ -1212,7 +1212,6 @@
         rows = gq.shape[1]
         for i in range(gq.shape[0]):
             gq[i] = accq[i * rows : (i + 1) * rows, :].astype(BF16)
-        share1.along_z()
         late.begin()
 
     @pl.when(step >= steps)
@@ -1232,19 +1231,20 @@
 
     @pl.when(step == steps + 1)
     def _():
+        late.pass_on(0, 1)
+
+    @pl.when(step == steps + 2)
+    def _():
+        late.pass_on(0, 0)
+        renew(early.totals(), momenta, slabs, (fresh0.at[1], fresh1.at[0], fresh1.at[1]), images)
+        share1.hand()
+
+    @pl.when(step == last)
+    def _():
+        share1.along_z()
         table_sums(dbias_ref, index_ref, table_scr, idx_scr, turned_idx)
-        share1.along_y()
-
-    @pl.when(step == steps + 2)
-    def _():
-        late.pass_on(0, 1)
-
-    @pl.when(step == last)
-    def _():
         pack_small(small, sums_ref, sums2_ref, hsum_ref, hidden_ref, table_scr)
-        late.pass_on(0, 0, tiny.begin)
-        tiny.step()
-        tiny.go_on()
+        tiny.begin()
         renew(late.totals(), (qkv_momentum,), (qkv_slab,), (fresh0.at[0],), images)
         tiny.step()
         share0.hand()
@@ -1252,6 +1252,7 @@
         tiny.step()
         tiny.go_on()
         share0.along_z()
+        share1.along_y()
         tiny.step()
         tiny.go_on()
         share0.along_y()

time: 220 us -> 213 us (0.968)
  Pallas kernels: 216 us -> 207 us
    pallas_call x1, Pallas kernels: 26.7 us -> 20.8 us  [newton_schulz(): pl.pallas_call(functools.partial(newton_schulz_kernel, nt, heights), out_...]
    pallas_call x1, Pallas kernels: 82.6 us -> 79.8 us  [attention_backward(): pl.pallas_call(functools.partial(attention_backward_kernel, ndp, nt, imag...]
where the time goes in v5:
time: 213 us; the launch traced here: 210 us
  Pallas kernels  207 us (97%)
    pallas_call x1, Pallas kernels, attention_backward(): pl.pallas_call(functools.partial(attention_backward_kernel, ndp, nt, imag...  79.8 us
    pallas_call x1, Pallas kernels, attention_forward(): pl.pallas_call(functools.partial(attention_forward_kernel, ndp, nt, steps...  57.9 us
    pallas_call x1, Pallas kernels, mlp(): pl.pallas_call(mlp_kernel, grid=(steps,), out_shape=(shape_of(out_grad.sh...  45.8 us
    pallas_call x1, Pallas kernels, newton_schulz(): pl.pallas_call(functools.partial(newton_schulz_kernel, nt, heights), out_...  20.8 us

profile of v5, /device:TPU:17, one launch (start us, length us, event | category | flops | bytes accessed | tf_op | source)
XLA Modules:
  0.0 209.5 jit_solution(5125357226829055082)
XLA Ops:
  0.7 57.9 %attention_forward.1 = (f32[2048,512]{1,0:T(8,128)}, bf16[2048,512]{1,0:T(8,128)(2,1)}, bf16[2048,1536]{1,0:T(8,128)(2,1)}, bf16[16384,128]{1,0:T(8,128)(2,1)}, ...) custom-call(f32[1568,512]{1,0:T(8,128)} %refs_0_.1, ...), custom_call_target="tpu_custom_call" | custom-call | tf_op jit(solution)/shard_map/attention_forward/pallas_call | solution.py:1303
  58.6 45.8 %mlp.1 = (f32[1568,512]{1,0:T(8,128)}, f32[2048,512]{1,0:T(8,128)}, bf16[2048,512]{1,0:T(8,128)(2,1)}, bf16[2048,512]{1,0:T(8,128)(2,1)}, bf16[512,512]{1,0:T(8,...) custom-call(f32[2048,512]{1,0:T(8,128)} %get-tuple-element.82.xs_ref.refs_1_, bf16[2048,512]{1,0:T(8,128)(2,1)} %get-tuple-element.83.o_ref, ...), custom_call_target="tpu_custom_call" | custom-call | tf_op jit(solution)/shard_map/mlp/pallas_call | solution.py:1360
  104.4 79.8 %attention_backward.1 = (f32[1568,512]{1,0:T(8,128)}, f32[16,512]{1,0:T(8,128)}, f32[64,512]{1,0:T(8,128)}, f32[64,512]{1,0:T(8,128)}, f32[48,512]{1,0:T(8,128)}...) custom-call(f32[2048,512]{1,0:T(8,128)} %get-tuple-element.88.refs_0_, ...), custom_call_target="tpu_custom_call" | custom-call | tf_op jit(solution)/shard_map/attention_backward/pallas_call | solution.py:1439
  184.3 0.0 copy-start
  184.3 20.8 %newton_schulz.1 = (bf16[2,48,512]{2,1,0:T(8,128)(2,1)}, bf16[2,64,512]{2,1,0:T(8,128)(2,1)}) custom-call(bf16[1536,512]{1,0:T(8,128)(2,1)} %bitcast.66, bf16[2048,512]{1,0:T(8,128)(2,1)} %bitcast.61), custom_call_target="tpu_custom_call" | custom-call | tf_op jit(solution)/shard_map/newton_schulz/pallas_call | solution.py:757
  205.1 2.7 %finish.1 = (f32[48,512]{1,0:T(8,128)}, f32[64,512]{1,0:T(8,128)}, f32[16,512]{1,0:T(8,128)}, f32[64,512]{1,0:T(8,128)}, f32[48,512]{1,0:T(8,128)}, /*index=5*/f...) custom-call(bf16[2,48,512]{2,1,0:T(8,128)(2,1)} %get-tuple-element.1, ...), custom_call_target="tpu_custom_call" | custom-call | tf_op jit(solution)/shard_map/finish/pallas_call | solution.py:815
  207.8 0.0 copy-done
  207.8 1.7 copy.52
Async XLA Ops:
  184.3 23.5 %copy-start = (f32[1568,512]{1,0:T(8,128)S(1)}, f32[1568,512]{1,0:T(8,128)}, u32[]{:S(2)}) copy-start(f32[1568,512]{1,0:T(8,128)} %get-tuple-element.165) | copy-start | bytes 9633796

commit v6 on v5

--- a/solution.py
+++ b/solution.py
@@ -1077,7 +1077,7 @@
         acc1[at, :] += dot_tn(dz, a2)
         return carry
 
-    lax.fori_loop(0, w1_ref.shape[0] // width, chunk, 0)
+    lax.fori_loop(0, w1_ref.shape[0] // width, chunk, 0, unroll=4)
     white, inverse = whiten(y_ref[...])
     out_ref[...] = y_ref[...] + m_scr[...] + shift_ref[3:4, :]
     da = da_scr[...]

time: 213 us -> 208 us (0.977)
  Pallas kernels: 207 us -> 202 us
    pallas_call x1, Pallas kernels: 45.8 us -> 40.9 us  [mlp(): pl.pallas_call(mlp_kernel, grid=(steps,), out_shape=(shape_of(out_grad.sh...]
where the time goes in v6:
time: 208 us; the launch traced here: 205 us
  Pallas kernels  202 us (97%)
    pallas_call x1, Pallas kernels, attention_backward(): pl.pallas_call(functools.partial(attention_backward_kernel, ndp, nt, imag...  79.9 us
    pallas_call x1, Pallas kernels, attention_forward(): pl.pallas_call(functools.partial(attention_forward_kernel, ndp, nt, steps...  57.9 us
    pallas_call x1, Pallas kernels, mlp(): pl.pallas_call(mlp_kernel, grid=(steps,), out_shape=(shape_of(out_grad.sh...  40.9 us
    pallas_call x1, Pallas kernels, newton_schulz(): pl.pallas_call(functools.partial(newton_schulz_kernel, nt, heights), out_...  20.9 us

profile of v6, /device:TPU:17, one launch (start us, length us, event | category | flops | bytes accessed | tf_op | source)
XLA Modules:
  0.0 204.7 jit_solution(8613690495553697130)
XLA Ops:
  0.7 57.9 %attention_forward.1 = (f32[2048,512]{1,0:T(8,128)}, bf16[2048,512]{1,0:T(8,128)(2,1)}, bf16[2048,1536]{1,0:T(8,128)(2,1)}, bf16[16384,128]{1,0:T(8,128)(2,1)}, ...) custom-call(f32[1568,512]{1,0:T(8,128)} %refs_0_.1, ...), custom_call_target="tpu_custom_call" | custom-call | tf_op jit(solution)/shard_map/attention_forward/pallas_call | solution.py:1303
  58.6 40.9 %mlp.1 = (f32[1568,512]{1,0:T(8,128)}, f32[2048,512]{1,0:T(8,128)}, bf16[2048,512]{1,0:T(8,128)(2,1)}, bf16[2048,512]{1,0:T(8,128)(2,1)}, bf16[512,512]{1,0:T(8,...) custom-call(f32[2048,512]{1,0:T(8,128)} %get-tuple-element.82.xs_ref.refs_1_, bf16[2048,512]{1,0:T(8,128)(2,1)} %get-tuple-element.83.o_ref, ...), custom_call_target="tpu_custom_call" | custom-call | tf_op jit(solution)/shard_map/mlp/pallas_call | solution.py:1360
  99.5 79.9 %attention_backward.1 = (f32[1568,512]{1,0:T(8,128)}, f32[16,512]{1,0:T(8,128)}, f32[64,512]{1,0:T(8,128)}, f32[64,512]{1,0:T(8,128)}, f32[48,512]{1,0:T(8,128)}...) custom-call(f32[2048,512]{1,0:T(8,128)} %get-tuple-element.88.refs_0_, ...), custom_call_target="tpu_custom_call" | custom-call | tf_op jit(solution)/shard_map/attention_backward/pallas_call | solution.py:1439
  179.4 0.0 copy-start
  179.4 20.9 %newton_schulz.1 = (bf16[2,48,512]{2,1,0:T(8,128)(2,1)}, bf16[2,64,512]{2,1,0:T(8,128)(2,1)}) custom-call(bf16[1536,512]{1,0:T(8,128)(2,1)} %bitcast.66, bf16[2048,512]{1,0:T(8,128)(2,1)} %bitcast.61), custom_call_target="tpu_custom_call" | custom-call | tf_op jit(solution)/shard_map/newton_schulz/pallas_call | solution.py:757
  200.3 2.7 %finish.1 = (f32[48,512]{1,0:T(8,128)}, f32[64,512]{1,0:T(8,128)}, f32[16,512]{1,0:T(8,128)}, f32[64,512]{1,0:T(8,128)}, f32[48,512]{1,0:T(8,128)}, /*index=5*/f...) custom-call(bf16[2,48,512]{2,1,0:T(8,128)(2,1)} %get-tuple-element.1, ...), custom_call_target="tpu_custom_call" | custom-call | tf_op jit(solution)/shard_map/finish/pallas_call | solution.py:815
  203.0 0.0 copy-done
  203.0 1.7 copy.52
Async XLA Ops:
  179.4 23.6 %copy-start = (f32[1568,512]{1,0:T(8,128)S(1)}, f32[1568,512]{1,0:T(8,128)}, u32[]{:S(2)}) copy-start(f32[1568,512]{1,0:T(8,128)} %get-tuple-element.165) | copy-start | bytes 9633796
